TPU v7x, 32 devices: a whole 2x2x4 slice. The times are simulated.
32 devices in a mesh: seq: 8 (over z, y), head: 4 (over x, core).
Axes of the slice: x: 2, y: 2, z: 4, core: 2. Of those that a mesh axis runs over, the one named last changes fastest.
Arguments:
- signal: bfloat16 [2048, 2048], P('seq', 'head'), may hold values from -6 to 6
- gate: bfloat16 [2048, 2048], P('seq', 'head'), may hold values from -6 to 6
- skip: float32 [2048], P('head'), may hold values from -4 to 4
- w_first: float32 [33, 64], replicated, may hold values from -1 to 1
- b_first: float32 [64], replicated, may hold values from -3.140625 to 3.140625
- freq: float32 [64], replicated, may hold values from 0.5 to 2
- w_mid: float32 [64, 64], replicated, may hold values from -0.75 to 0.75
- w_last: float32 [64, 2048], P(None, 'head'), may hold values from -0.046875 to 0.046875
- rate: float32 [2048], P('head'), may hold values from 0.00014648438 to 0.08
- out_w: bfloat16 [2048, 2048], P('head'), may hold values from -0.125 to 0.125
Outputs:
- output: bfloat16 [2048, 2048], P('seq', 'head')
All inputs are finite; a program needn't handle non-finite values.
Results may differ from a plain program's by a relative error of at most 0.0054.
Values may be sent and summed in bfloat16 or wider, within the bound.
No kernel may reach another device: no remote copies, remote signals or barrier semaphores. Data moves between devices by JAX's collectives and lax.ppermute only.
A program may use at most 64 MiB of HBM per device.

v0:
```python
import math

import jax
import jax.numpy as jnp
from jax import lax
from jax.sharding import PartitionSpec as P

K = 2048
BANDS = 16


def shifted(x, axis, by):
    size = lax.axis_size(axis)
    pairs = [(i, i + by) for i in range(size) if 0 <= i + by < size]
    return lax.ppermute(x, axis, pairs)


def make_filter(w_first, b_first, freq, w_mid, w_last, rate, count):
    highest = lax.Precision.HIGHEST
    position = jnp.arange(count).astype(jnp.float32)
    bands = jnp.arange(1, BANDS + 1).astype(jnp.float32)
    angles = 2.0 * math.pi * position[:, None] * bands[None, :] / K
    features = jnp.concatenate([position[:, None] / K, jnp.cos(angles), jnp.sin(angles)], 1)
    first = jnp.sin(freq * (jnp.dot(features, w_first, precision=highest) + b_first))
    second = jnp.sin(freq * jnp.dot(first, w_mid, precision=highest))
    raw = jnp.dot(second, w_last, precision=highest)
    return (raw * jnp.exp(-rate[None, :] * position[:, None])).astype(jnp.bfloat16)


def transform_tables(block):
    doubled = 2 * block
    taps = jnp.arange(block)
    freqs = jnp.arange(block)
    outputs = jnp.arange(doubled)
    scale_angle = 2.0 * math.pi / doubled
    phase = (freqs[:, None] * taps[None, :] % doubled).astype(jnp.float32) * scale_angle
    alternate = (1 - 2 * (taps % 2)).astype(jnp.float32)
    forward_real = jnp.cos(phase)
    forward_imag = jnp.where(freqs[:, None] == 0, alternate[None, :], -jnp.sin(phase))
    phase_back = (outputs[:, None] * freqs[None, :] % doubled).astype(jnp.float32) * scale_angle
    alternate_back = (1 - 2 * (outputs % 2)).astype(jnp.float32)
    weights = jnp.where(freqs == 0, 1.0, 2.0).astype(jnp.float32)
    back_real = weights[None, :] * jnp.cos(phase_back) / doubled
    back_imag = (
        jnp.where(freqs[None, :] == 0, alternate_back[:, None], -2.0 * jnp.sin(phase_back))
        / doubled
    )
    return (forward_real, forward_imag, back_real, back_imag)


def long_convolve(padded, filt, length_local):
    highest = lax.Precision.HIGHEST
    channels = padded.shape[1]
    block = min(128, length_local)
    segments = K // block
    out_blocks = length_local // block
    in_blocks = padded.shape[0] // block
    forward_real, forward_imag, back_real, back_imag = transform_tables(block)
    values = padded.astype(jnp.float32).reshape(in_blocks, block, channels)
    kernels = filt.astype(jnp.float32).reshape(segments, block, channels)[::-1]
    spec_real = jnp.einsum("ft,ntc->nfc", forward_real, values, precision=highest)
    spec_imag = jnp.einsum("ft,ntc->nfc", forward_imag, values, precision=highest)
    kern_real = jnp.einsum("ft,ntc->nfc", forward_real, kernels, precision=highest)
    kern_imag = jnp.einsum("ft,ntc->nfc", forward_imag, kernels, precision=highest)
    upper = (jnp.arange(block) >= 1).astype(jnp.float32)[:, None]
    sums_real = []
    sums_imag = []
    for index in range(out_blocks + 1):
        window_real = spec_real[index : index + segments]
        window_imag = spec_imag[index : index + segments]
        both_imag = kern_imag * window_imag
        sums_real.append(jnp.sum(kern_real * window_real - upper * both_imag, 0))
        cross = kern_real * window_imag + kern_imag * window_real
        sums_imag.append(jnp.sum(upper * cross + (1.0 - upper) * both_imag, 0))
    total_real = jnp.stack(sums_real, 0)
    total_imag = jnp.stack(sums_imag, 0)
    pieces = jnp.einsum("tf,kfc->ktc", back_real, total_real, precision=highest)
    pieces = pieces + jnp.einsum("tf,kfc->ktc", back_imag, total_imag, precision=highest)
    joined = pieces[1:, :block] + pieces[:-1, block:]
    return joined.reshape(length_local, channels)


def local(signal, gate, skip, w_first, b_first, freq, w_mid, w_last, rate, out_w):
    length_local, channels = signal.shape
    filt = make_filter(w_first, b_first, freq, w_mid, w_last, rate, K)
    reach = K // length_local
    earlier = [shifted(signal, "seq", step) for step in range(reach, 0, -1)]
    padded = jnp.concatenate(earlier + [signal], 0)
    conv = long_convolve(padded, filt, length_local)
    mixed = (gate.astype(jnp.float32) * (conv + skip[None, :] * signal.astype(jnp.float32))).astype(
        jnp.bfloat16
    )
    terms = jnp.dot(mixed, out_w, preferred_element_type=jnp.float32)
    result = lax.psum_scatter(terms, "head", scatter_dimension=1, tiled=True)
    return result.astype(jnp.bfloat16)


def solution(mesh):
    placed = (
        P("seq", "head"),
        P("seq", "head"),
        P("head"),
        P(),
        P(),
        P(),
        P(),
        P(None, "head"),
        P("head"),
        P("head", None),
    )
    return jax.shard_map(
        local, mesh=mesh, in_specs=placed, out_specs=P("seq", "head"), check_vma=False
    )
```

profile of v0, /device:TPU:0, one launch (start us, length us, event | category | flops | bytes accessed | tf_op | source)
XLA Modules:
  0.0 148.3 jit_solution(12778419984911320177)
XLA Ops:
  6.5 0.0 copy-start
  6.5 0.0 reduce-scatter.2.cloned.1.call-start
  6.5 1.5 %collective-permute-start = (bf16[256,512]{1,0:T(8,128)(2,1)}, bf16[256,512]{1,0:T(8,128)(2,1)}, u32[]{:S(2)}, u32[]{:S(2)}) collective-permute-start(bf16[256,512]{1,0:T(8,128)(2,1)} %param.10), channel_id=1, source_target_pairs={} | collective-permute-start | bytes 786440 | tf_op jit(solution)/shard_map/ppermute | solution.py:15
  8.0 8.6 %collective-permute-start.1 = (bf16[256,512]{1,0:T(8,128)(2,1)}, bf16[256,512]{1,0:T(8,128)(2,1)}, u32[]{:S(2)}, u32[]{:S(2)}) collective-permute-start(bf16[256,512]{1,0:T(8,128)(2,1)} %param.10), channel_id=1, source_target_pairs={{0,28},{1,29},{2,30},{3,31}} | collective-permute-start | bytes 786440 | tf_op jit(solution)/shard_map/ppermute | solution.py:15
  16.7 1.3 collective-permute-start.2
  18.0 1.3 collective-permute-start.3
  19.3 1.3 collective-permute-start.4
  20.7 0.7 neg.9
  21.4 0.5 fusion.54
  21.9 3.1 %fusion.19 = f32[2048,64]{0,1:T(8,128)S(1)} fusion(f32[33,64]{1,0:T(8,128)} %param.13, f32[2048,16]{0,1:T(8,128)S(1)} %get-tuple-element.12, f32[2048,16]{0,1:T(8,128)S(1)} %get-tuple-element.11, f32[2048,1]{0,1:T(1,128)S(1)} %convert_multiply_fusion, f32[64]{0:T(128)} %param.14, f32[64]{0:T(128)} %param.15), kind=kOutput, calls=%fused_computation.34 | convolution fusion | flops 52301824 | bytes 803584 | tf_op jit(solution)/shard_map/dot_general | solution.py:24
  25.0 3.0 %fusion.20 = f32[2048,64]{0,1:T(8,128)S(1)} fusion(f32[2048,64]{0,1:T(8,128)S(1)} %fusion.19, f32[64,64]{1,0:T(8,128)} %param.16, f32[64]{0:T(128)} %param.15), kind=kOutput, calls=%fused_computation.35 | convolution fusion | flops 100794368 | bytes 1065216 | tf_op jit(solution)/shard_map/dot_general | solution.py:25
  28.0 5.9 %multiply_convert_fusion = bf16[2048,512]{1,0:T(8,128)(2,1)} fusion(f32[2048,64]{0,1:T(8,128)S(1)} %fusion.20, f32[64,512]{1,0:T(8,128)} %param.17, f32[2048]{0:T(1024)S(1)} %iota_convert_fusion, f32[512]{0:T(512)S(1)} %neg.9), kind=kOutput, calls=%fused_computation.30 | convolution fusion | flops 808452096 | bytes 2762752 | tf_op jit(solution)/shard_map/dot_general | solution.py:26
  34.0 4.1 %copy.15 = f32[16,128,512]{1,2,0:T(8,128)} copy(bf16[16,128,512]{2,1,0:T(8,128)(2,1)} %bitcast.120) | data formatting | bytes 6291456 | tf_op jit(solution)/shard_map/reshape | solution.py:60
  38.0 4.6 %rev.3 = f32[16,128,512]{1,2,0:T(8,128)} reverse(f32[16,128,512]{1,2,0:T(8,128)} %copy.15), dimensions={0} | reverse | bytes 8388608 | tf_op jit(solution)/shard_map/rev | solution.py:60
  42.6 7.1 %fusion.63 = f32[16,512,128]{2,1,0:T(8,128)} fusion(f32[16,128,512]{1,2,0:T(8,128)} %rev.3), kind=kOutput, calls=%fused_computation.90 | convolution fusion | flops 1610842112 | bytes 8388608 | tf_op jit(solution)/shard_map/ft,ntc->nfc/dot_general | solution.py:63
  49.7 0.0 collective-permute-done
  49.7 0.0 copy-done.2
  49.7 1.8 %collective-permute-start.5 = (bf16[256,512]{1,0:T(8,128)(2,1)S(1)}, bf16[256,512]{1,0:T(8,128)(2,1)S(1)}, u32[]{:S(2)}, u32[]{:S(2)}) collective-permute-start(bf16[256,512]{1,0:T(8,128)(2,1)S(1)} %copy-done.2), channel_id=1, source_target_pairs={{0,12},{4,16},{8,20},{12,24},{16,28},{1,13},{5,17},{9,21},{13,25},... | collective-permute-start | bytes 786440 | tf_op jit(solution)/shard_map/ppermute | solution.py:15
  51.5 1.0 constant_dynamic-update-slice_fusion.8
  52.4 0.0 collective-permute-done.1
  52.5 1.3 collective-permute-start.6
  53.8 1.0 constant_dynamic-update-slice_fusion.7
  54.7 0.0 collective-permute-done.2
  54.8 3.3 %collective-permute-start.7 = (bf16[256,512]{1,0:T(8,128)(2,1)S(1)}, bf16[256,512]{1,0:T(8,128)(2,1)S(1)}, u32[]{:S(2)}, u32[]{:S(2)}) collective-permute-start(bf16[256,512]{1,0:T(8,128)(2,1)S(1)} %copy-done.2), channel_id=1, source_target_pairs={{0,4},{4,8},{8,12},{12,16},{16,20},{20,24},{24,28},{1,5},{5,9},{9,... | collective-permute-start | bytes 786440 | tf_op jit(solution)/shard_map/ppermute | solution.py:15
  58.1 0.0 collective-permute-done.3
  58.1 0.0 collective-permute-done.4
  58.1 0.0 collective-permute-done.5
  58.2 4.2 %collective-permute-done.6 = bf16[256,512]{1,0:T(8,128)(2,1)S(1)} collective-permute-done((bf16[256,512]{1,0:T(8,128)(2,1)S(1)}, bf16[256,512]{1,0:T(8,128)(2,1)S(1)}, u32[]{:S(2)}, u32[]{:S(2)}) %collective-permute-start.6) | collective-permute-done | bytes 262176 | tf_op jit(solution)/shard_map/ppermute | solution.py:15
  62.4 0.5 collective-permute-done.7
  62.9 3.0 %convolution_bitcast_fusion.1 = f32[18,128,512]{1,2,0:T(8,128)S(1)} fusion(bf16[18,128,512]{2,1,0:T(8,128)(2,1)S(1)} %bitcast.118), kind=kOutput, calls=%fused_computation.37 | convolution fusion | flops 1812168704 | bytes 7077888 | tf_op jit(solution)/shard_map/ft,ntc->nfc/dot_general | solution.py:61
  65.9 3.0 %convolution_bitcast_fusion = f32[18,128,512]{1,2,0:T(8,128)S(1)} fusion(bf16[18,128,512]{2,1,0:T(8,128)(2,1)S(1)} %bitcast.119, f32[128]{0:T(128)S(1)} %fusion.90, pred[128]{0:T(512)(128)(4,1)S(1)} %get-tuple-element.14), kind=kOutput, calls=%fused_computation.36 | convolution fusion | flops 1812201472 | bytes 7078528 | tf_op jit(solution)/shard_map/ft,ntc->nfc/dot_general | solution.py:62
  69.0 12.7 %fusion.3 = (f32[128,512]{0,1:T(8,128)}, f32[128,512]{0,1:T(8,128)}, f32[128,512]{0,1:T(8,128)}, f32[128,512]{0,1:T(8,128)}, f32[128,512]{0,1:T(8,128)}, /*index=5*/f32[128,512]{0,1:T(8,128)}) fusion(f32[16,512,128]{2,1,0:T(8,128)} %fusion.63, f32[18,128,512]{1,2,0:T(8,128)S(1)} %convolution_bitcast_fusion, ...), kind=kOutput, calls=%fused_computation.9 | convolution fusion | flops 1648230400 | bytes 35128960 | tf_op jit(solution)/shard_map/ft,ntc->nfc/dot_general | solution.py:64
  81.7 1.1 copy.20
  82.8 1.1 copy.18
  83.9 1.8 %copy.19 = f32[128,512]{1,0:T(8,128)} copy(f32[128,512]{0,1:T(8,128)} %get-tuple-element.8) | data formatting | bytes 524288 | tf_op jit(solution)/shard_map/reduce_sum | solution.py:72
  85.7 1.1 copy.21
  86.8 1.8 %copy.22 = f32[128,512]{1,0:T(8,128)} copy(f32[128,512]{0,1:T(8,128)} %get-tuple-element.6) | data formatting | bytes 524288 | tf_op jit(solution)/shard_map/reduce_sum | solution.py:74
  88.6 1.8 %copy.23 = f32[128,512]{1,0:T(8,128)} copy(f32[128,512]{0,1:T(8,128)} %get-tuple-element.7) | data formatting | bytes 524288 | tf_op jit(solution)/shard_map/reduce_sum | solution.py:74
  90.4 2.9 %fusion.21 = f32[3,512,256]{1,2,0:T(8,128)S(1)} fusion(f32[1,128,512]{2,1,0:T(8,128)S(1)} %bitcast.121, f32[1,128,512]{2,1,0:T(8,128)} %bitcast.125, f32[1,128,512]{2,1,0:T(8,128)S(1)} %bitcast.123, f32[128]{0:T(128)S(1)} %broadcast_select_fusion), kind=kOutput, calls=%fused_computation.39 | convolution fusion | flops 604897280 | bytes 2359808 | tf_op jit(solution)/shard_map/tf,kfc->ktc/dot_general | solution.py:77
  93.3 3.0 %add_bitcast_fusion = f32[3,256,512]{2,1,0:T(8,128)S(1)} fusion(f32[3,512,256]{1,2,0:T(8,128)S(1)} %fusion.21, f32[1,128,512]{2,1,0:T(8,128)} %bitcast.126, f32[1,128,512]{2,1,0:T(8,128)} %bitcast.124, f32[1,128,512]{2,1,0:T(8,128)S(1)} %bitcast.122, f32[256]{0:T(256)S(1)} %fusion.87, pred[128]{0:T(512)(128)(4,1)S(1)} %get-tuple-element.14), kind=kOutput, calls=%fused_computation.38 | convolution fusion | flops 605323264 | bytes 3933312 | tf_op jit(solution)/shard_map/tf,kfc->ktc/dot_general | solution.py:78
  96.3 0.1 slice_add_fusion
  96.4 0.0 copy-done.4
  96.4 0.0 copy-done.3
  96.4 0.1 fusion.33
  96.5 2.1 %fusion.121 = f32[256,2048]{1,0:T(8,128)} fusion(bf16[256,512]{1,0:T(8,128)(2,1)S(1)} %fusion.33, bf16[512,2048]{1,0:T(8,128)(2,1)S(1)} %copy-done), kind=kOutput, calls=%fused_computation.162 | convolution fusion | flops 536870912 | bytes 4456448 | tf_op jit(solution)/shard_map/dot_general | solution.py:93
  98.6 0.0 reduce-scatter.2.cloned.1.call-update
  98.6 41.0 %reduce-scatter.2.cloned.1.call-done = f32[256,512]{1,0:T(8,128)} async-done(((f32[256,2048]{1,0:T(8,128)}), f32[256,512]{1,0:T(8,128)}) %reduce-scatter.2.cloned.1.call-update) | async-done | bytes 524304 | tf_op jit(solution)/shard_map/reduce_scatter | solution.py:94
  139.7 1.8 %convert_element_type.117 = bf16[256,512]{1,0:T(8,128)(2,1)} convert(f32[256,512]{1,0:T(8,128)} %reduce-scatter.2.cloned.1.call-done) | non-fusion elementwise | flops 131072 | bytes 786432 | tf_op jit(solution)/shard_map/convert_element_type | solution.py:95
  (22 shorter events, 0.2 us)
Async XLA Ops:
  6.5 90.0 %copy-start = (bf16[512,2048]{1,0:T(8,128)(2,1)S(1)}, bf16[512,2048]{1,0:T(8,128)(2,1)}, u32[]{:S(2)}) copy-start(bf16[512,2048]{1,0:T(8,128)(2,1)} %param.19) | copy-start | bytes 6291460
  6.5 133.1 %reduce-scatter.2.cloned.1.call-start = ((), (), s32[]{:S(2)}) async-start(), calls=%async_computation.1 | async-start | bytes 2621440 | tf_op jit(solution)/shard_map/reduce_scatter | solution.py:94
  6.5 43.1 %collective-permute-start = (bf16[256,512]{1,0:T(8,128)(2,1)}, bf16[256,512]{1,0:T(8,128)(2,1)}, u32[]{:S(2)}, u32[]{:S(2)}) collective-permute-start(bf16[256,512]{1,0:T(8,128)(2,1)} %param.10), channel_id=1, source_target_pairs={} | collective-permute-start | bytes 786440 | tf_op jit(solution)/shard_map/ppermute | solution.py:15
  8.0 44.4 %collective-permute-start.1 = (bf16[256,512]{1,0:T(8,128)(2,1)}, bf16[256,512]{1,0:T(8,128)(2,1)}, u32[]{:S(2)}, u32[]{:S(2)}) collective-permute-start(bf16[256,512]{1,0:T(8,128)(2,1)} %param.10), channel_id=1, source_target_pairs={{0,28},{1,29},{2,30},{3,31}} | collective-permute-start | bytes 786440 | tf_op jit(solution)/shard_map/ppermute | solution.py:15
  16.7 38.1 %collective-permute-start.2 = (bf16[256,512]{1,0:T(8,128)(2,1)}, bf16[256,512]{1,0:T(8,128)(2,1)S(1)}, u32[]{:S(2)}, u32[]{:S(2)}) collective-permute-start(bf16[256,512]{1,0:T(8,128)(2,1)} %param.10), channel_id=1, source_target_pairs={{0,24},{4,28},{1,25},{5,29},{2,26},{6,30},{3,27},{7,31}} | collective-permute-start | bytes 786440 | tf_op jit(solution)/shard_map/ppermute | solution.py:15
  18.0 40.1 %collective-permute-start.3 = (bf16[256,512]{1,0:T(8,128)(2,1)}, bf16[256,512]{1,0:T(8,128)(2,1)S(1)}, u32[]{:S(2)}, u32[]{:S(2)}) collective-permute-start(bf16[256,512]{1,0:T(8,128)(2,1)} %param.10), channel_id=1, source_target_pairs={{0,20},{4,24},{8,28},{1,21},{5,25},{9,29},{2,22},{6,26},{10,30},{3... | collective-permute-start | bytes 786440 | tf_op jit(solution)/shard_map/ppermute | solution.py:15
  19.3 38.8 %collective-permute-start.4 = (bf16[256,512]{1,0:T(8,128)(2,1)}, bf16[256,512]{1,0:T(8,128)(2,1)S(1)}, u32[]{:S(2)}, u32[]{:S(2)}) collective-permute-start(bf16[256,512]{1,0:T(8,128)(2,1)} %param.10), channel_id=1, source_target_pairs={{0,16},{4,20},{8,24},{12,28},{1,17},{5,21},{9,25},{13,29},{2,18},{... | collective-permute-start | bytes 786440 | tf_op jit(solution)/shard_map/ppermute | solution.py:15
  42.6 7.1 %copy-start.2 = (bf16[256,512]{1,0:T(8,128)(2,1)S(1)}, bf16[256,512]{1,0:T(8,128)(2,1)}, u32[]{:S(2)}) copy-start(bf16[256,512]{1,0:T(8,128)(2,1)} %param.10) | copy-start | bytes 786436
  49.7 8.4 %collective-permute-start.5 = (bf16[256,512]{1,0:T(8,128)(2,1)S(1)}, bf16[256,512]{1,0:T(8,128)(2,1)S(1)}, u32[]{:S(2)}, u32[]{:S(2)}) collective-permute-start(bf16[256,512]{1,0:T(8,128)(2,1)S(1)} %copy-done.2), channel_id=1, source_target_pairs={{0,12},{4,16},{8,20},{12,24},{16,28},{1,13},{5,17},{9,21},{13,25},... | collective-permute-start | bytes 786440 | tf_op jit(solution)/shard_map/ppermute | solution.py:15
  52.5 9.9 %collective-permute-start.6 = (bf16[256,512]{1,0:T(8,128)(2,1)S(1)}, bf16[256,512]{1,0:T(8,128)(2,1)S(1)}, u32[]{:S(2)}, u32[]{:S(2)}) collective-permute-start(bf16[256,512]{1,0:T(8,128)(2,1)S(1)} %copy-done.2), channel_id=1, source_target_pairs={{0,8},{4,12},{8,16},{12,20},{16,24},{20,28},{1,9},{5,13},{9,17},{1... | collective-permute-start | bytes 786440 | tf_op jit(solution)/shard_map/ppermute | solution.py:15
  54.8 8.1 %collective-permute-start.7 = (bf16[256,512]{1,0:T(8,128)(2,1)S(1)}, bf16[256,512]{1,0:T(8,128)(2,1)S(1)}, u32[]{:S(2)}, u32[]{:S(2)}) collective-permute-start(bf16[256,512]{1,0:T(8,128)(2,1)S(1)} %copy-done.2), channel_id=1, source_target_pairs={{0,4},{4,8},{8,12},{12,16},{16,20},{20,24},{24,28},{1,5},{5,9},{9,... | collective-permute-start | bytes 786440 | tf_op jit(solution)/shard_map/ppermute | solution.py:15
  65.9 3.1 %copy-start.1 = (f32[16,128,512]{1,2,0:T(8,128)S(1)}, f32[16,128,512]{1,2,0:T(8,128)}, u32[]{:S(2)}) copy-start(f32[16,128,512]{1,2,0:T(8,128)} %rev.3) | copy-start | bytes 12582916
  88.6 7.8 %copy-start.4 = (f32[512]{0:T(512)S(1)}, f32[512]{0:T(512)}, u32[]{:S(2)}) copy-start(f32[512]{0:T(512)} %param.12) | copy-start | bytes 6148
  90.4 6.0 %copy-start.3 = (bf16[256,512]{1,0:T(8,128)(2,1)S(1)}, bf16[256,512]{1,0:T(8,128)(2,1)}, u32[]{:S(2)}) copy-start(bf16[256,512]{1,0:T(8,128)(2,1)} %param.11) | copy-start | bytes 786436
Sparse Core Ops, SparseCore 0:
  98.7 40.8 reduce-scatter.1
where the time goes:
time: 149 us; the launch traced here: 148 us
  matrix products  45.9 us (31%)
  waiting for transfers between devices  45.7 us (31%)
  starting transfers between devices  20.4 us (14%)
  local copies, waits for them, and re-layouts  19.3 us (13%)
  between operations  13.7 us (9%)
  other arithmetic  3.25 us (2%)
    reduce_scatter x1, waiting for transfers between devices, local(): result = lax.psum_scatter(terms, 'head', scatter_dimension=1, tiled=True)  41 us
    ppermute x8, starting transfers between devices, shifted(): return lax.ppermute(x, axis, pairs)  20.4 us
    dot_general x1, matrix products, long_convolve(): jnp.einsum('ft,ntc->nfc', forward_imag, kernels, precision=highest)  12.7 us
    dot_general x1, matrix products, long_convolve(): jnp.einsum('ft,ntc->nfc', forward_real, kernels, precision=highest)  7.05 us
    dot_general x1, matrix products, make_filter(): raw = jnp.dot(second, w_last, precision=highest)  5.92 us
    reduce_sum x3, local copies, waits for them, and re-layouts, long_convolve(): sums_imag.append(jnp.sum(upper * cross + (1.0 - upper) * both_imag, 0))  4.66 us
    ppermute x8, waiting for transfers between devices, shifted(): return lax.ppermute(x, axis, pairs)  4.64 us
    rev x1, local copies, waits for them, and re-layouts, long_convolve(): kernels = filt.astype(jnp.float32).reshape(segments, block, channels)[::-1]  4.56 us
  transfers between devices with their start and end apart: 9, of which 3 were waited for; matrix products, arithmetic and copies ran while one was open for 21% of the time, Pallas kernels for 0%

commit v1 on v0

--- a/solution.py
+++ b/solution.py
@@ -1,12 +1,323 @@
+import functools
 import math
 
 import jax
 import jax.numpy as jnp
+import numpy as np
 from jax import lax
+from jax.experimental import pallas as pl
+from jax.experimental.pallas import tpu as pltpu
 from jax.sharding import PartitionSpec as P
 
 K = 2048
 BANDS = 16
+BLOCK = 128
+VMEM = pltpu.MemorySpace.VMEM
+SMEM = pltpu.MemorySpace.SMEM
+BF16 = jnp.bfloat16
+F32 = jnp.float32
+HIGHEST = lax.Precision.HIGHEST
+
+
+def feature_table():
+    taps = np.arange(K, dtype=np.float64)
+    bands = np.arange(1, BANDS + 1, dtype=np.float64)
+    angles = 2.0 * np.pi * ((taps[None, :] * bands[:, None]) % K) / K
+    return np.concatenate([taps[None, :] / K, np.cos(angles), np.sin(angles)], 0).astype(np.float32)
+
+
+def split(table):
+    table = np.asarray(table, np.float32)
+    high = table.astype(BF16)
+    low = (table - high.astype(np.float32)).astype(BF16)
+    return high, low
+
+
+def forward_table():
+    size = 2 * BLOCK
+    samples = np.arange(size)
+    freqs = np.arange(BLOCK)
+    phase = 2.0 * np.pi * ((samples[:, None] * freqs[None, :]) % size) / size
+    real = np.cos(phase)
+    imag = -np.sin(phase)
+    imag[:, 0] = 1.0 - 2.0 * (samples % 2)
+    return np.concatenate([real, imag], 1)
+
+
+def backward_table():
+    size = 2 * BLOCK
+    samples = np.arange(BLOCK, size)
+    freqs = np.arange(BLOCK)
+    phase = 2.0 * np.pi * ((freqs[:, None] * samples[None, :]) % size) / size
+    real = 2.0 * np.cos(phase)
+    imag = -2.0 * np.sin(phase)
+    real[0] = 1.0
+    imag[0] = 1.0 - 2.0 * (samples % 2)
+    return np.concatenate([real, imag], 0) / size
+
+
+def dot(a, b):
+    return jnp.dot(a, b, preferred_element_type=F32)
+
+
+def sine(x):
+    turns = jnp.round(x * (1.0 / math.pi))
+    r = x - turns * 3.140625
+    r = r - turns * 9.67502593994140625e-4
+    r = r - turns * 1.50995799097e-7
+    odd = turns - 2.0 * jnp.floor(turns * 0.5)
+    sign = 1.0 - 2.0 * odd
+    s = r * r
+    p = -2.5052108385e-8
+    p = p * s + 2.7557319224e-6
+    p = p * s - 1.9841269841e-4
+    p = p * s + 8.3333333333e-3
+    p = p * s - 1.6666666667e-1
+    return sign * (r + r * (s * p))
+
+
+def filter_kernel(feat, w_first, bias, freq, w_mid, w_last, rate, table, real_out, imag_out, real2_out):
+    first = sine(freq[...] * (jnp.dot(w_first[...], feat[...], precision=HIGHEST) + bias[...]))
+    second = sine(freq[...] * jnp.dot(w_mid[...], first, precision=HIGHEST))
+    raw = jnp.dot(w_last[...], second, precision=HIGHEST)
+    channels, taps = raw.shape
+    position = lax.broadcasted_iota(jnp.int32, (1, taps), 1).astype(F32)
+    filt = (raw * jnp.exp(-rate[...] * position)).astype(BF16)
+    count = taps // BLOCK
+    rows = jnp.concatenate([filt[:, j * BLOCK : (j + 1) * BLOCK] for j in range(count)], 0)
+    spec = dot(jnp.concatenate([rows, rows], 1), table[...])
+    real, imag = spec[:, :BLOCK], spec[:, BLOCK:]
+    lane = lax.broadcasted_iota(jnp.int32, real.shape, 1)
+    shape = (count, channels, BLOCK)
+    real_out[...] = real.reshape(shape)
+    imag_out[...] = jnp.where(lane == 0, 0.0, imag).reshape(shape)
+    real2_out[...] = jnp.where(lane == 0, imag, real).reshape(shape)
+
+
+def conv_kernel(pieces, index, real, imag, real2, table_high, table_low, back_high, back_low, *refs):
+    ins, outs = refs[:pieces], refs[pieces : 2 * pieces]
+    samples, spec, total, result = refs[2 * pieces :]
+    me = index[0]
+    blocks, channels = total.shape[0], total.shape[1]
+    per = ins[0].shape[2] // BLOCK
+    samples[0] = jnp.zeros((channels, BLOCK), BF16)
+    for k in range(pieces):
+        for r in range(2):
+            place = lax.bitwise_xor(me, 2 * k + r) * per
+            for part in range(per):
+                samples[place + (1 + part)] = ins[k][r, :, part * BLOCK : (part + 1) * BLOCK]
+    before = samples[0:blocks].reshape(blocks * channels, BLOCK)
+    current = samples[1 : blocks + 1].reshape(blocks * channels, BLOCK)
+    window = jnp.concatenate([before, current], 1)
+    spec[...] = (dot(window, table_high[...]) + dot(window, table_low[...])).reshape(spec.shape)
+    taps = real.shape[0]
+
+    def group(g, carry):
+        at = pl.ds(pl.multiple_of(g * 8, 8), 8)
+        for k in range(blocks):
+            acc_real = acc_imag = None
+            for j in range(min(k + 1, taps)):
+                x_real = spec[k - j, at, :BLOCK]
+                x_imag = spec[k - j, at, BLOCK:]
+                f_real, f_imag, f_real2 = real[j, at, :], imag[j, at, :], real2[j, at, :]
+                term_real = x_real * f_real - x_imag * f_imag
+                term_imag = x_real * f_imag + x_imag * f_real2
+                acc_real = term_real if acc_real is None else acc_real + term_real
+                acc_imag = term_imag if acc_imag is None else acc_imag + term_imag
+            total[k, at, :BLOCK] = acc_real
+            total[k, at, BLOCK:] = acc_imag
+        return carry
+
+    lax.fori_loop(0, channels // 8, group, 0)
+    sums = total[...].reshape(blocks * channels, 2 * BLOCK)
+    high = sums.astype(BF16)
+    low = (sums - high.astype(F32)).astype(BF16)
+    conv = dot(high, back_high[...]) + dot(low, back_high[...]) + dot(high, back_low[...])
+    result[...] = conv.astype(BF16).reshape(result.shape)
+    for k in range(pieces):
+        for r in range(2):
+            place = lax.bitwise_xor(me, 2 * k + r) * per
+            for part in range(per):
+                outs[k][r, :, part * BLOCK : (part + 1) * BLOCK] = result[place + part]
+
+
+def mix_kernel(pieces, index, signal, gate, skip, other, *refs):
+    ins, (keep_out, send_out), conv = refs[:pieces], refs[pieces : pieces + 2], refs[pieces + 2]
+    me, core = index[0], index[1]
+    channels = ins[0].shape[1]
+    for k in range(pieces):
+        conv[lax.bitwise_xor(me, 2 * k)] = ins[k][0]
+        conv[lax.bitwise_xor(me, 2 * k + 1)] = other[k]
+    turned = conv[...].reshape(-1, conv.shape[-1]).T.astype(F32)
+    mixed = (
+        gate[...].astype(F32) * (turned + skip[...] * signal[...].astype(F32))
+    ).astype(BF16)
+    half = mixed.shape[0] // 2
+    low, high = mixed[:half], mixed[half:]
+    keep_out[...] = jnp.where(core == 0, low, high)
+    send_out[...] = jnp.where(core == 0, high, low)
+
+
+def terms_kernel(head_xors, index, mine, theirs, own_w, other_w, *outs):
+    head = index[2]
+    width = outs[0].shape[1]
+    for flip, out in zip(head_xors, outs):
+        at = pl.ds(pl.multiple_of(lax.bitwise_xor(head, flip) * width, width), width)
+        out[...] = (dot(mine[...], own_w[:, at]) + dot(theirs[...], other_w[:, at])).astype(out.dtype)
+
+
+def sum_kernel(index, own, a, b, c, out):
+    core = index[1]
+    half = own.shape[0]
+    here = own[...] + a[...].astype(F32)
+    there = c[...].astype(F32) + b[...].astype(F32)
+    out[pl.ds(pl.multiple_of(core * half, half), half), :] = here.astype(BF16)
+    out[pl.ds(pl.multiple_of((1 - core) * half, half), half), :] = there.astype(BF16)
+
+
+def turn_kernel(x, out):
+    out[...] = x[...].T
+
+
+def spec_of(space):
+    return pl.BlockSpec(memory_space=space)
+
+
+def call(kernel, outs, *args, scratch=(), flops=0, name=None, scalars=0):
+    return pl.pallas_call(
+        kernel,
+        out_shape=outs,
+        in_specs=[spec_of(SMEM)] * scalars + [spec_of(VMEM)] * (len(args) - scalars),
+        out_specs=jax.tree.map(lambda _: spec_of(VMEM), outs),
+        scratch_shapes=list(scratch),
+        cost_estimate=pl.CostEstimate(flops=flops, bytes_accessed=0, transcendentals=0),
+        name=name,
+    )(*args)
+
+
+def shape(dims, dtype=BF16):
+    return jax.ShapeDtypeStruct(dims, dtype)
+
+
+def flip(x, axis, by):
+    size = lax.axis_size(axis)
+    return lax.ppermute(x, axis, [(i, i ^ by) for i in range(size)])
+
+
+def spread(signal, gate, skip, w_first, b_first, freq, w_mid, w_last, rate, out_w):
+    length_local, channels = signal.shape
+    ranks = lax.axis_size("seq")
+    pieces = ranks // 2
+    share = channels // ranks
+    blocks = ranks * length_local // BLOCK
+    taps = K // BLOCK
+    me = lax.axis_index("seq")
+    head = lax.axis_index("head")
+    side = me % 2
+    index = jnp.stack([me, head % 2, head]).astype(jnp.int32)
+    other_w = flip(out_w, "head", 1)
+
+    turned = call(turn_kernel, shape((channels, length_local)), signal, name="turn")
+    turned = turned.reshape(pieces, 2, share, length_local)
+    keep = lax.dynamic_index_in_dim(turned, side, 1, keepdims=True)
+    send = lax.dynamic_index_in_dim(turned, 1 - side, 1, keepdims=True)
+    stack = jnp.concatenate([keep, flip(send, "seq", 1)], 1)
+    parts = [
+        lax.dynamic_index_in_dim(stack, (me // 2) ^ k, 0, keepdims=False) for k in range(pieces)
+    ]
+    parts = [flip(part, "seq", 2 * k) if k else part for k, part in enumerate(parts)]
+
+    column = lambda v: v.reshape(-1, 1)
+    forward_high, forward_low = split(forward_table())
+    back_high, back_low = split(backward_table())
+    filter_table = np.concatenate([forward_high[:BLOCK], forward_low[:BLOCK]], 0)
+    spectrum = shape((taps, share, BLOCK), F32)
+    real, imag, real2 = call(
+        filter_kernel,
+        (spectrum,) * 3,
+        feature_table(),
+        w_first.T,
+        column(b_first),
+        column(freq),
+        w_mid.T,
+        lax.dynamic_slice_in_dim(w_last, me * share, share, 1).T,
+        column(lax.dynamic_slice_in_dim(rate, me * share, share, 0)),
+        filter_table,
+        flops=2_000_000_000,
+        name="filter",
+    )
+
+    piece = shape((2, share, length_local))
+    convs = call(
+        functools.partial(conv_kernel, pieces),
+        (piece,) * pieces,
+        index,
+        real,
+        imag,
+        real2,
+        forward_high,
+        forward_low,
+        back_high,
+        back_low,
+        *parts,
+        scratch=[
+            pltpu.VMEM((blocks + 1, share, BLOCK), BF16),
+            pltpu.VMEM((blocks, share, 2 * BLOCK), F32),
+            pltpu.VMEM((blocks, share, 2 * BLOCK), F32),
+            pltpu.VMEM((blocks, share, BLOCK), BF16),
+        ],
+        flops=2_000_000_000,
+        name="conv",
+        scalars=1,
+    )
+
+    convs = [flip(conv, "seq", 2 * k) if k else conv for k, conv in enumerate(convs)]
+    other = flip(jnp.stack([conv[1] for conv in convs]), "seq", 1)
+    half = length_local // 2
+    keep, send = call(
+        functools.partial(mix_kernel, pieces),
+        (shape((half, channels)),) * 2,
+        index,
+        signal,
+        gate,
+        skip.reshape(1, -1),
+        other,
+        *convs,
+        scratch=[pltpu.VMEM((ranks, share, length_local), BF16)],
+        flops=500_000_000,
+        name="mix",
+        scalars=1,
+    )
+    got = flip(send, "head", 1)
+    width = out_w.shape[1] // lax.axis_size("head")
+    terms = shape((half, width))
+    a, b = call(
+        functools.partial(terms_kernel, (2, 3)),
+        (terms, terms),
+        index,
+        keep,
+        got,
+        out_w,
+        other_w,
+        flops=500_000_000,
+        name="terms_far",
+        scalars=1,
+    )
+    a, b = flip(a, "head", 2), flip(b, "head", 3)
+    c, own = call(
+        functools.partial(terms_kernel, (1, 0)),
+        (terms, shape((half, width), F32)),
+        index,
+        keep,
+        got,
+        out_w,
+        other_w,
+        flops=500_000_000,
+        name="terms_near",
+        scalars=1,
+    )
+    c = flip(c, "head", 1)
+    return call(sum_kernel, shape((length_local, width)), index, own, a, b, c, name="sum", scalars=1)
 
 
 def shifted(x, axis, by):
@@ -16,14 +327,13 @@
 
 
 def make_filter(w_first, b_first, freq, w_mid, w_last, rate, count):
-    highest = lax.Precision.HIGHEST
     position = jnp.arange(count).astype(jnp.float32)
     bands = jnp.arange(1, BANDS + 1).astype(jnp.float32)
     angles = 2.0 * math.pi * position[:, None] * bands[None, :] / K
     features = jnp.concatenate([position[:, None] / K, jnp.cos(angles), jnp.sin(angles)], 1)
-    first = jnp.sin(freq * (jnp.dot(features, w_first, precision=highest) + b_first))
-    second = jnp.sin(freq * jnp.dot(first, w_mid, precision=highest))
-    raw = jnp.dot(second, w_last, precision=highest)
+    first = jnp.sin(freq * (jnp.dot(features, w_first, precision=HIGHEST) + b_first))
+    second = jnp.sin(freq * jnp.dot(first, w_mid, precision=HIGHEST))
+    raw = jnp.dot(second, w_last, precision=HIGHEST)
     return (raw * jnp.exp(-rate[None, :] * position[:, None])).astype(jnp.bfloat16)
 
 
@@ -49,7 +359,6 @@
 
 
 def long_convolve(padded, filt, length_local):
-    highest = lax.Precision.HIGHEST
     channels = padded.shape[1]
     block = min(128, length_local)
     segments = K // block
@@ -58,10 +367,10 @@
     forward_real, forward_imag, back_real, back_imag = transform_tables(block)
     values = padded.astype(jnp.float32).reshape(in_blocks, block, channels)
     kernels = filt.astype(jnp.float32).reshape(segments, block, channels)[::-1]
-    spec_real = jnp.einsum("ft,ntc->nfc", forward_real, values, precision=highest)
-    spec_imag = jnp.einsum("ft,ntc->nfc", forward_imag, values, precision=highest)
-    kern_real = jnp.einsum("ft,ntc->nfc", forward_real, kernels, precision=highest)
-    kern_imag = jnp.einsum("ft,ntc->nfc", forward_imag, kernels, precision=highest)
+    spec_real = jnp.einsum("ft,ntc->nfc", forward_real, values, precision=HIGHEST)
+    spec_imag = jnp.einsum("ft,ntc->nfc", forward_imag, values, precision=HIGHEST)
+    kern_real = jnp.einsum("ft,ntc->nfc", forward_real, kernels, precision=HIGHEST)
+    kern_imag = jnp.einsum("ft,ntc->nfc", forward_imag, kernels, precision=HIGHEST)
     upper = (jnp.arange(block) >= 1).astype(jnp.float32)[:, None]
     sums_real = []
     sums_imag = []
@@ -74,13 +383,13 @@
         sums_imag.append(jnp.sum(upper * cross + (1.0 - upper) * both_imag, 0))
     total_real = jnp.stack(sums_real, 0)
     total_imag = jnp.stack(sums_imag, 0)
-    pieces = jnp.einsum("tf,kfc->ktc", back_real, total_real, precision=highest)
-    pieces = pieces + jnp.einsum("tf,kfc->ktc", back_imag, total_imag, precision=highest)
+    pieces = jnp.einsum("tf,kfc->ktc", back_real, total_real, precision=HIGHEST)
+    pieces = pieces + jnp.einsum("tf,kfc->ktc", back_imag, total_imag, precision=HIGHEST)
     joined = pieces[1:, :block] + pieces[:-1, block:]
     return joined.reshape(length_local, channels)
 
 
-def local(signal, gate, skip, w_first, b_first, freq, w_mid, w_last, rate, out_w):
+def halo(signal, gate, skip, w_first, b_first, freq, w_mid, w_last, rate, out_w):
     length_local, channels = signal.shape
     filt = make_filter(w_first, b_first, freq, w_mid, w_last, rate, K)
     reach = K // length_local
@@ -93,6 +402,16 @@
     terms = jnp.dot(mixed, out_w, preferred_element_type=jnp.float32)
     result = lax.psum_scatter(terms, "head", scatter_dimension=1, tiled=True)
     return result.astype(jnp.bfloat16)
+
+
+def local(signal, *rest):
+    ranks, heads = lax.axis_size("seq"), lax.axis_size("head")
+    length_local, channels = signal.shape
+    small = ranks * length_local <= K and heads == 4
+    fits = ranks >= 2 and ranks & (ranks - 1) == 0 and channels % (16 * ranks) == 0
+    if small and fits and length_local % (2 * BLOCK) == 0:
+        return spread(signal, *rest)
+    return halo(signal, *rest)
 
 
 def solution(mesh):

time: 149 us -> 68.9 us (0.46)
  matrix products: 45.9 us -> 0 us
  waiting for transfers between devices: 45.7 us -> 17.1 us
  Pallas kernels: 0 us -> 22.2 us
  between operations: 13.7 us -> 0.05 us
  local copies, waits for them, and re-layouts: 19.3 us -> 13 us
  starting transfers between devices: 20.4 us -> 14.6 us
  other arithmetic: 3.25 us -> 1.34 us
    dot_general x10 -> x0, matrix products: 45.9 us -> none  [the longest x1 12.7 us: long_convolve(): jnp.einsum('ft,ntc->nfc', forward_imag, kernels, precision=highest)]
    reduce_scatter x1 -> x0, waiting for transfers between devices: 41 us -> none  [local(): result = lax.psum_scatter(terms, 'head', scatter_dimension=1, tiled=True)]
    pallas_call x0 -> x7, Pallas kernels: none -> 22.2 us  [call(): pl.pallas_call(kernel, out_shape=outs, in_specs=[spec_of(SMEM)] * scalars...]
    ppermute x8 -> x13, waiting for transfers between devices: 4.64 us -> 17.1 us  [flip(): return lax.ppermute(x, axis, [(i, i ^ by) for i in range(size)])]
    reduce_sum x6 -> x0, local copies, waits for them, and re-layouts: 8.59 us -> none  [the longest x3 4.66 us: long_convolve(): sums_imag.append(jnp.sum(upper * cross + (1.0 - upper) * both_imag, 0))]
    ppermute x8 -> x13, starting transfers between devices: 20.4 us -> 14.6 us  [flip(): return lax.ppermute(x, axis, [(i, i ^ by) for i in range(size)])]
    unnamed x18 -> x29, local copies, waits for them, and re-layouts: 2.07 us -> 6.95 us
    rev x1 -> x0, local copies, waits for them, and re-layouts: 4.56 us -> none  [long_convolve(): kernels = filt.astype(jnp.float32).reshape(segments, block, channels)[::-1]]
  transfers between devices with their start and end apart: 9 -> 13, of which waited for: 3 -> 8; matrix products, arithmetic and copies ran while one was open for 21% -> 16% of each run, Pallas kernels for 0% -> 25%
where the time goes in v1:
time: 68.9 us; the launch traced here: 68.2 us
  Pallas kernels  22.2 us (32%)
  waiting for transfers between devices  17.1 us (25%)
  starting transfers between devices  14.6 us (21%)
  local copies, waits for them, and re-layouts  13 us (19%)
  other arithmetic  1.34 us (2%)
    pallas_call x7, Pallas kernels, call(): pl.pallas_call(kernel, out_shape=outs, in_specs=[spec_of(SMEM)] * scalars...  22.2 us
    ppermute x13, waiting for transfers between devices, flip(): return lax.ppermute(x, axis, [(i, i ^ by) for i in range(size)])  17.1 us
    ppermute x13, starting transfers between devices, flip(): return lax.ppermute(x, axis, [(i, i ^ by) for i in range(size)])  14.6 us
    unnamed x29, local copies, waits for them, and re-layouts  6.95 us
    reshape x4, local copies, waits for them, and re-layouts, spread(): column = lambda v: v.reshape(-1, 1)  4.18 us
  transfers between devices with their start and end apart: 13, of which 8 were waited for; matrix products, arithmetic and copies ran while one was open for 16% of the time, Pallas kernels for 25%

profile of v1, /device:TPU:0, one launch (start us, length us, event | category | flops | bytes accessed | tf_op | source)
XLA Modules:
  0.0 68.2 jit_solution(3787591015592198864)
XLA Ops:
  0.0 0.5 collective-permute-start.9
  0.5 1.8 %turn.1 = bf16[512,256]{1,0:T(8,128)(2,1)} custom-call(bf16[256,512]{1,0:T(8,128)(2,1)} %signal.1), custom_call_target="tpu_custom_call" | custom-call | tf_op jit(solution)/shard_map/turn/pallas_call | solution.py:187
  2.3 1.0 %constant_dynamic-slice_fusion = (bf16[4,1,64,256]{3,2,1,0:T(8,128)(2,1)S(1)}, bf16[4,1,64,256]{3,2,1,0:T(8,128)(2,1)S(1)}) fusion(bf16[4,2,64,256]{3,2,1,0:T(8,128)(2,1)} %bitcast.20, s32[]{:T(128)S(6)} %select_n.46, s32[]{:T(128)S(6)} %select_n.45), kind=kLoop, calls=%fused_computation.17 | loop fusion | bytes 524296 | tf_op jit(solution)/shard_map/jit(dynamic_index_in_dim)/dynamic_slice | solution.py:223
  3.3 2.6 %collective-permute-start = (bf16[4,1,64,256]{3,2,1,0:T(8,128)(2,1)S(1)}, bf16[4,1,64,256]{3,2,1,0:T(8,128)(2,1)S(1)}, u32[]{:S(2)}, u32[]{:S(2)}) collective-permute-start(bf16[4,1,64,256]{3,2,1,0:T(8,128)(2,1)S(1)} %get-tuple-element.35), channel_id=1, source_target_pairs={{0,4},{4,0},{8,12},{12,8},{16,20},{20,16},{24,28},{28,24},{1,5},{5... | collective-permute-start | bytes 393224 | tf_op jit(solution)/shard_map/ppermute | solution.py:204
  5.9 0.1 constant_dynamic-slice_fusion.2
  6.0 0.7 %copy.23 = f32[64,64]{0,1:T(8,128)} copy(f32[64,64]{1,0:T(8,128)S(1)} %constant_dynamic-slice_fusion.2) | data formatting | bytes 32768
  6.7 0.8 %dynamic-slice_bitcast_fusion = f32[64,1]{0,1:T(1,128)S(1)} fusion(f32[512]{0:T(512)} %param.24, s32[]{:T(128)S(6)} %select_n.43), kind=kLoop, calls=%fused_computation.21 | loop fusion | bytes 516 | tf_op jit(solution)/shard_map/reshape | solution.py:230
  7.4 0.7 %copy.22.rate = f32[64,1]{1,0:T(8,128)} copy(f32[64,1]{0,1:T(1,128)S(1)} %dynamic-slice_bitcast_fusion) | data formatting | bytes 512 | tf_op jit(solution)/shard_map/reshape | solution.py:230
  8.1 1.4 %copy.17 = f32[33,64]{0,1:T(8,128)} copy(f32[33,64]{1,0:T(8,128)} %param.19) | data formatting | bytes 16896 | tf_op args[3]
  9.6 1.5 %copy.18 = f32[64,64]{0,1:T(8,128)} copy(f32[64,64]{1,0:T(8,128)} %param.22) | data formatting | bytes 32768 | tf_op args[6]
  11.0 1.4 %copy.20.bias = f32[64,1]{1,0:T(8,128)} copy(f32[64,1]{0,1:T(1,128)} %bitcast.24) | data formatting | bytes 512 | tf_op jit(solution)/shard_map/reshape | solution.py:230
  12.4 1.4 %copy.21.freq = f32[64,1]{1,0:T(8,128)} copy(f32[64,1]{0,1:T(1,128)} %bitcast.25) | data formatting | bytes 512 | tf_op jit(solution)/shard_map/reshape | solution.py:230
  13.7 4.4 %filter.1 = (f32[16,64,128]{2,1,0:T(8,128)}, f32[16,64,128]{2,1,0:T(8,128)}, f32[16,64,128]{2,1,0:T(8,128)}) custom-call(f32[33,2048]{1,0:T(8,128)} %constant.81.clone.feat, f32[64,33]{1,0:T(8,128)} %bitcast.23, f32[64,1]{1,0:T(8,128)} %copy.20.bias, f32[64,1]{1,0:T(8,128)} %copy.21.freq, f32[64,64]{1,0:T(8,128)} %bitcast.22, f32[64,64]{1,0:T(8,128)} %bitcast.21, ...), custom_call_target="tpu_custom_call" | custom-call | flops 2000000000 | tf_op jit(solution)/shard_map/filter/pallas_call | solution.py:187
  18.1 0.7 fusion.1
  18.8 1.6 %collective-permute-start.1 = (bf16[2,64,256]{2,1,0:T(8,128)(2,1)S(1)}, bf16[2,64,256]{2,1,0:T(8,128)(2,1)S(1)}, u32[]{:S(2)}, u32[]{:S(2)}) collective-permute-start(bf16[2,64,256]{2,1,0:T(8,128)(2,1)S(1)} %get-tuple-element.33), channel_id=1, source_target_pairs={{0,8},{4,12},{8,0},{12,4},{16,24},{20,28},{24,16},{28,20},{1,9},{5... | collective-permute-start | bytes 196616 | tf_op jit(solution)/shard_map/ppermute | solution.py:204
  20.4 2.6 %collective-permute-start.2 = (bf16[2,64,256]{2,1,0:T(8,128)(2,1)S(1)}, bf16[2,64,256]{2,1,0:T(8,128)(2,1)S(1)}, u32[]{:S(2)}, u32[]{:S(2)}) collective-permute-start(bf16[2,64,256]{2,1,0:T(8,128)(2,1)S(1)} %get-tuple-element.34), channel_id=1, source_target_pairs={{0,16},{4,20},{8,24},{12,28},{16,0},{20,4},{24,8},{28,12},{1,17},{... | collective-permute-start | bytes 196616 | tf_op jit(solution)/shard_map/ppermute | solution.py:204
  23.0 0.2 collective-permute-start.3
  23.2 0.7 pad_add_fusion.index
  23.9 0.0 collective-permute-done.1.refs_1_
  23.9 4.1 %collective-permute-done.2.refs_2_ = bf16[2,64,256]{2,1,0:T(8,128)(2,1)S(1)} collective-permute-done((bf16[2,64,256]{2,1,0:T(8,128)(2,1)S(1)}, bf16[2,64,256]{2,1,0:T(8,128)(2,1)S(1)}, u32[]{:S(2)}, u32[]{:S(2)}) %collective-permute-start.2) | collective-permute-done | bytes 65568 | tf_op jit(solution)/shard_map/ppermute | solution.py:204
  27.9 1.2 %collective-permute-done.3.refs_3_ = bf16[2,64,256]{2,1,0:T(8,128)(2,1)S(1)} collective-permute-done((bf16[2,64,256]{2,1,0:T(8,128)(2,1)S(1)}, bf16[2,64,256]{2,1,0:T(8,128)(2,1)S(1)}, u32[]{:S(2)}, u32[]{:S(2)}) %collective-permute-start.3) | collective-permute-done | bytes 65568 | tf_op jit(solution)/shard_map/ppermute | solution.py:204
  29.1 0.6 copy-done.12
  29.8 5.1 %conv.1 = (bf16[2,64,256]{2,1,0:T(8,128)(2,1)}, bf16[2,64,256]{2,1,0:T(8,128)(2,1)}, bf16[2,64,256]{2,1,0:T(8,128)(2,1)}, bf16[2,64,256]{2,1,0:T(8,128)(2,1)}) custom-call(s32[3]{0:T(128)} %pad_add_fusion.index, f32[16,64,128]{2,1,0:T(8,128)} %get-tuple-element.18.real, f32[16,64,128]{2,1,0:T(8,128)} %get-tuple-element.19.imag, ...), custom_call_target="tpu_custom_call" | custom-call | flops 2000000000 | tf_op jit(solution)/shard_map/conv/pallas_call | solution.py:187
  34.8 0.9 %collective-permute-start.4 = (bf16[2,64,256]{2,1,0:T(8,128)(2,1)}, bf16[2,64,256]{2,1,0:T(8,128)(2,1)S(1)}, u32[]{:S(2)}, u32[]{:S(2)}) collective-permute-start(bf16[2,64,256]{2,1,0:T(8,128)(2,1)} %get-tuple-element.22), channel_id=1, source_target_pairs={{0,8},{4,12},{8,0},{12,4},{16,24},{20,28},{24,16},{28,20},{1,9},{5... | collective-permute-start | bytes 196616 | tf_op jit(solution)/shard_map/ppermute | solution.py:204
  35.7 1.7 %collective-permute-start.5 = (bf16[2,64,256]{2,1,0:T(8,128)(2,1)}, bf16[2,64,256]{2,1,0:T(8,128)(2,1)S(1)}, u32[]{:S(2)}, u32[]{:S(2)}) collective-permute-start(bf16[2,64,256]{2,1,0:T(8,128)(2,1)} %get-tuple-element.23), channel_id=1, source_target_pairs={{0,16},{4,20},{8,24},{12,28},{16,0},{20,4},{24,8},{28,12},{1,17},{... | collective-permute-start | bytes 196616 | tf_op jit(solution)/shard_map/ppermute | solution.py:204
  37.4 1.8 %collective-permute-start.6 = (bf16[2,64,256]{2,1,0:T(8,128)(2,1)}, bf16[2,64,256]{2,1,0:T(8,128)(2,1)S(1)}, u32[]{:S(2)}, u32[]{:S(2)}) collective-permute-start(bf16[2,64,256]{2,1,0:T(8,128)(2,1)} %get-tuple-element.24), channel_id=1, source_target_pairs={{0,24},{4,28},{8,16},{12,20},{16,8},{20,12},{24,0},{28,4},{1,25},{... | collective-permute-start | bytes 196616 | tf_op jit(solution)/shard_map/ppermute | solution.py:204
  39.2 0.8 %slice.12 = bf16[1,64,256]{2,1,0:T(8,128)(2,1)S(1)} slice(bf16[2,64,256]{2,1,0:T(8,128)(2,1)} %get-tuple-element.21.refs_0_), slice={[1:2], [0:64], [0:256]} | slice | bytes 65536 | tf_op jit(solution)/shard_map/slice | solution.py:275
  40.0 0.0 collective-permute-done.4.refs_1_
  40.0 2.2 %collective-permute-done.5.refs_2_ = bf16[2,64,256]{2,1,0:T(8,128)(2,1)S(1)} collective-permute-done((bf16[2,64,256]{2,1,0:T(8,128)(2,1)}, bf16[2,64,256]{2,1,0:T(8,128)(2,1)S(1)}, u32[]{:S(2)}, u32[]{:S(2)}) %collective-permute-start.5) | collective-permute-done | bytes 65568 | tf_op jit(solution)/shard_map/ppermute | solution.py:204
  42.1 1.6 %collective-permute-done.6.refs_3_ = bf16[2,64,256]{2,1,0:T(8,128)(2,1)S(1)} collective-permute-done((bf16[2,64,256]{2,1,0:T(8,128)(2,1)}, bf16[2,64,256]{2,1,0:T(8,128)(2,1)S(1)}, u32[]{:S(2)}, u32[]{:S(2)}) %collective-permute-start.6) | collective-permute-done | bytes 65568 | tf_op jit(solution)/shard_map/ppermute | solution.py:204
  43.7 0.6 collective-permute-start.7
  44.3 4.5 %collective-permute-done.7.other = bf16[4,64,256]{2,1,0:T(8,128)(2,1)S(1)} collective-permute-done((bf16[4,64,256]{2,1,0:T(8,128)(2,1)S(1)}, bf16[4,64,256]{2,1,0:T(8,128)(2,1)S(1)}, u32[]{:S(2)}, u32[]{:S(2)}) %collective-permute-start.7) | collective-permute-done | bytes 131104 | tf_op jit(solution)/shard_map/ppermute | solution.py:204
  48.8 0.6 copy-done.9
  49.4 2.0 %mix.1 = (bf16[128,512]{1,0:T(8,128)(2,1)}, bf16[128,512]{1,0:T(8,128)(2,1)}) custom-call(s32[3]{0:T(128)} %pad_add_fusion.index, bf16[256,512]{1,0:T(8,128)(2,1)} %signal.1, bf16[256,512]{1,0:T(8,128)(2,1)} %gate.1, f32[1,512]{1,0:T(1,128)} %bitcast.26, bf16[4,64,256]{2,1,0:T(8,128)(2,1)} %copy-done.9, bf16[2,64,256]{2,1,0:T(8,128)(2,1)} %get-tuple-element.21.refs_0_, ...), custom_call_target="tpu_custom_call" | custom-call | flops 500000000 | tf_op jit(solution)/shard_map/mix/pallas_call | solution.py:187
  51.5 0.0 collective-permute-start.8
  51.5 1.6 %collective-permute-done.8.theirs = bf16[128,512]{1,0:T(8,128)(2,1)S(1)} collective-permute-done((bf16[128,512]{1,0:T(8,128)(2,1)}, bf16[128,512]{1,0:T(8,128)(2,1)S(1)}, u32[]{:S(2)}, u32[]{:S(2)}) %collective-permute-start.8) | collective-permute-done | bytes 131104 | tf_op jit(solution)/shard_map/ppermute | solution.py:204
  53.0 0.6 copy-done.2
  53.7 0.7 %copy-done.1 = bf16[512,2048]{1,0:T(8,128)(2,1)} copy-done((bf16[512,2048]{1,0:T(8,128)(2,1)}, bf16[512,2048]{1,0:T(8,128)(2,1)S(1)}, u32[]{:S(2)}) %copy-start.1) | copy-done | bytes 2097176
  54.4 3.5 %terms_far.1 = (bf16[128,512]{1,0:T(8,128)(2,1)}, bf16[128,512]{1,0:T(8,128)(2,1)}) custom-call(s32[3]{0:T(128)} %pad_add_fusion.index, bf16[128,512]{1,0:T(8,128)(2,1)} %get-tuple-element.25.mine, bf16[128,512]{1,0:T(8,128)(2,1)} %copy-done.2, bf16[512,2048]{1,0:T(8,128)(2,1)} %own_w.3, bf16[512,2048]{1,0:T(8,128)(2,1)} %copy-done.1), custom_call_target="tpu_custom_call" | custom-call | flops 500000000 | tf_op jit(solution)/shard_map/terms_far/pallas_call | solution.py:187
  57.9 1.5 %collective-permute-start.10 = (bf16[128,512]{1,0:T(8,128)(2,1)}, bf16[128,512]{1,0:T(8,128)(2,1)S(1)}, u32[]{:S(2)}, u32[]{:S(2)}) collective-permute-start(bf16[128,512]{1,0:T(8,128)(2,1)} %get-tuple-element.28), channel_id=1, source_target_pairs={{0,2},{1,3},{2,0},{3,1},{4,6},{5,7},{6,4},{7,5},{8,10},{9,11},{10,... | collective-permute-start | bytes 393224 | tf_op jit(solution)/shard_map/ppermute | solution.py:204
  59.4 0.0 collective-permute-start.11
  59.4 3.6 %terms_near.1 = (bf16[128,512]{1,0:T(8,128)(2,1)}, f32[128,512]{1,0:T(8,128)}) custom-call(s32[3]{0:T(128)} %pad_add_fusion.index, bf16[128,512]{1,0:T(8,128)(2,1)} %get-tuple-element.25.mine, bf16[128,512]{1,0:T(8,128)(2,1)} %copy-done.2, bf16[512,2048]{1,0:T(8,128)(2,1)} %own_w.3, bf16[512,2048]{1,0:T(8,128)(2,1)} %copy-done.1), custom_call_target="tpu_custom_call" | custom-call | flops 500000000 | tf_op jit(solution)/shard_map/terms_near/pallas_call | solution.py:187
  63.0 0.6 collective-permute-start.12
  63.6 0.9 %collective-permute-done.10.a = bf16[128,512]{1,0:T(8,128)(2,1)S(1)} collective-permute-done((bf16[128,512]{1,0:T(8,128)(2,1)}, bf16[128,512]{1,0:T(8,128)(2,1)S(1)}, u32[]{:S(2)}, u32[]{:S(2)}) %collective-permute-start.10) | collective-permute-done | bytes 131104 | tf_op jit(solution)/shard_map/ppermute | solution.py:204
  64.5 1.2 %collective-permute-done.11.b = bf16[128,512]{1,0:T(8,128)(2,1)S(1)} collective-permute-done((bf16[128,512]{1,0:T(8,128)(2,1)}, bf16[128,512]{1,0:T(8,128)(2,1)S(1)}, u32[]{:S(2)}, u32[]{:S(2)}) %collective-permute-start.11) | collective-permute-done | bytes 131104 | tf_op jit(solution)/shard_map/ppermute | solution.py:204
  65.7 0.6 copy-done.4
  66.3 0.0 copy-done.5
  66.4 1.9 %sum.1 = bf16[256,512]{1,0:T(8,128)(2,1)} custom-call(s32[3]{0:T(128)} %pad_add_fusion.index, f32[128,512]{1,0:T(8,128)} %get-tuple-element.27.own, bf16[128,512]{1,0:T(8,128)(2,1)} %copy-done.3, bf16[128,512]{1,0:T(8,128)(2,1)} %copy-done.4, bf16[128,512]{1,0:T(8,128)(2,1)} %copy-done.5), custom_call_target="tpu_custom_call" | custom-call | tf_op jit(solution)/shard_map/sum/pallas_call | solution.py:187
  (27 shorter events, 0.1 us)
Async XLA Ops:
  0.0 5.9 %copy-start = (f32[64,512]{1,0:T(8,128)S(1)}, f32[64,512]{1,0:T(8,128)}, u32[]{:S(2)}) copy-start(f32[64,512]{1,0:T(8,128)} %param.23) | copy-start | bytes 393220
  0.0 53.0 %collective-permute-start.9 = (bf16[512,2048]{1,0:T(8,128)(2,1)}, bf16[512,2048]{1,0:T(8,128)(2,1)S(1)}, u32[]{:S(2)}, u32[]{:S(2)}) collective-permute-start(bf16[512,2048]{1,0:T(8,128)(2,1)} %own_w.3), channel_id=1, source_target_pairs={{0,1},{1,0},{2,3},{3,2},{4,5},{5,4},{6,7},{7,6},{8,9},{9,8},{10,11... | collective-permute-start | bytes 6291464 | tf_op jit(solution)/shard_map/ppermute | solution.py:204
  3.3 14.9 %collective-permute-start = (bf16[4,1,64,256]{3,2,1,0:T(8,128)(2,1)S(1)}, bf16[4,1,64,256]{3,2,1,0:T(8,128)(2,1)S(1)}, u32[]{:S(2)}, u32[]{:S(2)}) collective-permute-start(bf16[4,1,64,256]{3,2,1,0:T(8,128)(2,1)S(1)} %get-tuple-element.35), channel_id=1, source_target_pairs={{0,4},{4,0},{8,12},{12,8},{16,20},{20,16},{24,28},{28,24},{1,5},{5... | collective-permute-start | bytes 393224 | tf_op jit(solution)/shard_map/ppermute | solution.py:204
  18.8 5.1 %collective-permute-start.1 = (bf16[2,64,256]{2,1,0:T(8,128)(2,1)S(1)}, bf16[2,64,256]{2,1,0:T(8,128)(2,1)S(1)}, u32[]{:S(2)}, u32[]{:S(2)}) collective-permute-start(bf16[2,64,256]{2,1,0:T(8,128)(2,1)S(1)} %get-tuple-element.33), channel_id=1, source_target_pairs={{0,8},{4,12},{8,0},{12,4},{16,24},{20,28},{24,16},{28,20},{1,9},{5... | collective-permute-start | bytes 196616 | tf_op jit(solution)/shard_map/ppermute | solution.py:204
  20.4 7.5 %collective-permute-start.2 = (bf16[2,64,256]{2,1,0:T(8,128)(2,1)S(1)}, bf16[2,64,256]{2,1,0:T(8,128)(2,1)S(1)}, u32[]{:S(2)}, u32[]{:S(2)}) collective-permute-start(bf16[2,64,256]{2,1,0:T(8,128)(2,1)S(1)} %get-tuple-element.34), channel_id=1, source_target_pairs={{0,16},{4,20},{8,24},{12,28},{16,0},{20,4},{24,8},{28,12},{1,17},{... | collective-permute-start | bytes 196616 | tf_op jit(solution)/shard_map/ppermute | solution.py:204
  23.0 6.2 %collective-permute-start.3 = (bf16[2,64,256]{2,1,0:T(8,128)(2,1)S(1)}, bf16[2,64,256]{2,1,0:T(8,128)(2,1)S(1)}, u32[]{:S(2)}, u32[]{:S(2)}) collective-permute-start(bf16[2,64,256]{2,1,0:T(8,128)(2,1)S(1)} %get-tuple-element.31), channel_id=1, source_target_pairs={{0,24},{4,28},{8,16},{12,20},{16,8},{20,12},{24,0},{28,4},{1,25},{... | collective-permute-start | bytes 196616 | tf_op jit(solution)/shard_map/ppermute | solution.py:204
  23.9 5.3 %copy-start.10 = (bf16[2,64,256]{2,1,0:T(8,128)(2,1)}, bf16[2,64,256]{2,1,0:T(8,128)(2,1)S(1)}, u32[]{:S(2)}) copy-start(bf16[2,64,256]{2,1,0:T(8,128)(2,1)S(1)} %collective-permute-done.1.refs_1_) | copy-start | bytes 196612
  27.9 1.2 %copy-start.11 = (bf16[2,64,256]{2,1,0:T(8,128)(2,1)}, bf16[2,64,256]{2,1,0:T(8,128)(2,1)S(1)}, u32[]{:S(2)}) copy-start(bf16[2,64,256]{2,1,0:T(8,128)(2,1)S(1)} %collective-permute-done.2.refs_2_) | copy-start | bytes 196612
  29.1 0.6 copy-start.12
  34.8 5.2 %collective-permute-start.4 = (bf16[2,64,256]{2,1,0:T(8,128)(2,1)}, bf16[2,64,256]{2,1,0:T(8,128)(2,1)S(1)}, u32[]{:S(2)}, u32[]{:S(2)}) collective-permute-start(bf16[2,64,256]{2,1,0:T(8,128)(2,1)} %get-tuple-element.22), channel_id=1, source_target_pairs={{0,8},{4,12},{8,0},{12,4},{16,24},{20,28},{24,16},{28,20},{1,9},{5... | collective-permute-start | bytes 196616 | tf_op jit(solution)/shard_map/ppermute | solution.py:204
  35.7 6.5 %collective-permute-start.5 = (bf16[2,64,256]{2,1,0:T(8,128)(2,1)}, bf16[2,64,256]{2,1,0:T(8,128)(2,1)S(1)}, u32[]{:S(2)}, u32[]{:S(2)}) collective-permute-start(bf16[2,64,256]{2,1,0:T(8,128)(2,1)} %get-tuple-element.23), channel_id=1, source_target_pairs={{0,16},{4,20},{8,24},{12,28},{16,0},{20,4},{24,8},{28,12},{1,17},{... | collective-permute-start | bytes 196616 | tf_op jit(solution)/shard_map/ppermute | solution.py:204
  37.4 6.3 %collective-permute-start.6 = (bf16[2,64,256]{2,1,0:T(8,128)(2,1)}, bf16[2,64,256]{2,1,0:T(8,128)(2,1)S(1)}, u32[]{:S(2)}, u32[]{:S(2)}) collective-permute-start(bf16[2,64,256]{2,1,0:T(8,128)(2,1)} %get-tuple-element.24), channel_id=1, source_target_pairs={{0,24},{4,28},{8,16},{12,20},{16,8},{20,12},{24,0},{28,4},{1,25},{... | collective-permute-start | bytes 196616 | tf_op jit(solution)/shard_map/ppermute | solution.py:204
  40.0 8.8 %copy-start.6 = (bf16[2,64,256]{2,1,0:T(8,128)(2,1)}, bf16[2,64,256]{2,1,0:T(8,128)(2,1)S(1)}, u32[]{:S(2)}) copy-start(bf16[2,64,256]{2,1,0:T(8,128)(2,1)S(1)} %collective-permute-done.4.refs_1_) | copy-start | bytes 196612
  42.1 6.6 %copy-start.7 = (bf16[2,64,256]{2,1,0:T(8,128)(2,1)}, bf16[2,64,256]{2,1,0:T(8,128)(2,1)S(1)}, u32[]{:S(2)}) copy-start(bf16[2,64,256]{2,1,0:T(8,128)(2,1)S(1)} %collective-permute-done.5.refs_2_) | copy-start | bytes 196612
  43.7 5.1 %copy-start.8 = (bf16[2,64,256]{2,1,0:T(8,128)(2,1)}, bf16[2,64,256]{2,1,0:T(8,128)(2,1)S(1)}, u32[]{:S(2)}) copy-start(bf16[2,64,256]{2,1,0:T(8,128)(2,1)S(1)} %collective-permute-done.6.refs_3_) | copy-start | bytes 196612
  43.7 5.0 %collective-permute-start.7 = (bf16[4,64,256]{2,1,0:T(8,128)(2,1)S(1)}, bf16[4,64,256]{2,1,0:T(8,128)(2,1)S(1)}, u32[]{:S(2)}, u32[]{:S(2)}) collective-permute-start(bf16[4,64,256]{2,1,0:T(8,128)(2,1)S(1)} %pad_maximum_fusion), channel_id=1, source_target_pairs={{0,4},{4,0},{8,12},{12,8},{16,20},{20,16},{24,28},{28,24},{1,5},{5... | collective-permute-start | bytes 393224 | tf_op jit(solution)/shard_map/ppermute | solution.py:204
  48.8 0.7 copy-start.9
  51.5 1.6 %collective-permute-start.8 = (bf16[128,512]{1,0:T(8,128)(2,1)}, bf16[128,512]{1,0:T(8,128)(2,1)S(1)}, u32[]{:S(2)}, u32[]{:S(2)}) collective-permute-start(bf16[128,512]{1,0:T(8,128)(2,1)} %get-tuple-element.26), channel_id=1, source_target_pairs={{0,1},{1,0},{2,3},{3,2},{4,5},{5,4},{6,7},{7,6},{8,9},{9,8},{10,11... | collective-permute-start | bytes 393224 | tf_op jit(solution)/shard_map/ppermute | solution.py:204
  53.0 0.7 copy-start.2
  53.0 1.4 %copy-start.1 = (bf16[512,2048]{1,0:T(8,128)(2,1)}, bf16[512,2048]{1,0:T(8,128)(2,1)S(1)}, u32[]{:S(2)}) copy-start(bf16[512,2048]{1,0:T(8,128)(2,1)S(1)} %collective-permute-done.9.other_w) | copy-start | bytes 6291460
  57.9 6.6 %collective-permute-start.10 = (bf16[128,512]{1,0:T(8,128)(2,1)}, bf16[128,512]{1,0:T(8,128)(2,1)S(1)}, u32[]{:S(2)}, u32[]{:S(2)}) collective-permute-start(bf16[128,512]{1,0:T(8,128)(2,1)} %get-tuple-element.28), channel_id=1, source_target_pairs={{0,2},{1,3},{2,0},{3,1},{4,6},{5,7},{6,4},{7,5},{8,10},{9,11},{10,... | collective-permute-start | bytes 393224 | tf_op jit(solution)/shard_map/ppermute | solution.py:204
  59.4 6.3 %collective-permute-start.11 = (bf16[128,512]{1,0:T(8,128)(2,1)}, bf16[128,512]{1,0:T(8,128)(2,1)S(1)}, u32[]{:S(2)}, u32[]{:S(2)}) collective-permute-start(bf16[128,512]{1,0:T(8,128)(2,1)} %get-tuple-element.29), channel_id=1, source_target_pairs={{0,3},{1,2},{2,1},{3,0},{4,7},{5,6},{6,5},{7,4},{8,11},{9,10},{10,... | collective-permute-start | bytes 393224 | tf_op jit(solution)/shard_map/ppermute | solution.py:204
  63.0 2.7 %collective-permute-start.12 = (bf16[128,512]{1,0:T(8,128)(2,1)}, bf16[128,512]{1,0:T(8,128)(2,1)S(1)}, u32[]{:S(2)}, u32[]{:S(2)}) collective-permute-start(bf16[128,512]{1,0:T(8,128)(2,1)} %get-tuple-element.30), channel_id=1, source_target_pairs={{0,1},{1,0},{2,3},{3,2},{4,5},{5,4},{6,7},{7,6},{8,9},{9,8},{10,11... | collective-permute-start | bytes 393224 | tf_op jit(solution)/shard_map/ppermute | solution.py:204
  64.5 1.2 %copy-start.3 = (bf16[128,512]{1,0:T(8,128)(2,1)}, bf16[128,512]{1,0:T(8,128)(2,1)S(1)}, u32[]{:S(2)}) copy-start(bf16[128,512]{1,0:T(8,128)(2,1)S(1)} %collective-permute-done.10.a) | copy-start | bytes 393220
  65.7 0.7 copy-start.4
  65.7 0.7 %copy-start.5 = (bf16[128,512]{1,0:T(8,128)(2,1)}, bf16[128,512]{1,0:T(8,128)(2,1)S(1)}, u32[]{:S(2)}) copy-start(bf16[128,512]{1,0:T(8,128)(2,1)S(1)} %collective-permute-done.12.c) | copy-start | bytes 393220

commit v2 on v1

v2 whole, which is shorter than its diff:
```python
import functools
import math

import jax
import jax.numpy as jnp
import numpy as np
from jax import lax
from jax.experimental import pallas as pl
from jax.experimental.pallas import tpu as pltpu
from jax.sharding import PartitionSpec as P


K = 2048
BANDS = 16
BLOCK = 128
VMEM = pltpu.MemorySpace.VMEM
BF16 = jnp.bfloat16
F32 = jnp.float32
HIGHEST = lax.Precision.HIGHEST


def feature_table():
    taps = np.arange(K, dtype=np.float64)
    bands = np.arange(1, BANDS + 1, dtype=np.float64)
    angles = 2.0 * np.pi * ((taps[None, :] * bands[:, None]) % K) / K
    return np.concatenate([taps[None, :] / K, np.cos(angles), np.sin(angles)], 0).astype(np.float32)


def split(table):
    table = np.asarray(table, np.float32)
    high = table.astype(BF16)
    low = (table - high.astype(np.float32)).astype(BF16)
    return high, low


def forward_table():
    size = 2 * BLOCK
    samples = np.arange(size)
    freqs = np.arange(BLOCK)
    phase = 2.0 * np.pi * ((samples[:, None] * freqs[None, :]) % size) / size
    real = np.cos(phase)
    imag = -np.sin(phase)
    imag[:, 0] = 1.0 - 2.0 * (samples % 2)
    return np.concatenate([real, imag], 1)


def backward_table():
    size = 2 * BLOCK
    samples = np.arange(BLOCK, size)
    freqs = np.arange(BLOCK)
    phase = 2.0 * np.pi * ((freqs[:, None] * samples[None, :]) % size) / size
    real = 2.0 * np.cos(phase)
    imag = -2.0 * np.sin(phase)
    real[0] = 1.0
    imag[0] = 1.0 - 2.0 * (samples % 2)
    return np.concatenate([real, imag], 0) / size


def dot(a, b):
    return jnp.dot(a, b, preferred_element_type=F32)


def sine(x):
    turns = jnp.round(x * (1.0 / math.pi))
    r = x - turns * 3.140625
    r = r - turns * 9.67502593994140625e-4
    r = r - turns * 1.50995799097e-7
    odd = turns - 2.0 * jnp.floor(turns * 0.5)
    sign = 1.0 - 2.0 * odd
    s = r * r
    p = -2.5052108385e-8
    p = p * s + 2.7557319224e-6
    p = p * s - 1.9841269841e-4
    p = p * s + 8.3333333333e-3
    p = p * s - 1.6666666667e-1
    return sign * (r + r * (s * p))


def column(row):
    n = row.shape[1]
    square = (n, n)
    diagonal = lax.broadcasted_iota(jnp.int32, square, 0) == lax.broadcasted_iota(jnp.int32, square, 1)
    return jnp.sum(jnp.where(diagonal, jnp.broadcast_to(row, square), 0.0), 1, keepdims=True)


def dot_first(a, b):
    return lax.dot_general(
        a, b, (((0,), (0,)), ((), ())), precision=HIGHEST, preferred_element_type=F32
    )


def share_of(share):
    me = lax.axis_index("seq")
    groups = 128 // share
    lanes = pl.ds(pl.multiple_of((me // groups) * 128, 128), 128)
    rows = pl.ds(pl.multiple_of(lax.rem(me, groups) * share, share), share)
    return lanes, rows


def fetch(sources, targets, sems):
    copies = [
        pltpu.make_async_copy(source, target, sems.at[n])
        for n, (source, target) in enumerate(zip(sources, targets))
    ]
    for copy in copies:
        copy.start()
    return copies


def filter_kernel(count, *refs):
    out, weights, scales, sems = refs[count], refs[2 * count + 1], refs[2 * count + 2], refs[2 * count + 3]
    held = refs[count + 1 : 2 * count + 1]
    for copy in fetch(refs[:count], held, sems):
        copy.wait()
    feat, w_first, bias, freq, w_mid, w_last, rate, table = held
    share = out.shape[1]
    lanes, own = share_of(share)
    freqs = column(freq[...])
    first = sine(freqs * (dot_first(w_first[...], feat[...]) + column(bias[...])))
    second = sine(freqs * dot_first(w_mid[...], first))
    weights[...] = w_last[:, lanes].T
    scales[...] = jnp.broadcast_to(column(rate[:, lanes]), scales.shape)
    raw = jnp.dot(weights[own, :], second, precision=HIGHEST)
    taps = raw.shape[1]
    decay = scales[own, :][:, :1]
    position = lax.broadcasted_iota(jnp.int32, (1, taps), 1).astype(F32)
    filt = (raw * jnp.exp(-decay * position)).astype(BF16)
    count = taps // BLOCK
    rows = jnp.concatenate([filt[:, j * BLOCK : (j + 1) * BLOCK] for j in range(count)], 0)
    spec = dot(jnp.concatenate([rows, rows], 1), table[...])
    out[...] = spec.reshape(out.shape)


def conv_kernel(pieces, filt, table_high, table_low, back_high, back_low, *refs):
    own_in, beside_in = refs[:2]
    ins, outs = refs[2 : pieces + 1], refs[pieces + 1 : 2 * pieces + 2]
    samples, spec, total, result = refs[2 * pieces + 2 :]
    me = lax.axis_index("seq")
    blocks, channels = total.shape[0], total.shape[1]
    per = own_in.shape[1] // BLOCK
    samples[0] = jnp.zeros((channels, BLOCK), BF16)

    def place(values, flips):
        at = lax.bitwise_xor(me, flips) * per
        for part in range(per):
            samples[at + (1 + part)] = values[:, part * BLOCK : (part + 1) * BLOCK]

    place(own_in[...], 0)
    place(beside_in[0], 1)
    for k in range(1, pieces):
        for side in range(2):
            place(ins[k - 1][side], 2 * k + side)
    before = samples[0:blocks].reshape(blocks * channels, BLOCK)
    current = samples[1 : blocks + 1].reshape(blocks * channels, BLOCK)
    window = jnp.concatenate([before, current], 1)
    spec[...] = (dot(window, table_high[...]) + dot(window, table_low[...])).reshape(spec.shape)
    taps = filt.shape[0]

    packed = lax.broadcasted_iota(jnp.int32, (8, BLOCK), 1) == 0

    def group(g, carry):
        at = pl.ds(pl.multiple_of(g * 8, 8), 8)
        for k in range(blocks):
            both_real = both_imag = cross = None
            for j in range(min(k + 1, taps)):
                x_real, x_imag = spec[k - j, at, :BLOCK], spec[k - j, at, BLOCK:]
                f_real, f_imag = filt[j, at, :BLOCK], filt[j, at, BLOCK:]
                terms = (x_real * f_real, x_imag * f_imag, x_real * f_imag + x_imag * f_real)
                if j == 0:
                    both_real, both_imag, cross = terms
                else:
                    both_real, both_imag, cross = both_real + terms[0], both_imag + terms[1], cross + terms[2]
            total[k, at, :BLOCK] = both_real - jnp.where(packed, 0.0, both_imag)
            total[k, at, BLOCK:] = jnp.where(packed, both_imag, cross)
        return carry

    lax.fori_loop(0, channels // 8, group, 0)
    sums = total[...].reshape(blocks * channels, 2 * BLOCK)
    high = sums.astype(BF16)
    low = (sums - high.astype(F32)).astype(BF16)
    conv = dot(high, back_high[...]) + dot(low, back_high[...]) + dot(high, back_low[...])
    result[...] = conv.astype(BF16).reshape(result.shape)

    def taken(flips):
        at = lax.bitwise_xor(me, flips) * per
        return jnp.concatenate([result[at + part] for part in range(per)], 1)

    outs[0][...] = taken(0)
    outs[1][...] = taken(1)
    for k in range(1, pieces):
        for side in range(2):
            outs[k + 1][side] = taken(2 * k + side)


def mix_kernel(pieces, signal, gate, skip, own_in, *refs):
    ins, beside = refs[: pieces - 1], refs[pieces - 1 : pieces - 1 + pieces // 2]
    keep_out, send_out, conv = refs[-3:]
    me = lax.axis_index("seq")
    core = lax.rem(lax.axis_index("head"), 2)
    conv[me] = own_in[...]
    for k in range(1, pieces):
        conv[lax.bitwise_xor(me, 2 * k)] = ins[k - 1][0]
    for k in range(pieces):
        conv[lax.bitwise_xor(me, 2 * k + 1)] = beside[k // 2][k % 2]
    turned = conv[...].reshape(-1, conv.shape[-1]).T.astype(F32)
    mixed = (gate[...].astype(F32) * (turned + skip[...] * signal[...].astype(F32))).astype(BF16)
    half = keep_out.shape[0]
    low, high = mixed[:half], mixed[half:]
    keep_out[...] = jnp.where(core == 0, low, high)
    send_out[...] = jnp.where(core == 0, high, low)


def project_kernel(flips, own, other, own_w, other_w, *outs):
    head = lax.axis_index("head")
    width = outs[0].shape[1]
    for flip, out in zip(flips, outs):
        columns = pl.ds(pl.multiple_of(lax.bitwise_xor(head, flip) * width, width), width)
        terms = dot(own[...], own_w[:, columns]) + dot(other[...], other_w[:, columns])
        out[...] = terms.astype(out.dtype)


def sum_kernel(own, a, b, c, out):
    core = lax.rem(lax.axis_index("head"), 2)
    half = own.shape[0]
    here = own[...] + a[...].astype(F32)
    there = c[...].astype(F32) + b[...].astype(F32)
    out[pl.ds(pl.multiple_of(core * half, half), half), :] = here.astype(BF16)
    out[pl.ds(pl.multiple_of((1 - core) * half, half), half), :] = there.astype(BF16)


def turn_kernel(pieces, signal, *refs):
    own, beside = refs[:pieces], refs[pieces : pieces + pieces // 2]
    held, turned, sems = refs[pieces + pieces // 2 :]
    me = lax.axis_index("seq")
    share = own[0].shape[0]
    parts = held.shape[0]
    wide = held.shape[2]
    sources = [signal.at[:, n * wide : (n + 1) * wide] for n in range(parts)]
    copies = fetch(sources, [held.at[n] for n in range(parts)], sems)
    for n, copy in enumerate(copies):
        copy.wait()
        turned[n * (wide // share) : (n + 1) * (wide // share)] = held[n].T.reshape(-1, share, held.shape[1])
    for k in range(pieces):
        own[k][...] = turned[lax.bitwise_xor(me, 2 * k)]
        beside[k // 2][k % 2] = turned[lax.bitwise_xor(me, 2 * k + 1)]


def call(kernel, outs, *args, scratch=(), flops=0, grant=12, space=VMEM):
    run = pl.pallas_call(
        kernel,
        out_shape=outs,
        in_specs=[pl.BlockSpec(memory_space=space)] * len(args),
        out_specs=jax.tree.map(lambda _: pl.BlockSpec(memory_space=VMEM), outs),
        scratch_shapes=list(scratch),
        cost_estimate=pl.CostEstimate(flops=flops, bytes_accessed=0, transcendentals=0),
        compiler_params=pltpu.CompilerParams(vmem_limit_bytes=grant << 20),
    )
    if space is not VMEM:
        args = [pltpu.with_memory_space_constraint(arg, space) for arg in args]
    return run(*args)


def shape(dims, dtype=BF16):
    return jax.ShapeDtypeStruct(dims, dtype)


def flip(x, axis, by):
    size = lax.axis_size(axis)
    return lax.ppermute(x, axis, [(i, i ^ by) for i in range(size)])


def spread(signal, gate, skip, w_first, b_first, freq, w_mid, w_last, rate, out_w):
    length_local, channels = signal.shape
    ranks, heads = lax.axis_size("seq"), lax.axis_size("head")
    pieces = ranks // 2
    share = channels // ranks
    blocks = ranks * length_local // BLOCK
    taps = K // BLOCK
    half = length_local // 2
    width = out_w.shape[1] // heads
    row = lambda v: v.reshape(1, -1)

    piece, pair = shape((share, length_local)), shape((2, share, length_local))
    *own, near, far = call(
        functools.partial(turn_kernel, pieces),
        (piece,) * pieces + (pair,) * 2,
        signal,
        scratch=[
            pltpu.VMEM((channels // 128, length_local, 128), BF16),
            pltpu.VMEM((ranks, share, length_local), BF16),
            pltpu.SemaphoreType.DMA((channels // 128,)),
        ],
        space=pltpu.HBM,
    )
    far = flip(far, "seq", 1)
    near = flip(near, "seq", 1)
    beside = [near[0], near[1], far[0], far[1]]
    parts = {k: flip(jnp.stack([own[k], beside[k]]), "seq", 2 * k) for k in (2, 3, 1)}

    forward_high, forward_low = split(forward_table())
    back_high, back_low = split(backward_table())
    filter_table = np.concatenate([forward_high[:BLOCK], forward_low[:BLOCK]], 0)
    operands = (
        jnp.asarray(feature_table()),
        w_first,
        row(b_first),
        row(freq),
        w_mid,
        w_last,
        row(rate),
        jnp.asarray(filter_table),
    )
    filt = call(
        functools.partial(filter_kernel, len(operands)),
        shape((taps, share, 2 * BLOCK), F32),
        *operands,
        scratch=[pltpu.VMEM(v.shape, v.dtype) for v in operands]
        + [
            pltpu.VMEM((128, w_last.shape[0]), F32),
            pltpu.VMEM((128, BLOCK), F32),
            pltpu.SemaphoreType.DMA((len(operands),)),
        ],
        flops=5_000_000_000,
        space=pltpu.HBM,
    )
    other_w = flip(out_w, "head", 1)
    conv_own, conv_beside, *convs = call(
        functools.partial(conv_kernel, pieces),
        (piece,) * 2 + (pair,) * (pieces - 1),
        filt,
        forward_high,
        forward_low,
        back_high,
        back_low,
        own[0],
        near,
        *[parts[k] for k in range(1, pieces)],
        scratch=[
            pltpu.VMEM((blocks + 1, share, BLOCK), BF16),
            pltpu.VMEM((blocks, share, 2 * BLOCK), F32),
            pltpu.VMEM((blocks, share, 2 * BLOCK), F32),
            pltpu.VMEM((blocks, share, BLOCK), BF16),
        ],
        flops=3_000_000_000,
    )

    got = {k: flip(convs[k - 1], "seq", 2 * k) for k in (2, 3, 1)}
    near = flip(jnp.stack([conv_beside, got[1][1]]), "seq", 1)
    far = flip(jnp.stack([got[2][1], got[3][1]]), "seq", 1)
    mixed = shape((half, channels))
    keep, send = call(
        functools.partial(mix_kernel, pieces),
        (mixed, mixed),
        signal,
        gate,
        row(skip),
        conv_own,
        got[1],
        got[2],
        got[3],
        near,
        far,
        scratch=[pltpu.VMEM((ranks, share, length_local), BF16)],
        flops=500_000_000,
    )
    received = flip(send, "head", 1)
    terms, wide = shape((half, width)), shape((half, width), F32)
    a, b, c, here = call(
        functools.partial(project_kernel, (2, 3, 1, 0)),
        (terms, terms, wide, wide),
        keep,
        received,
        out_w,
        other_w,
        flops=500_000_000,
    )
    a, b, c = flip(a, "head", 2), flip(b, "head", 3), flip(c, "head", 1)
    return call(sum_kernel, shape((length_local, width)), here, a, b, c)


def shifted(x, axis, by):
    size = lax.axis_size(axis)
    pairs = [(i, i + by) for i in range(size) if 0 <= i + by < size]
    return lax.ppermute(x, axis, pairs)


def make_filter(w_first, b_first, freq, w_mid, w_last, rate, count):
    position = jnp.arange(count).astype(jnp.float32)
    bands = jnp.arange(1, BANDS + 1).astype(jnp.float32)
    angles = 2.0 * math.pi * position[:, None] * bands[None, :] / K
    features = jnp.concatenate([position[:, None] / K, jnp.cos(angles), jnp.sin(angles)], 1)
    first = jnp.sin(freq * (jnp.dot(features, w_first, precision=HIGHEST) + b_first))
    second = jnp.sin(freq * jnp.dot(first, w_mid, precision=HIGHEST))
    raw = jnp.dot(second, w_last, precision=HIGHEST)
    return (raw * jnp.exp(-rate[None, :] * position[:, None])).astype(jnp.bfloat16)


def transform_tables(block):
    doubled = 2 * block
    taps = jnp.arange(block)
    freqs = jnp.arange(block)
    outputs = jnp.arange(doubled)
    scale_angle = 2.0 * math.pi / doubled
    phase = (freqs[:, None] * taps[None, :] % doubled).astype(jnp.float32) * scale_angle
    alternate = (1 - 2 * (taps % 2)).astype(jnp.float32)
    forward_real = jnp.cos(phase)
    forward_imag = jnp.where(freqs[:, None] == 0, alternate[None, :], -jnp.sin(phase))
    phase_back = (outputs[:, None] * freqs[None, :] % doubled).astype(jnp.float32) * scale_angle
    alternate_back = (1 - 2 * (outputs % 2)).astype(jnp.float32)
    weights = jnp.where(freqs == 0, 1.0, 2.0).astype(jnp.float32)
    back_real = weights[None, :] * jnp.cos(phase_back) / doubled
    back_imag = (
        jnp.where(freqs[None, :] == 0, alternate_back[:, None], -2.0 * jnp.sin(phase_back))
        / doubled
    )
    return (forward_real, forward_imag, back_real, back_imag)


def long_convolve(padded, filt, length_local):
    channels = padded.shape[1]
    block = min(128, length_local)
    segments = K // block
    out_blocks = length_local // block
    in_blocks = padded.shape[0] // block
    forward_real, forward_imag, back_real, back_imag = transform_tables(block)
    values = padded.astype(jnp.float32).reshape(in_blocks, block, channels)
    kernels = filt.astype(jnp.float32).reshape(segments, block, channels)[::-1]
    spec_real = jnp.einsum("ft,ntc->nfc", forward_real, values, precision=HIGHEST)
    spec_imag = jnp.einsum("ft,ntc->nfc", forward_imag, values, precision=HIGHEST)
    kern_real = jnp.einsum("ft,ntc->nfc", forward_real, kernels, precision=HIGHEST)
    kern_imag = jnp.einsum("ft,ntc->nfc", forward_imag, kernels, precision=HIGHEST)
    upper = (jnp.arange(block) >= 1).astype(jnp.float32)[:, None]
    sums_real = []
    sums_imag = []
    for index in range(out_blocks + 1):
        window_real = spec_real[index : index + segments]
        window_imag = spec_imag[index : index + segments]
        both_imag = kern_imag * window_imag
        sums_real.append(jnp.sum(kern_real * window_real - upper * both_imag, 0))
        cross = kern_real * window_imag + kern_imag * window_real
        sums_imag.append(jnp.sum(upper * cross + (1.0 - upper) * both_imag, 0))
    total_real = jnp.stack(sums_real, 0)
    total_imag = jnp.stack(sums_imag, 0)
    pieces = jnp.einsum("tf,kfc->ktc", back_real, total_real, precision=HIGHEST)
    pieces = pieces + jnp.einsum("tf,kfc->ktc", back_imag, total_imag, precision=HIGHEST)
    joined = pieces[1:, :block] + pieces[:-1, block:]
    return joined.reshape(length_local, channels)


def halo(signal, gate, skip, w_first, b_first, freq, w_mid, w_last, rate, out_w):
    length_local, _ = signal.shape
    filt = make_filter(w_first, b_first, freq, w_mid, w_last, rate, K)
    reach = K // length_local
    earlier = [shifted(signal, "seq", step) for step in range(reach, 0, -1)]
    padded = jnp.concatenate(earlier + [signal], 0)
    conv = long_convolve(padded, filt, length_local)
    mixed = (gate.astype(jnp.float32) * (conv + skip[None, :] * signal.astype(jnp.float32))).astype(
        jnp.bfloat16
    )
    terms = jnp.dot(mixed, out_w, preferred_element_type=jnp.float32)
    result = lax.psum_scatter(terms, "head", scatter_dimension=1, tiled=True)
    return result.astype(jnp.bfloat16)


def local(signal, *rest):
    ranks, heads = lax.axis_size("seq"), lax.axis_size("head")
    length_local, channels = signal.shape
    share = channels // ranks
    small = ranks == 8 and ranks * length_local <= K and heads == 4 and length_local == 2 * BLOCK
    if small and channels % ranks == 0 and share % 16 == 0 and 128 % share == 0:
        return spread(signal, *rest)
    return halo(signal, *rest)


def solution(mesh):
    placed = (
        P("seq", "head"),
        P("seq", "head"),
        P("head"),
        P(),
        P(),
        P(),
        P(),
        P(None, "head"),
        P("head"),
        P("head", None),
    )
    return jax.shard_map(
        local, mesh=mesh, in_specs=placed, out_specs=P("seq", "head"), check_vma=False
    )
```

time: 68.9 us -> 45.4 us (0.66)
  Pallas kernels: 22.2 us -> 9.09 us
  local copies, waits for them, and re-layouts: 13 us -> 0.06 us
  starting transfers between devices: 14.6 us -> 18.5 us
  other arithmetic: 1.34 us -> 0.04 us
    pallas_call x7 -> x6, Pallas kernels: 22.2 us -> 9.09 us  [call(): return run(*args)]
    unnamed x29 -> x16, local copies, waits for them, and re-layouts: 6.95 us -> 0.04 us
    reshape x4 -> x0, local copies, waits for them, and re-layouts: 4.18 us -> none  [spread(): column = lambda v: v.reshape(-1, 1)]
    ppermute x13 -> x15, starting transfers between devices: 14.6 us -> 18.5 us  [flip(): return lax.ppermute(x, axis, [(i, i ^ by) for i in range(size)])]
    dynamic_slice x2 -> x0, local copies, waits for them, and re-layouts: 1.06 us -> none  [the longest x1 0.99 us: spread(): send = lax.dynamic_index_in_dim(turned, 1 - side, 1, keepdims=True)]
    slice x4 -> x5, local copies, waits for them, and re-layouts: 0.77 us -> 0.02 us  [the longest x2 0.01 us: spread(): beside = [near[0], near[1], far[0], far[1]]]
    ppermute x13 -> x15, waiting for transfers between devices: 17.1 us -> 17.4 us  [flip(): return lax.ppermute(x, axis, [(i, i ^ by) for i in range(size)])]
  transfers between devices with their start and end apart: 13 -> 15, of which waited for: 8 -> 8; matrix products, arithmetic and copies ran while one was open for 16% -> 0% of each run, Pallas kernels for 25% -> 17%
where the time goes in v2:
time: 45.4 us; the launch traced here: 45.2 us
  starting transfers between devices  18.5 us (41%)
  waiting for transfers between devices  17.4 us (38%)
  Pallas kernels  9.09 us (20%)
    ppermute x15, starting transfers between devices, flip(): return lax.ppermute(x, axis, [(i, i ^ by) for i in range(size)])  18.5 us
    ppermute x15, waiting for transfers between devices, flip(): return lax.ppermute(x, axis, [(i, i ^ by) for i in range(size)])  17.4 us
    pallas_call x6, Pallas kernels, call(): return run(*args)  9.09 us
  transfers between devices with their start and end apart: 15, of which 8 were waited for; matrix products, arithmetic and copies ran while one was open for 0% of the time, Pallas kernels for 17%

profile of v2, /device:TPU:0, one launch (start us, length us, event | category | flops | bytes accessed | tf_op | source)
XLA Modules:
  0.0 45.2 jit_solution(1245027539127610429)
XLA Ops:
  0.0 0.5 %collective-permute-start.11 = (bf16[512,2048]{1,0:T(8,128)(2,1)}, bf16[512,2048]{1,0:T(8,128)(2,1)S(1)}, u32[]{:S(2)}, u32[]{:S(2)}) collective-permute-start(bf16[512,2048]{1,0:T(8,128)(2,1)} %own_w.1), channel_id=1, source_target_pairs={{0,1},{1,0},{2,3},{3,2},{4,5},{5,4},{6,7},{7,6},{8,9},{9,8},{10,11... | collective-permute-start | bytes 6291464 | tf_op jit(solution)/shard_map/ppermute | solution.py:269
  0.5 1.2 %shard_map.155 = (bf16[64,256]{1,0:T(8,128)(2,1)S(1)}, bf16[64,256]{1,0:T(8,128)(2,1)S(1)}, bf16[64,256]{1,0:T(8,128)(2,1)S(1)}, bf16[64,256]{1,0:T(8,128)(2,1)S...) custom-call(bf16[256,512]{1,0:T(8,128)(2,1)} %signal.3), custom_call_target="tpu_custom_call" | custom-call | tf_op jit(solution)/shard_map/pallas_call | solution.py:260
  1.7 2.6 %collective-permute-start = (bf16[2,64,256]{2,1,0:T(8,128)(2,1)S(1)}, bf16[2,64,256]{2,1,0:T(8,128)(2,1)S(1)}, u32[]{:S(2)}, u32[]{:S(2)}) collective-permute-start(bf16[2,64,256]{2,1,0:T(8,128)(2,1)S(1)} %get-tuple-element.23), channel_id=1, source_target_pairs={{0,4},{4,0},{8,12},{12,8},{16,20},{20,16},{24,28},{28,24},{1,5},{5... | collective-permute-start | bytes 196616 | tf_op jit(solution)/shard_map/ppermute | solution.py:269
  4.3 0.1 collective-permute-start.2
  4.3 2.7 %collective-permute-done.refs_1_ = bf16[2,64,256]{2,1,0:T(8,128)(2,1)S(1)} collective-permute-done((bf16[2,64,256]{2,1,0:T(8,128)(2,1)S(1)}, bf16[2,64,256]{2,1,0:T(8,128)(2,1)S(1)}, u32[]{:S(2)}, u32[]{:S(2)}) %collective-permute-start) | collective-permute-done | bytes 65568 | tf_op jit(solution)/shard_map/ppermute | solution.py:269
  7.0 2.0 %collective-permute-start.1 = (bf16[2,64,256]{2,1,0:T(8,128)(2,1)S(1)}, bf16[2,64,256]{2,1,0:T(8,128)(2,1)S(1)}, u32[]{:S(2)}, u32[]{:S(2)}) collective-permute-start(bf16[2,64,256]{2,1,0:T(8,128)(2,1)S(1)} %pad_maximum_fusion), channel_id=1, source_target_pairs={{0,8},{4,12},{8,0},{12,4},{16,24},{20,28},{24,16},{28,20},{1,9},{5... | collective-permute-start | bytes 196616 | tf_op jit(solution)/shard_map/ppermute | solution.py:269
  9.1 0.0 collective-permute-done.2
  9.1 2.7 %collective-permute-start.3 = (bf16[2,64,256]{2,1,0:T(8,128)(2,1)S(1)}, bf16[2,64,256]{2,1,0:T(8,128)(2,1)S(1)}, u32[]{:S(2)}, u32[]{:S(2)}) collective-permute-start(bf16[2,64,256]{2,1,0:T(8,128)(2,1)S(1)} %pad_maximum_fusion.1), channel_id=1, source_target_pairs={{0,16},{4,20},{8,24},{12,28},{16,0},{20,4},{24,8},{28,12},{1,17},{... | collective-permute-start | bytes 196616 | tf_op jit(solution)/shard_map/ppermute | solution.py:269
  11.7 1.0 %collective-permute-start.4 = (bf16[2,64,256]{2,1,0:T(8,128)(2,1)S(1)}, bf16[2,64,256]{2,1,0:T(8,128)(2,1)S(1)}, u32[]{:S(2)}, u32[]{:S(2)}) collective-permute-start(bf16[2,64,256]{2,1,0:T(8,128)(2,1)S(1)} %pad_maximum_fusion.2), channel_id=1, source_target_pairs={{0,24},{4,28},{8,16},{12,20},{16,8},{20,12},{24,0},{28,4},{1,25},{... | collective-permute-start | bytes 196616 | tf_op jit(solution)/shard_map/ppermute | solution.py:269
  12.7 3.4 %shard_map.154.filt = f32[16,64,256]{2,1,0:T(8,128)S(1)} custom-call(f32[33,2048]{1,0:T(8,128)} %constant.12.clone.refs_0_, f32[33,64]{1,0:T(8,128)} %refs_1_.1, f32[1,64]{1,0:T(1,128)} %bitcast.14, f32[1,64]{1,0:T(1,128)} %bitcast.15, f32[64,64]{1,0:T(8,128)} %refs_4_.1, f32[64,512]{1,0:T(8,128)} %refs_5_.1, f32[1,512]{1,0:T(1,128)} %bitcast.13, ...), custom_call_target="tpu_custom_call" | custom-call | flops 5000000000 | tf_op jit(solution)/shard_map/pallas_call | solution.py:260
  16.2 0.0 collective-permute-done.1.refs_2_
  16.2 0.0 collective-permute-done.3.refs_3_
  16.2 1.7 %collective-permute-done.4.refs_4_ = bf16[2,64,256]{2,1,0:T(8,128)(2,1)S(1)} collective-permute-done((bf16[2,64,256]{2,1,0:T(8,128)(2,1)S(1)}, bf16[2,64,256]{2,1,0:T(8,128)(2,1)S(1)}, u32[]{:S(2)}, u32[]{:S(2)}) %collective-permute-start.4) | collective-permute-done | bytes 65568 | tf_op jit(solution)/shard_map/ppermute | solution.py:269
  17.9 0.0 copy-done.4
  18.0 0.0 copy-done.5
  18.0 0.0 copy-done.6
  18.0 0.0 copy-done.7
  18.0 0.0 copy-start.1
  18.0 0.0 copy-start.2
  18.0 0.0 copy-start.3
  18.0 2.8 %shard_map.156 = (bf16[64,256]{1,0:T(8,128)(2,1)S(1)}, bf16[64,256]{1,0:T(8,128)(2,1)S(1)}, bf16[2,64,256]{2,1,0:T(8,128)(2,1)S(1)}, bf16[2,64,256]{2,1,0:T(8,128)(2,1)S(1)}, bf16[2,64,256]{2,1,0:T(8,128)(2,1)S(1)}) custom-call(f32[16,64,256]{2,1,0:T(8,128)S(1)} %shard_map.154.filt, bf16[256,256]{1,0:T(8,128)(2,1)S(1)} %copy-done.5, ...), custom_call_target="tpu_custom_call" | custom-call | flops 3000000000 | tf_op jit(solution)/shard_map/pallas_call | solution.py:260
  20.8 0.0 copy-start
  20.8 0.3 collective-permute-start.5
  21.1 2.3 %collective-permute-start.6 = (bf16[2,64,256]{2,1,0:T(8,128)(2,1)S(1)}, bf16[2,64,256]{2,1,0:T(8,128)(2,1)S(1)}, u32[]{:S(2)}, u32[]{:S(2)}) collective-permute-start(bf16[2,64,256]{2,1,0:T(8,128)(2,1)S(1)} %get-tuple-element.30), channel_id=1, source_target_pairs={{0,16},{4,20},{8,24},{12,28},{16,0},{20,4},{24,8},{28,12},{1,17},{... | collective-permute-start | bytes 196616 | tf_op jit(solution)/shard_map/ppermute | solution.py:269
  23.4 1.9 %collective-permute-start.7 = (bf16[2,64,256]{2,1,0:T(8,128)(2,1)S(1)}, bf16[2,64,256]{2,1,0:T(8,128)(2,1)S(1)}, u32[]{:S(2)}, u32[]{:S(2)}) collective-permute-start(bf16[2,64,256]{2,1,0:T(8,128)(2,1)S(1)} %get-tuple-element.31), channel_id=1, source_target_pairs={{0,24},{4,28},{8,16},{12,20},{16,8},{20,12},{24,0},{28,4},{1,25},{... | collective-permute-start | bytes 196616 | tf_op jit(solution)/shard_map/ppermute | solution.py:269
  25.3 0.2 collective-permute-done.5.refs_0_
  25.5 1.6 %collective-permute-start.8 = (bf16[2,64,256]{2,1,0:T(8,128)(2,1)S(1)}, bf16[2,64,256]{2,1,0:T(8,128)(2,1)S(1)}, u32[]{:S(2)}, u32[]{:S(2)}) collective-permute-start(bf16[2,64,256]{2,1,0:T(8,128)(2,1)S(1)} %pad_maximum_fusion.3), channel_id=1, source_target_pairs={{0,4},{4,0},{8,12},{12,8},{16,20},{20,16},{24,28},{28,24},{1,5},{5... | collective-permute-start | bytes 196616 | tf_op jit(solution)/shard_map/ppermute | solution.py:269
  27.1 2.5 %collective-permute-done.6.refs_1_ = bf16[2,64,256]{2,1,0:T(8,128)(2,1)S(1)} collective-permute-done((bf16[2,64,256]{2,1,0:T(8,128)(2,1)S(1)}, bf16[2,64,256]{2,1,0:T(8,128)(2,1)S(1)}, u32[]{:S(2)}, u32[]{:S(2)}) %collective-permute-start.6) | collective-permute-done | bytes 65568 | tf_op jit(solution)/shard_map/ppermute | solution.py:269
  29.6 0.0 collective-permute-done.7.refs_2_
  29.6 1.6 %collective-permute-start.9 = (bf16[2,64,256]{2,1,0:T(8,128)(2,1)S(1)}, bf16[2,64,256]{2,1,0:T(8,128)(2,1)S(1)}, u32[]{:S(2)}, u32[]{:S(2)}) collective-permute-start(bf16[2,64,256]{2,1,0:T(8,128)(2,1)S(1)} %pad_maximum_fusion.4), channel_id=1, source_target_pairs={{0,4},{4,0},{8,12},{12,8},{16,20},{20,16},{24,28},{28,24},{1,5},{5... | collective-permute-start | bytes 196616 | tf_op jit(solution)/shard_map/ppermute | solution.py:269
  31.3 0.0 collective-permute-done.8.refs_3_
  31.3 2.7 %collective-permute-done.9.refs_4_ = bf16[2,64,256]{2,1,0:T(8,128)(2,1)S(1)} collective-permute-done((bf16[2,64,256]{2,1,0:T(8,128)(2,1)S(1)}, bf16[2,64,256]{2,1,0:T(8,128)(2,1)S(1)}, u32[]{:S(2)}, u32[]{:S(2)}) %collective-permute-start.9) | collective-permute-done | bytes 65568 | tf_op jit(solution)/shard_map/ppermute | solution.py:269
  34.0 0.0 copy-done.1
  34.0 0.0 copy-done.2
  34.0 0.0 copy-done.3
  34.0 0.2 shard_map.157
  34.2 0.1 collective-permute-start.10
  34.2 1.3 %collective-permute-done.10.other = bf16[128,512]{1,0:T(8,128)(2,1)S(1)} collective-permute-done((bf16[128,512]{1,0:T(8,128)(2,1)S(1)}, bf16[128,512]{1,0:T(8,128)(2,1)S(1)}, u32[]{:S(2)}, u32[]{:S(2)}) %collective-permute-start.10) | collective-permute-done | bytes 131104 | tf_op jit(solution)/shard_map/ppermute | solution.py:269
  35.6 0.0 collective-permute-done.11.other_w
  35.6 0.0 copy-done
  35.6 0.7 %shard_map.158 = (bf16[128,512]{1,0:T(8,128)(2,1)S(1)}, bf16[128,512]{1,0:T(8,128)(2,1)S(1)}, f32[128,512]{1,0:T(8,128)S(1)}, f32[128,512]{1,0:T(8,128)S(1)}) custom-call(bf16[128,512]{1,0:T(8,128)(2,1)S(1)} %get-tuple-element.33.own, bf16[128,512]{1,0:T(8,128)(2,1)S(1)} %collective-permute-done.10.other, bf16[512,2048]{1,0:T(8,128)(2,1)S(1)} %copy-done, ...), custom_call_target="tpu_custom_call" | custom-call | flops 500000000 | tf_op jit(solution)/shard_map/pallas_call | solution.py:260
  36.3 0.2 collective-permute-start.14
  36.5 1.5 %collective-permute-start.12 = (bf16[128,512]{1,0:T(8,128)(2,1)S(1)}, bf16[128,512]{1,0:T(8,128)(2,1)S(1)}, u32[]{:S(2)}, u32[]{:S(2)}) collective-permute-start(bf16[128,512]{1,0:T(8,128)(2,1)S(1)} %get-tuple-element.36), channel_id=1, source_target_pairs={{0,2},{1,3},{2,0},{3,1},{4,6},{5,7},{6,4},{7,5},{8,10},{9,11},{10,... | collective-permute-start | bytes 393224 | tf_op jit(solution)/shard_map/ppermute | solution.py:269
  38.0 0.2 collective-permute-start.13
  38.2 4.7 %collective-permute-done.12.a = bf16[128,512]{1,0:T(8,128)(2,1)S(1)} collective-permute-done((bf16[128,512]{1,0:T(8,128)(2,1)S(1)}, bf16[128,512]{1,0:T(8,128)(2,1)S(1)}, u32[]{:S(2)}, u32[]{:S(2)}) %collective-permute-start.12) | collective-permute-done | bytes 131104 | tf_op jit(solution)/shard_map/ppermute | solution.py:269
  42.9 1.6 %collective-permute-done.13.b = bf16[128,512]{1,0:T(8,128)(2,1)S(1)} collective-permute-done((bf16[128,512]{1,0:T(8,128)(2,1)S(1)}, bf16[128,512]{1,0:T(8,128)(2,1)S(1)}, u32[]{:S(2)}, u32[]{:S(2)}) %collective-permute-start.13) | collective-permute-done | bytes 131104 | tf_op jit(solution)/shard_map/ppermute | solution.py:269
  44.5 0.0 collective-permute-done.14.c
  44.5 0.7 %shard_map.159 = bf16[256,512]{1,0:T(8,128)(2,1)} custom-call(f32[128,512]{1,0:T(8,128)S(1)} %get-tuple-element.35.own, bf16[128,512]{1,0:T(8,128)(2,1)S(1)} %collective-permute-done.12.a, bf16[128,512]{1,0:T(8,128)(2,1)S(1)} %collective-permute-done.13.b, f32[128,512]{1,0:T(8,128)S(1)} %collective-permute-done.14.c), custom_call_target="tpu_custom_call" | custom-call | tf_op jit(solution)/shard_map/pallas_call | solution.py:260
  (14 shorter events, 0.1 us)
Async XLA Ops:
  0.0 35.6 %collective-permute-start.11 = (bf16[512,2048]{1,0:T(8,128)(2,1)}, bf16[512,2048]{1,0:T(8,128)(2,1)S(1)}, u32[]{:S(2)}, u32[]{:S(2)}) collective-permute-start(bf16[512,2048]{1,0:T(8,128)(2,1)} %own_w.1), channel_id=1, source_target_pairs={{0,1},{1,0},{2,3},{3,2},{4,5},{5,4},{6,7},{7,6},{8,9},{9,8},{10,11... | collective-permute-start | bytes 6291464 | tf_op jit(solution)/shard_map/ppermute | solution.py:269
  1.7 5.3 %collective-permute-start = (bf16[2,64,256]{2,1,0:T(8,128)(2,1)S(1)}, bf16[2,64,256]{2,1,0:T(8,128)(2,1)S(1)}, u32[]{:S(2)}, u32[]{:S(2)}) collective-permute-start(bf16[2,64,256]{2,1,0:T(8,128)(2,1)S(1)} %get-tuple-element.23), channel_id=1, source_target_pairs={{0,4},{4,0},{8,12},{12,8},{16,20},{20,16},{24,28},{28,24},{1,5},{5... | collective-permute-start | bytes 196616 | tf_op jit(solution)/shard_map/ppermute | solution.py:269
  4.3 4.8 %collective-permute-start.2 = (bf16[2,64,256]{2,1,0:T(8,128)(2,1)S(1)}, bf16[2,64,256]{2,1,0:T(8,128)(2,1)S(1)}, u32[]{:S(2)}, u32[]{:S(2)}) collective-permute-start(bf16[2,64,256]{2,1,0:T(8,128)(2,1)S(1)} %get-tuple-element.26), channel_id=1, source_target_pairs={{0,4},{4,0},{8,12},{12,8},{16,20},{20,16},{24,28},{28,24},{1,5},{5... | collective-permute-start | bytes 196616 | tf_op jit(solution)/shard_map/ppermute | solution.py:269
  7.0 9.2 %collective-permute-start.1 = (bf16[2,64,256]{2,1,0:T(8,128)(2,1)S(1)}, bf16[2,64,256]{2,1,0:T(8,128)(2,1)S(1)}, u32[]{:S(2)}, u32[]{:S(2)}) collective-permute-start(bf16[2,64,256]{2,1,0:T(8,128)(2,1)S(1)} %pad_maximum_fusion), channel_id=1, source_target_pairs={{0,8},{4,12},{8,0},{12,4},{16,24},{20,28},{24,16},{28,20},{1,9},{5... | collective-permute-start | bytes 196616 | tf_op jit(solution)/shard_map/ppermute | solution.py:269
  9.1 7.1 %collective-permute-start.3 = (bf16[2,64,256]{2,1,0:T(8,128)(2,1)S(1)}, bf16[2,64,256]{2,1,0:T(8,128)(2,1)S(1)}, u32[]{:S(2)}, u32[]{:S(2)}) collective-permute-start(bf16[2,64,256]{2,1,0:T(8,128)(2,1)S(1)} %pad_maximum_fusion.1), channel_id=1, source_target_pairs={{0,16},{4,20},{8,24},{12,28},{16,0},{20,4},{24,8},{28,12},{1,17},{... | collective-permute-start | bytes 196616 | tf_op jit(solution)/shard_map/ppermute | solution.py:269
  11.7 6.2 %collective-permute-start.4 = (bf16[2,64,256]{2,1,0:T(8,128)(2,1)S(1)}, bf16[2,64,256]{2,1,0:T(8,128)(2,1)S(1)}, u32[]{:S(2)}, u32[]{:S(2)}) collective-permute-start(bf16[2,64,256]{2,1,0:T(8,128)(2,1)S(1)} %pad_maximum_fusion.2), channel_id=1, source_target_pairs={{0,24},{4,28},{8,16},{12,20},{16,8},{20,12},{24,0},{28,4},{1,25},{... | collective-permute-start | bytes 196616 | tf_op jit(solution)/shard_map/ppermute | solution.py:269
  12.7 5.2 %copy-start.4 = (bf16[256,256]{1,0:T(8,128)(2,1)S(1)}, bf16[256,256]{1,0:T(8,128)(2,1)}, u32[]{:S(2)}) copy-start(bf16[256,256]{1,0:T(8,128)(2,1)} %constant.15.clone.table_low) | copy-start | bytes 393220
  12.7 5.2 %copy-start.5 = (bf16[256,256]{1,0:T(8,128)(2,1)S(1)}, bf16[256,256]{1,0:T(8,128)(2,1)}, u32[]{:S(2)}) copy-start(bf16[256,256]{1,0:T(8,128)(2,1)} %constant.14.clone.table_high) | copy-start | bytes 393220
  12.7 5.2 %copy-start.6 = (bf16[256,128]{1,0:T(8,128)(2,1)S(1)}, bf16[256,128]{1,0:T(8,128)(2,1)}, u32[]{:S(2)}) copy-start(bf16[256,128]{1,0:T(8,128)(2,1)} %constant.17.clone.back_low) | copy-start | bytes 196612
  12.7 5.2 %copy-start.7 = (bf16[256,128]{1,0:T(8,128)(2,1)S(1)}, bf16[256,128]{1,0:T(8,128)(2,1)}, u32[]{:S(2)}) copy-start(bf16[256,128]{1,0:T(8,128)(2,1)} %constant.16.clone.back_high) | copy-start | bytes 196612
  18.0 16.0 %copy-start.1 = (bf16[256,512]{1,0:T(8,128)(2,1)S(1)}, bf16[256,512]{1,0:T(8,128)(2,1)}, u32[]{:S(2)}) copy-start(bf16[256,512]{1,0:T(8,128)(2,1)} %signal.3) | copy-start | bytes 786436
  18.0 16.0 %copy-start.2 = (bf16[256,512]{1,0:T(8,128)(2,1)S(1)}, bf16[256,512]{1,0:T(8,128)(2,1)}, u32[]{:S(2)}) copy-start(bf16[256,512]{1,0:T(8,128)(2,1)} %gate.1) | copy-start | bytes 786436
  18.0 16.0 %copy-start.3 = (f32[512]{0:T(512)S(1)}, f32[512]{0:T(512)}, u32[]{:S(2)}) copy-start(f32[512]{0:T(512)} %param.18) | copy-start | bytes 6148
  20.8 14.8 %copy-start = (bf16[512,2048]{1,0:T(8,128)(2,1)S(1)}, bf16[512,2048]{1,0:T(8,128)(2,1)}, u32[]{:S(2)}) copy-start(bf16[512,2048]{1,0:T(8,128)(2,1)} %own_w.1) | copy-start | bytes 6291460
  20.8 4.6 %collective-permute-start.5 = (bf16[2,64,256]{2,1,0:T(8,128)(2,1)S(1)}, bf16[2,64,256]{2,1,0:T(8,128)(2,1)S(1)}, u32[]{:S(2)}, u32[]{:S(2)}) collective-permute-start(bf16[2,64,256]{2,1,0:T(8,128)(2,1)S(1)} %get-tuple-element.29), channel_id=1, source_target_pairs={{0,8},{4,12},{8,0},{12,4},{16,24},{20,28},{24,16},{28,20},{1,9},{5... | collective-permute-start | bytes 196616 | tf_op jit(solution)/shard_map/ppermute | solution.py:269
  21.1 8.5 %collective-permute-start.6 = (bf16[2,64,256]{2,1,0:T(8,128)(2,1)S(1)}, bf16[2,64,256]{2,1,0:T(8,128)(2,1)S(1)}, u32[]{:S(2)}, u32[]{:S(2)}) collective-permute-start(bf16[2,64,256]{2,1,0:T(8,128)(2,1)S(1)} %get-tuple-element.30), channel_id=1, source_target_pairs={{0,16},{4,20},{8,24},{12,28},{16,0},{20,4},{24,8},{28,12},{1,17},{... | collective-permute-start | bytes 196616 | tf_op jit(solution)/shard_map/ppermute | solution.py:269
  23.4 6.2 %collective-permute-start.7 = (bf16[2,64,256]{2,1,0:T(8,128)(2,1)S(1)}, bf16[2,64,256]{2,1,0:T(8,128)(2,1)S(1)}, u32[]{:S(2)}, u32[]{:S(2)}) collective-permute-start(bf16[2,64,256]{2,1,0:T(8,128)(2,1)S(1)} %get-tuple-element.31), channel_id=1, source_target_pairs={{0,24},{4,28},{8,16},{12,20},{16,8},{20,12},{24,0},{28,4},{1,25},{... | collective-permute-start | bytes 196616 | tf_op jit(solution)/shard_map/ppermute | solution.py:269
  25.5 5.8 %collective-permute-start.8 = (bf16[2,64,256]{2,1,0:T(8,128)(2,1)S(1)}, bf16[2,64,256]{2,1,0:T(8,128)(2,1)S(1)}, u32[]{:S(2)}, u32[]{:S(2)}) collective-permute-start(bf16[2,64,256]{2,1,0:T(8,128)(2,1)S(1)} %pad_maximum_fusion.3), channel_id=1, source_target_pairs={{0,4},{4,0},{8,12},{12,8},{16,20},{20,16},{24,28},{28,24},{1,5},{5... | collective-permute-start | bytes 196616 | tf_op jit(solution)/shard_map/ppermute | solution.py:269
  29.6 4.3 %collective-permute-start.9 = (bf16[2,64,256]{2,1,0:T(8,128)(2,1)S(1)}, bf16[2,64,256]{2,1,0:T(8,128)(2,1)S(1)}, u32[]{:S(2)}, u32[]{:S(2)}) collective-permute-start(bf16[2,64,256]{2,1,0:T(8,128)(2,1)S(1)} %pad_maximum_fusion.4), channel_id=1, source_target_pairs={{0,4},{4,0},{8,12},{12,8},{16,20},{20,16},{24,28},{28,24},{1,5},{5... | collective-permute-start | bytes 196616 | tf_op jit(solution)/shard_map/ppermute | solution.py:269
  34.2 1.4 %collective-permute-start.10 = (bf16[128,512]{1,0:T(8,128)(2,1)S(1)}, bf16[128,512]{1,0:T(8,128)(2,1)S(1)}, u32[]{:S(2)}, u32[]{:S(2)}) collective-permute-start(bf16[128,512]{1,0:T(8,128)(2,1)S(1)} %get-tuple-element.34), channel_id=1, source_target_pairs={{0,1},{1,0},{2,3},{3,2},{4,5},{5,4},{6,7},{7,6},{8,9},{9,8},{10,11... | collective-permute-start | bytes 393224 | tf_op jit(solution)/shard_map/ppermute | solution.py:269
  36.3 8.2 %collective-permute-start.14 = (f32[128,512]{1,0:T(8,128)S(1)}, f32[128,512]{1,0:T(8,128)S(1)}, u32[]{:S(2)}, u32[]{:S(2)}) collective-permute-start(f32[128,512]{1,0:T(8,128)S(1)} %get-tuple-element.38), channel_id=1, source_target_pairs={{0,1},{1,0},{2,3},{3,2},{4,5},{5,4},{6,7},{7,6},{8,9},{9,8},{10,11... | collective-permute-start | bytes 786440 | tf_op jit(solution)/shard_map/ppermute | solution.py:269
  36.5 6.4 %collective-permute-start.12 = (bf16[128,512]{1,0:T(8,128)(2,1)S(1)}, bf16[128,512]{1,0:T(8,128)(2,1)S(1)}, u32[]{:S(2)}, u32[]{:S(2)}) collective-permute-start(bf16[128,512]{1,0:T(8,128)(2,1)S(1)} %get-tuple-element.36), channel_id=1, source_target_pairs={{0,2},{1,3},{2,0},{3,1},{4,6},{5,7},{6,4},{7,5},{8,10},{9,11},{10,... | collective-permute-start | bytes 393224 | tf_op jit(solution)/shard_map/ppermute | solution.py:269
  38.0 6.5 %collective-permute-start.13 = (bf16[128,512]{1,0:T(8,128)(2,1)S(1)}, bf16[128,512]{1,0:T(8,128)(2,1)S(1)}, u32[]{:S(2)}, u32[]{:S(2)}) collective-permute-start(bf16[128,512]{1,0:T(8,128)(2,1)S(1)} %get-tuple-element.37), channel_id=1, source_target_pairs={{0,3},{1,2},{2,1},{3,0},{4,7},{5,6},{6,5},{7,4},{8,11},{9,10},{10,... | collective-permute-start | bytes 393224 | tf_op jit(solution)/shard_map/ppermute | solution.py:269

commit v3 on v2

--- a/solution.py
+++ b/solution.py
@@ -89,14 +89,6 @@
     )
 
 
-def share_of(share):
-    me = lax.axis_index("seq")
-    groups = 128 // share
-    lanes = pl.ds(pl.multiple_of((me // groups) * 128, 128), 128)
-    rows = pl.ds(pl.multiple_of(lax.rem(me, groups) * share, share), share)
-    return lanes, rows
-
-
 def fetch(sources, targets, sems):
     copies = [
         pltpu.make_async_copy(source, target, sems.at[n])
@@ -107,101 +99,96 @@
     return copies
 
 
-def filter_kernel(count, *refs):
-    out, weights, scales, sems = refs[count], refs[2 * count + 1], refs[2 * count + 2], refs[2 * count + 3]
-    held = refs[count + 1 : 2 * count + 1]
+def hidden_kernel(count, *refs):
+    out, held, sems = refs[count], refs[count + 1 : 2 * count + 1], refs[2 * count + 1]
     for copy in fetch(refs[:count], held, sems):
         copy.wait()
-    feat, w_first, bias, freq, w_mid, w_last, rate, table = held
-    share = out.shape[1]
-    lanes, own = share_of(share)
+    feat, w_first, bias, freq, w_mid = held
     freqs = column(freq[...])
     first = sine(freqs * (dot_first(w_first[...], feat[...]) + column(bias[...])))
-    second = sine(freqs * dot_first(w_mid[...], first))
-    weights[...] = w_last[:, lanes].T
-    scales[...] = jnp.broadcast_to(column(rate[:, lanes]), scales.shape)
-    raw = jnp.dot(weights[own, :], second, precision=HIGHEST)
+    out[...] = sine(freqs * dot_first(w_mid[...], first))
+
+
+def filter_kernel(count, hidden, *refs):
+    out, held, sems = refs[count], refs[count + 1 : 2 * count + 1], refs[2 * count + 1]
+    for copy in fetch(refs[:count], held, sems):
+        copy.wait()
+    w_last, rate, table = held
+    share = out.shape[1]
+    own = pl.ds(pl.multiple_of((lax.axis_index("seq") // 2) * share, share), share)
+    raw = dot_first(w_last[:, own], hidden[...])
     taps = raw.shape[1]
-    decay = scales[own, :][:, :1]
     position = lax.broadcasted_iota(jnp.int32, (1, taps), 1).astype(F32)
-    filt = (raw * jnp.exp(-decay * position)).astype(BF16)
-    count = taps // BLOCK
-    rows = jnp.concatenate([filt[:, j * BLOCK : (j + 1) * BLOCK] for j in range(count)], 0)
+    filt = (raw * jnp.exp(-column(rate[:, own]) * position)).astype(BF16)
+    blocks = taps // BLOCK
+    rows = jnp.concatenate([filt[:, j * BLOCK : (j + 1) * BLOCK] for j in range(blocks)], 0)
     spec = dot(jnp.concatenate([rows, rows], 1), table[...])
     out[...] = spec.reshape(out.shape)
 
 
 def conv_kernel(pieces, filt, table_high, table_low, back_high, back_low, *refs):
-    own_in, beside_in = refs[:2]
-    ins, outs = refs[2 : pieces + 1], refs[pieces + 1 : 2 * pieces + 2]
-    samples, spec, total, result = refs[2 * pieces + 2 :]
+    ins, outs = refs[: 2 * pieces], refs[2 * pieces : 3 * pieces]
+    samples, spec, total, result = refs[3 * pieces :]
     me = lax.axis_index("seq")
-    blocks, channels = total.shape[0], total.shape[1]
-    per = own_in.shape[1] // BLOCK
+    side = lax.rem(me, 2)
+    blocks, channels = samples.shape[0] - 1, samples.shape[1]
+    per = ins[0].shape[1] // BLOCK
     samples[0] = jnp.zeros((channels, BLOCK), BF16)
-
-    def place(values, flips):
+    for flips, piece in enumerate(ins):
         at = lax.bitwise_xor(me, flips) * per
         for part in range(per):
-            samples[at + (1 + part)] = values[:, part * BLOCK : (part + 1) * BLOCK]
-
-    place(own_in[...], 0)
-    place(beside_in[0], 1)
-    for k in range(1, pieces):
-        for side in range(2):
-            place(ins[k - 1][side], 2 * k + side)
+            samples[at + (1 + part)] = piece[:, part * BLOCK : (part + 1) * BLOCK]
     before = samples[0:blocks].reshape(blocks * channels, BLOCK)
     current = samples[1 : blocks + 1].reshape(blocks * channels, BLOCK)
     window = jnp.concatenate([before, current], 1)
-    spec[...] = (dot(window, table_high[...]) + dot(window, table_low[...])).reshape(spec.shape)
+    spec[0:per] = jnp.zeros((per,) + spec.shape[1:], F32)
+    spec[per:] = (dot(window, table_high[...]) + dot(window, table_low[...])).reshape((blocks,) + spec.shape[1:])
     taps = filt.shape[0]
-
     packed = lax.broadcasted_iota(jnp.int32, (8, BLOCK), 1) == 0
 
     def group(g, carry):
         at = pl.ds(pl.multiple_of(g * 8, 8), 8)
-        for k in range(blocks):
-            both_real = both_imag = cross = None
-            for j in range(min(k + 1, taps)):
-                x_real, x_imag = spec[k - j, at, :BLOCK], spec[k - j, at, BLOCK:]
-                f_real, f_imag = filt[j, at, :BLOCK], filt[j, at, BLOCK:]
-                terms = (x_real * f_real, x_imag * f_imag, x_real * f_imag + x_imag * f_real)
-                if j == 0:
-                    both_real, both_imag, cross = terms
-                else:
-                    both_real, both_imag, cross = both_real + terms[0], both_imag + terms[1], cross + terms[2]
-            total[k, at, :BLOCK] = both_real - jnp.where(packed, 0.0, both_imag)
-            total[k, at, BLOCK:] = jnp.where(packed, both_imag, cross)
+
+        def load(ref, index):
+            real, imag = ref[index, at, :BLOCK], ref[index, at, BLOCK:]
+            return real, imag, real + imag
+
+        for place in range(pieces):
+            first = 2 * per * place + per
+            count = min(first + per, taps)
+            sums = [None] * per
+            held = [load(spec, side * per + (first + q)) for q in range(per)]
+            for j in range(count):
+                taken = load(filt, j)
+                for q in range(per):
+                    if j <= first + q:
+                        terms = tuple(x * f for x, f in zip(held[q], taken))
+                        sums[q] = terms if sums[q] is None else tuple(s + t for s, t in zip(sums[q], terms))
+                if j + 1 < count:
+                    below = [load(spec, side * per + (first - j - 1))] if j < first else [None]
+                    held = below + held[:-1]
+            for q, (real, imag, both) in enumerate(sums):
+                total[per * place + q, at, :BLOCK] = real - jnp.where(packed, 0.0, imag)
+                total[per * place + q, at, BLOCK:] = jnp.where(packed, imag, both - real - imag)
         return carry
 
     lax.fori_loop(0, channels // 8, group, 0)
-    sums = total[...].reshape(blocks * channels, 2 * BLOCK)
+    sums = total[...].reshape(-1, 2 * BLOCK)
     high = sums.astype(BF16)
     low = (sums - high.astype(F32)).astype(BF16)
     conv = dot(high, back_high[...]) + dot(low, back_high[...]) + dot(high, back_low[...])
     result[...] = conv.astype(BF16).reshape(result.shape)
-
-    def taken(flips):
-        at = lax.bitwise_xor(me, flips) * per
-        return jnp.concatenate([result[at + part] for part in range(per)], 1)
-
-    outs[0][...] = taken(0)
-    outs[1][...] = taken(1)
-    for k in range(1, pieces):
-        for side in range(2):
-            outs[k + 1][side] = taken(2 * k + side)
-
-
-def mix_kernel(pieces, signal, gate, skip, own_in, *refs):
-    ins, beside = refs[: pieces - 1], refs[pieces - 1 : pieces - 1 + pieces // 2]
-    keep_out, send_out, conv = refs[-3:]
-    me = lax.axis_index("seq")
+    for k, out in enumerate(outs):
+        at = lax.bitwise_xor(me // 2, k) * per
+        out[...] = jnp.concatenate([result[at + part] for part in range(per)], 1)
+
+
+def mix_kernel(pieces, signal, gate, skip, *refs):
+    ins, (keep_out, send_out, conv) = refs[:pieces], refs[pieces:]
+    place = lax.axis_index("seq") // 2
     core = lax.rem(lax.axis_index("head"), 2)
-    conv[me] = own_in[...]
-    for k in range(1, pieces):
-        conv[lax.bitwise_xor(me, 2 * k)] = ins[k - 1][0]
     for k in range(pieces):
-        conv[lax.bitwise_xor(me, 2 * k + 1)] = beside[k // 2][k % 2]
+        conv[lax.bitwise_xor(place, k)] = ins[k][...]
     turned = conv[...].reshape(-1, conv.shape[-1]).T.astype(F32)
     mixed = (gate[...].astype(F32) * (turned + skip[...] * signal[...].astype(F32))).astype(BF16)
     half = keep_out.shape[0]
@@ -228,35 +215,33 @@
     out[pl.ds(pl.multiple_of((1 - core) * half, half), half), :] = there.astype(BF16)
 
 
-def turn_kernel(pieces, signal, *refs):
-    own, beside = refs[:pieces], refs[pieces : pieces + pieces // 2]
-    held, turned, sems = refs[pieces + pieces // 2 :]
-    me = lax.axis_index("seq")
-    share = own[0].shape[0]
-    parts = held.shape[0]
-    wide = held.shape[2]
-    sources = [signal.at[:, n * wide : (n + 1) * wide] for n in range(parts)]
-    copies = fetch(sources, [held.at[n] for n in range(parts)], sems)
-    for n, copy in enumerate(copies):
-        copy.wait()
-        turned[n * (wide // share) : (n + 1) * (wide // share)] = held[n].T.reshape(-1, share, held.shape[1])
-    for k in range(pieces):
-        own[k][...] = turned[lax.bitwise_xor(me, 2 * k)]
-        beside[k // 2][k % 2] = turned[lax.bitwise_xor(me, 2 * k + 1)]
-
-
-def call(kernel, outs, *args, scratch=(), flops=0, grant=12, space=VMEM):
+def turn_kernel(pieces, signal, *outs):
+    outs, (held, sems) = outs[:pieces], outs[pieces:]
+    place = lax.axis_index("seq") // 2
+    share = outs[0].shape[0]
+    order = [*range(1, pieces), 0]
+    starts = [pl.multiple_of(lax.bitwise_xor(place, k) * share, share) for k in order]
+    copies = fetch([signal.at[:, pl.ds(at, share)] for at in starts], [held.at[n] for n in range(pieces)], sems)
+    for n, k in enumerate(order):
+        copies[n].wait()
+        outs[k][...] = held[n].T
+
+
+def call(kernel, outs, *args, scratch=(), flops=0, grant=12, hbm=()):
+    spaces = [pltpu.HBM if n in hbm else VMEM for n in range(len(args))]
     run = pl.pallas_call(
         kernel,
         out_shape=outs,
-        in_specs=[pl.BlockSpec(memory_space=space)] * len(args),
+        in_specs=[pl.BlockSpec(memory_space=space) for space in spaces],
         out_specs=jax.tree.map(lambda _: pl.BlockSpec(memory_space=VMEM), outs),
         scratch_shapes=list(scratch),
         cost_estimate=pl.CostEstimate(flops=flops, bytes_accessed=0, transcendentals=0),
         compiler_params=pltpu.CompilerParams(vmem_limit_bytes=grant << 20),
     )
-    if space is not VMEM:
-        args = [pltpu.with_memory_space_constraint(arg, space) for arg in args]
+    args = [
+        pltpu.with_memory_space_constraint(arg, pltpu.HBM) if n in hbm else arg
+        for n, arg in enumerate(args)
+    ]
     return run(*args)
 
 
@@ -273,80 +258,71 @@
     length_local, channels = signal.shape
     ranks, heads = lax.axis_size("seq"), lax.axis_size("head")
     pieces = ranks // 2
-    share = channels // ranks
-    blocks = ranks * length_local // BLOCK
+    share = channels // pieces
+    per = length_local // BLOCK
+    blocks = ranks * per
     taps = K // BLOCK
     half = length_local // 2
     width = out_w.shape[1] // heads
     row = lambda v: v.reshape(1, -1)
 
-    piece, pair = shape((share, length_local)), shape((2, share, length_local))
-    *own, near, far = call(
+    piece = shape((share, length_local))
+    own = call(
         functools.partial(turn_kernel, pieces),
-        (piece,) * pieces + (pair,) * 2,
+        (piece,) * pieces,
         signal,
-        scratch=[
-            pltpu.VMEM((channels // 128, length_local, 128), BF16),
-            pltpu.VMEM((ranks, share, length_local), BF16),
-            pltpu.SemaphoreType.DMA((channels // 128,)),
-        ],
-        space=pltpu.HBM,
-    )
-    far = flip(far, "seq", 1)
-    near = flip(near, "seq", 1)
-    beside = [near[0], near[1], far[0], far[1]]
-    parts = {k: flip(jnp.stack([own[k], beside[k]]), "seq", 2 * k) for k in (2, 3, 1)}
+        scratch=[pltpu.VMEM((pieces, length_local, share), BF16), pltpu.SemaphoreType.DMA((pieces,))],
+        hbm=(0,),
+    )
+    parts = []
+    for k in range(pieces):
+        part = flip(own[k], "seq", 2 * k) if k else own[0]
+        parts += [part, flip(part, "seq", 1)]
 
     forward_high, forward_low = split(forward_table())
     back_high, back_low = split(backward_table())
     filter_table = np.concatenate([forward_high[:BLOCK], forward_low[:BLOCK]], 0)
-    operands = (
-        jnp.asarray(feature_table()),
-        w_first,
-        row(b_first),
-        row(freq),
-        w_mid,
-        w_last,
-        row(rate),
-        jnp.asarray(filter_table),
-    )
+    operands = (jnp.asarray(feature_table()), w_first, row(b_first), row(freq), w_mid)
+    hidden = call(
+        functools.partial(hidden_kernel, len(operands)),
+        shape((w_mid.shape[1], K), F32),
+        *operands,
+        scratch=[pltpu.VMEM(v.shape, v.dtype) for v in operands]
+        + [pltpu.SemaphoreType.DMA((len(operands),))],
+        flops=1_000_000_000,
+        hbm=range(len(operands)),
+    )
+    operands = (w_last, row(rate), jnp.asarray(filter_table))
     filt = call(
         functools.partial(filter_kernel, len(operands)),
         shape((taps, share, 2 * BLOCK), F32),
+        hidden,
         *operands,
         scratch=[pltpu.VMEM(v.shape, v.dtype) for v in operands]
-        + [
-            pltpu.VMEM((128, w_last.shape[0]), F32),
-            pltpu.VMEM((128, BLOCK), F32),
-            pltpu.SemaphoreType.DMA((len(operands),)),
-        ],
-        flops=5_000_000_000,
-        space=pltpu.HBM,
+        + [pltpu.SemaphoreType.DMA((len(operands),))],
+        flops=2_000_000_000,
+        hbm=range(1, 1 + len(operands)),
     )
     other_w = flip(out_w, "head", 1)
-    conv_own, conv_beside, *convs = call(
+    convs = call(
         functools.partial(conv_kernel, pieces),
-        (piece,) * 2 + (pair,) * (pieces - 1),
+        (piece,) * pieces,
         filt,
         forward_high,
         forward_low,
         back_high,
         back_low,
-        own[0],
-        near,
-        *[parts[k] for k in range(1, pieces)],
+        *parts,
         scratch=[
             pltpu.VMEM((blocks + 1, share, BLOCK), BF16),
-            pltpu.VMEM((blocks, share, 2 * BLOCK), F32),
-            pltpu.VMEM((blocks, share, 2 * BLOCK), F32),
-            pltpu.VMEM((blocks, share, BLOCK), BF16),
+            pltpu.VMEM((per + blocks, share, 2 * BLOCK), F32),
+            pltpu.VMEM((blocks // 2, share, 2 * BLOCK), F32),
+            pltpu.VMEM((blocks // 2, share, BLOCK), BF16),
         ],
         flops=3_000_000_000,
     )
 
-    got = {k: flip(convs[k - 1], "seq", 2 * k) for k in (2, 3, 1)}
-    near = flip(jnp.stack([conv_beside, got[1][1]]), "seq", 1)
-    far = flip(jnp.stack([got[2][1], got[3][1]]), "seq", 1)
+    convs = [flip(conv, "seq", 2 * k) if k else conv for k, conv in enumerate(convs)]
     mixed = shape((half, channels))
     keep, send = call(
         functools.partial(mix_kernel, pieces),
@@ -354,27 +330,17 @@
         signal,
         gate,
         row(skip),
-        conv_own,
-        got[1],
-        got[2],
-        got[3],
-        near,
-        far,
-        scratch=[pltpu.VMEM((ranks, share, length_local), BF16)],
+        *convs,
+        scratch=[pltpu.VMEM((pieces, share, length_local), BF16)],
         flops=500_000_000,
     )
     received = flip(send, "head", 1)
     terms, wide = shape((half, width)), shape((half, width), F32)
-    a, b, c, here = call(
-        functools.partial(project_kernel, (2, 3, 1, 0)),
-        (terms, terms, wide, wide),
-        keep,
-        received,
-        out_w,
-        other_w,
-        flops=500_000_000,
-    )
-    a, b, c = flip(a, "head", 2), flip(b, "head", 3), flip(c, "head", 1)
+    factors = (keep, received, out_w, other_w)
+    a, b = call(functools.partial(project_kernel, (2, 3)), (terms, terms), *factors, flops=500_000_000)
+    a, b = flip(a, "head", 2), flip(b, "head", 3)
+    c, here = call(functools.partial(project_kernel, (1, 0)), (wide, wide), *factors, flops=500_000_000)
+    c = flip(c, "head", 1)
     return call(sum_kernel, shape((length_local, width)), here, a, b, c)
 
 
@@ -465,9 +431,8 @@
 def local(signal, *rest):
     ranks, heads = lax.axis_size("seq"), lax.axis_size("head")
     length_local, channels = signal.shape
-    share = channels // ranks
     small = ranks == 8 and ranks * length_local <= K and heads == 4 and length_local == 2 * BLOCK
-    if small and channels % ranks == 0 and share % 16 == 0 and 128 % share == 0:
+    if small and channels == 128 * (ranks // 2):
         return spread(signal, *rest)
     return halo(signal, *rest)
 
@@ -485,6 +450,8 @@
         P("head"),
         P("head", None),
     )
+
+
     return jax.shard_map(
         local, mesh=mesh, in_specs=placed, out_specs=P("seq", "head"), check_vma=False
     )

time: 45.4 us -> 43.3 us (0.954)
  waiting for transfers between devices: 17.4 us -> 14.2 us
  Pallas kernels: 9.09 us -> 11.6 us
  starting transfers between devices: 18.5 us -> 17.1 us
    ppermute x15, waiting for transfers between devices: 17.4 us -> 14.2 us  [flip(): return lax.ppermute(x, axis, [(i, i ^ by) for i in range(size)])]
    pallas_call x6 -> x8, Pallas kernels: 9.09 us -> 11.6 us  [call(): return run(*args)]
    ppermute x15, starting transfers between devices: 18.5 us -> 17.1 us  [flip(): return lax.ppermute(x, axis, [(i, i ^ by) for i in range(size)])]
  transfers between devices with their start and end apart: 15 -> 15, of which waited for: 8 -> 7; matrix products, arithmetic and copies ran while one was open for 0% -> 0% of each run, Pallas kernels for 17% -> 24%
where the time goes in v3:
time: 43.3 us; the launch traced here: 43.1 us
  starting transfers between devices  17.1 us (39%)
  waiting for transfers between devices  14.2 us (33%)
  Pallas kernels  11.6 us (27%)
    ppermute x15, starting transfers between devices, flip(): return lax.ppermute(x, axis, [(i, i ^ by) for i in range(size)])  17.1 us
    ppermute x15, waiting for transfers between devices, flip(): return lax.ppermute(x, axis, [(i, i ^ by) for i in range(size)])  14.2 us
    pallas_call x8, Pallas kernels, call(): return run(*args)  11.6 us
  transfers between devices with their start and end apart: 15, of which 7 were waited for; matrix products, arithmetic and copies ran while one was open for 0% of the time, Pallas kernels for 24%

profile of v3, /device:TPU:0, one launch (start us, length us, event | category | flops | bytes accessed | tf_op | source)
XLA Modules:
  0.0 43.1 jit_solution(14134729133727965827)
XLA Ops:
  0.0 0.5 %collective-permute-start.11 = (bf16[512,2048]{1,0:T(8,128)(2,1)}, bf16[512,2048]{1,0:T(8,128)(2,1)S(1)}, u32[]{:S(2)}, u32[]{:S(2)}) collective-permute-start(bf16[512,2048]{1,0:T(8,128)(2,1)} %own_w.3), channel_id=1, source_target_pairs={{0,1},{1,0},{2,3},{3,2},{4,5},{5,4},{6,7},{7,6},{8,9},{9,8},{10,11... | collective-permute-start | bytes 6291464 | tf_op jit(solution)/shard_map/ppermute | solution.py:254
  0.5 1.2 %shard_map.156 = (bf16[128,256]{1,0:T(8,128)(2,1)S(1)}, bf16[128,256]{1,0:T(8,128)(2,1)S(1)}, bf16[128,256]{1,0:T(8,128)(2,1)S(1)}, bf16[128,256]{1,0:T(8,128)(2,1)S(1)}) custom-call(bf16[256,512]{1,0:T(8,128)(2,1)} %signal.3), custom_call_target="tpu_custom_call" | custom-call | tf_op jit(solution)/shard_map/pallas_call | solution.py:245
  1.7 2.6 %collective-permute-start.1 = (bf16[128,256]{1,0:T(8,128)(2,1)S(1)}, bf16[128,256]{1,0:T(8,128)(2,1)S(1)}, u32[]{:S(2)}, u32[]{:S(2)}) collective-permute-start(bf16[128,256]{1,0:T(8,128)(2,1)S(1)} %get-tuple-element.20), channel_id=1, source_target_pairs={{0,8},{4,12},{8,0},{12,4},{16,24},{20,28},{24,16},{28,20},{1,9},{5... | collective-permute-start | bytes 196616 | tf_op jit(solution)/shard_map/ppermute | solution.py:254
  4.3 2.6 %collective-permute-start.3 = (bf16[128,256]{1,0:T(8,128)(2,1)S(1)}, bf16[128,256]{1,0:T(8,128)(2,1)S(1)}, u32[]{:S(2)}, u32[]{:S(2)}) collective-permute-start(bf16[128,256]{1,0:T(8,128)(2,1)S(1)} %get-tuple-element.21), channel_id=1, source_target_pairs={{0,16},{4,20},{8,24},{12,28},{16,0},{20,4},{24,8},{28,12},{1,17},{... | collective-permute-start | bytes 196616 | tf_op jit(solution)/shard_map/ppermute | solution.py:254
  6.9 0.0 collective-permute-start.5
  6.9 1.7 %collective-permute-start = (bf16[128,256]{1,0:T(8,128)(2,1)S(1)}, bf16[128,256]{1,0:T(8,128)(2,1)S(1)}, u32[]{:S(2)}, u32[]{:S(2)}) collective-permute-start(bf16[128,256]{1,0:T(8,128)(2,1)S(1)} %get-tuple-element.19.refs_0_), channel_id=1, source_target_pairs={{0,4},{4,0},{8,12},{12,8},{16,20},{20,16},{24,28},{28,24},{1,5},{5... | collective-permute-start | bytes 196616 | tf_op jit(solution)/shard_map/ppermute | solution.py:254
  8.6 2.6 %shard_map.154.hidden = f32[64,2048]{1,0:T(8,128)S(1)} custom-call(f32[33,2048]{1,0:T(8,128)} %constant.12.clone.refs_0_, f32[33,64]{1,0:T(8,128)} %refs_1_.1, f32[1,64]{1,0:T(1,128)} %bitcast.6, f32[1,64]{1,0:T(1,128)} %bitcast.7, f32[64,64]{1,0:T(8,128)} %refs_4_.1), custom_call_target="tpu_custom_call" | custom-call | flops 1000000000 | tf_op jit(solution)/shard_map/pallas_call | solution.py:245
  11.3 0.0 collective-permute-done.1.refs_2_
  11.3 0.4 collective-permute-start.2
  11.6 0.0 collective-permute-done.3.refs_4_
  11.6 1.7 %collective-permute-start.4 = (bf16[128,256]{1,0:T(8,128)(2,1)S(1)}, bf16[128,256]{1,0:T(8,128)(2,1)S(1)}, u32[]{:S(2)}, u32[]{:S(2)}) collective-permute-start(bf16[128,256]{1,0:T(8,128)(2,1)S(1)} %collective-permute-done.3.refs_4_), channel_id=1, source_target_pairs={{0,4},{4,0},{8,12},{12,8},{16,20},{20,16},{24,28},{28,24},{1,5},{5... | collective-permute-start | bytes 196616 | tf_op jit(solution)/shard_map/ppermute | solution.py:254
  13.4 0.0 collective-permute-done.5.refs_6_
  13.4 1.1 %collective-permute-start.6 = (bf16[128,256]{1,0:T(8,128)(2,1)S(1)}, bf16[128,256]{1,0:T(8,128)(2,1)S(1)}, u32[]{:S(2)}, u32[]{:S(2)}) collective-permute-start(bf16[128,256]{1,0:T(8,128)(2,1)S(1)} %collective-permute-done.5.refs_6_), channel_id=1, source_target_pairs={{0,4},{4,0},{8,12},{12,8},{16,20},{20,16},{24,28},{28,24},{1,5},{5... | collective-permute-start | bytes 196616 | tf_op jit(solution)/shard_map/ppermute | solution.py:254
  14.5 2.4 %shard_map.155.filt = f32[16,128,256]{2,1,0:T(8,128)S(1)} custom-call(f32[64,2048]{1,0:T(8,128)S(1)} %shard_map.154.hidden, f32[64,512]{1,0:T(8,128)} %refs_0_.2, f32[1,512]{1,0:T(1,128)} %bitcast.5, bf16[256,256]{1,0:T(8,128)(2,1)} %constant.13.clone.refs_2_), custom_call_target="tpu_custom_call" | custom-call | flops 2000000000 | tf_op jit(solution)/shard_map/pallas_call | solution.py:245
  16.9 0.0 copy-start.1
  16.9 0.0 copy-start.2
  16.9 0.0 copy-start.3
  16.9 0.0 collective-permute-done.refs_1_
  16.9 0.0 collective-permute-done.2.refs_3_
  16.9 0.0 collective-permute-done.4.refs_5_
  17.0 0.7 %collective-permute-done.6.refs_7_ = bf16[128,256]{1,0:T(8,128)(2,1)S(1)} collective-permute-done((bf16[128,256]{1,0:T(8,128)(2,1)S(1)}, bf16[128,256]{1,0:T(8,128)(2,1)S(1)}, u32[]{:S(2)}, u32[]{:S(2)}) %collective-permute-start.6) | collective-permute-done | bytes 65568 | tf_op jit(solution)/shard_map/ppermute | solution.py:254
  17.7 0.0 copy-done.4
  17.7 0.0 copy-done.5
  17.7 0.0 copy-done.6
  17.7 0.0 copy-done.7
  17.7 0.0 copy-start
  17.7 3.5 %shard_map.157 = (bf16[128,256]{1,0:T(8,128)(2,1)S(1)}, bf16[128,256]{1,0:T(8,128)(2,1)S(1)}, bf16[128,256]{1,0:T(8,128)(2,1)S(1)}, bf16[128,256]{1,0:T(8,128)(2,1)S(1)}) custom-call(f32[16,128,256]{2,1,0:T(8,128)S(1)} %shard_map.155.filt, bf16[256,256]{1,0:T(8,128)(2,1)S(1)} %copy-done.4, bf16[256,256]{1,0:T(8,128)(2,1)S(1)} %copy-done.5, ...), custom_call_target="tpu_custom_call" | custom-call | flops 3000000000 | tf_op jit(solution)/shard_map/pallas_call | solution.py:245
  21.2 0.9 %collective-permute-start.7 = (bf16[128,256]{1,0:T(8,128)(2,1)S(1)}, bf16[128,256]{1,0:T(8,128)(2,1)S(1)}, u32[]{:S(2)}, u32[]{:S(2)}) collective-permute-start(bf16[128,256]{1,0:T(8,128)(2,1)S(1)} %get-tuple-element.24), channel_id=1, source_target_pairs={{0,8},{4,12},{8,0},{12,4},{16,24},{20,28},{24,16},{28,20},{1,9},{5... | collective-permute-start | bytes 196616 | tf_op jit(solution)/shard_map/ppermute | solution.py:254
  22.1 3.3 %collective-permute-start.8 = (bf16[128,256]{1,0:T(8,128)(2,1)S(1)}, bf16[128,256]{1,0:T(8,128)(2,1)S(1)}, u32[]{:S(2)}, u32[]{:S(2)}) collective-permute-start(bf16[128,256]{1,0:T(8,128)(2,1)S(1)} %get-tuple-element.25), channel_id=1, source_target_pairs={{0,16},{4,20},{8,24},{12,28},{16,0},{20,4},{24,8},{28,12},{1,17},{... | collective-permute-start | bytes 196616 | tf_op jit(solution)/shard_map/ppermute | solution.py:254
  25.4 0.3 collective-permute-start.9
  25.7 0.1 collective-permute-done.7.refs_1_
  25.8 3.3 %collective-permute-done.8.refs_2_ = bf16[128,256]{1,0:T(8,128)(2,1)S(1)} collective-permute-done((bf16[128,256]{1,0:T(8,128)(2,1)S(1)}, bf16[128,256]{1,0:T(8,128)(2,1)S(1)}, u32[]{:S(2)}, u32[]{:S(2)}) %collective-permute-start.8) | collective-permute-done | bytes 65568 | tf_op jit(solution)/shard_map/ppermute | solution.py:254
  29.1 2.4 %collective-permute-done.9.refs_3_ = bf16[128,256]{1,0:T(8,128)(2,1)S(1)} collective-permute-done((bf16[128,256]{1,0:T(8,128)(2,1)S(1)}, bf16[128,256]{1,0:T(8,128)(2,1)S(1)}, u32[]{:S(2)}, u32[]{:S(2)}) %collective-permute-start.9) | collective-permute-done | bytes 65568 | tf_op jit(solution)/shard_map/ppermute | solution.py:254
  31.5 0.0 copy-done.1
  31.5 0.0 copy-done.2
  31.5 0.2 shard_map.158
  31.7 0.1 collective-permute-start.10
  31.8 1.3 %collective-permute-done.10.other = bf16[128,512]{1,0:T(8,128)(2,1)S(1)} collective-permute-done((bf16[128,512]{1,0:T(8,128)(2,1)S(1)}, bf16[128,512]{1,0:T(8,128)(2,1)S(1)}, u32[]{:S(2)}, u32[]{:S(2)}) %collective-permute-start.10) | collective-permute-done | bytes 131104 | tf_op jit(solution)/shard_map/ppermute | solution.py:254
  33.1 0.0 collective-permute-done.11.other_w
  33.1 0.5 %shard_map.159 = (f32[128,512]{1,0:T(8,128)S(1)}, f32[128,512]{1,0:T(8,128)S(1)}) custom-call(bf16[128,512]{1,0:T(8,128)(2,1)S(1)} %get-tuple-element.27.own, bf16[128,512]{1,0:T(8,128)(2,1)S(1)} %collective-permute-done.10.other, bf16[512,2048]{1,0:T(8,128)(2,1)S(1)} %copy-done, bf16[512,2048]{1,0:T(8,128)(2,1)S(1)} %collective-permute-done.11.other_w), custom_call_target="tpu_custom_call" | custom-call | flops 500000000 | tf_op jit(solution)/shard_map/pallas_call | solution.py:245
  33.6 0.2 collective-permute-start.14
  33.8 0.5 %shard_map.160 = (bf16[128,512]{1,0:T(8,128)(2,1)S(1)}, bf16[128,512]{1,0:T(8,128)(2,1)S(1)}) custom-call(bf16[128,512]{1,0:T(8,128)(2,1)S(1)} %get-tuple-element.27.own, bf16[128,512]{1,0:T(8,128)(2,1)S(1)} %collective-permute-done.10.other, bf16[512,2048]{1,0:T(8,128)(2,1)S(1)} %copy-done, bf16[512,2048]{1,0:T(8,128)(2,1)S(1)} %collective-permute-done.11.other_w), custom_call_target="tpu_custom_call" | custom-call | flops 500000000 | tf_op jit(solution)/shard_map/pallas_call | solution.py:245
  34.3 1.6 %collective-permute-start.12 = (bf16[128,512]{1,0:T(8,128)(2,1)S(1)}, bf16[128,512]{1,0:T(8,128)(2,1)S(1)}, u32[]{:S(2)}, u32[]{:S(2)}) collective-permute-start(bf16[128,512]{1,0:T(8,128)(2,1)S(1)} %get-tuple-element.30), channel_id=1, source_target_pairs={{0,2},{1,3},{2,0},{3,1},{4,6},{5,7},{6,4},{7,5},{8,10},{9,11},{10,... | collective-permute-start | bytes 393224 | tf_op jit(solution)/shard_map/ppermute | solution.py:254
  35.9 0.2 collective-permute-start.13
  36.1 4.7 %collective-permute-done.12.a = bf16[128,512]{1,0:T(8,128)(2,1)S(1)} collective-permute-done((bf16[128,512]{1,0:T(8,128)(2,1)S(1)}, bf16[128,512]{1,0:T(8,128)(2,1)S(1)}, u32[]{:S(2)}, u32[]{:S(2)}) %collective-permute-start.12) | collective-permute-done | bytes 131104 | tf_op jit(solution)/shard_map/ppermute | solution.py:254
  40.7 1.6 %collective-permute-done.13.b = bf16[128,512]{1,0:T(8,128)(2,1)S(1)} collective-permute-done((bf16[128,512]{1,0:T(8,128)(2,1)S(1)}, bf16[128,512]{1,0:T(8,128)(2,1)S(1)}, u32[]{:S(2)}, u32[]{:S(2)}) %collective-permute-start.13) | collective-permute-done | bytes 131104 | tf_op jit(solution)/shard_map/ppermute | solution.py:254
  42.3 0.0 collective-permute-done.14.c
  42.3 0.8 %shard_map.161 = bf16[256,512]{1,0:T(8,128)(2,1)} custom-call(f32[128,512]{1,0:T(8,128)S(1)} %get-tuple-element.29.own, bf16[128,512]{1,0:T(8,128)(2,1)S(1)} %collective-permute-done.12.a, bf16[128,512]{1,0:T(8,128)(2,1)S(1)} %collective-permute-done.13.b, f32[128,512]{1,0:T(8,128)S(1)} %collective-permute-done.14.c), custom_call_target="tpu_custom_call" | custom-call | tf_op jit(solution)/shard_map/pallas_call | solution.py:245
  (6 shorter events, 0.0 us)
Async XLA Ops:
  0.0 33.1 %collective-permute-start.11 = (bf16[512,2048]{1,0:T(8,128)(2,1)}, bf16[512,2048]{1,0:T(8,128)(2,1)S(1)}, u32[]{:S(2)}, u32[]{:S(2)}) collective-permute-start(bf16[512,2048]{1,0:T(8,128)(2,1)} %own_w.3), channel_id=1, source_target_pairs={{0,1},{1,0},{2,3},{3,2},{4,5},{5,4},{6,7},{7,6},{8,9},{9,8},{10,11... | collective-permute-start | bytes 6291464 | tf_op jit(solution)/shard_map/ppermute | solution.py:254
  1.7 9.6 %collective-permute-start.1 = (bf16[128,256]{1,0:T(8,128)(2,1)S(1)}, bf16[128,256]{1,0:T(8,128)(2,1)S(1)}, u32[]{:S(2)}, u32[]{:S(2)}) collective-permute-start(bf16[128,256]{1,0:T(8,128)(2,1)S(1)} %get-tuple-element.20), channel_id=1, source_target_pairs={{0,8},{4,12},{8,0},{12,4},{16,24},{20,28},{24,16},{28,20},{1,9},{5... | collective-permute-start | bytes 196616 | tf_op jit(solution)/shard_map/ppermute | solution.py:254
  4.3 7.3 %collective-permute-start.3 = (bf16[128,256]{1,0:T(8,128)(2,1)S(1)}, bf16[128,256]{1,0:T(8,128)(2,1)S(1)}, u32[]{:S(2)}, u32[]{:S(2)}) collective-permute-start(bf16[128,256]{1,0:T(8,128)(2,1)S(1)} %get-tuple-element.21), channel_id=1, source_target_pairs={{0,16},{4,20},{8,24},{12,28},{16,0},{20,4},{24,8},{28,12},{1,17},{... | collective-permute-start | bytes 196616 | tf_op jit(solution)/shard_map/ppermute | solution.py:254
  6.9 6.5 %collective-permute-start.5 = (bf16[128,256]{1,0:T(8,128)(2,1)S(1)}, bf16[128,256]{1,0:T(8,128)(2,1)S(1)}, u32[]{:S(2)}, u32[]{:S(2)}) collective-permute-start(bf16[128,256]{1,0:T(8,128)(2,1)S(1)} %get-tuple-element.22), channel_id=1, source_target_pairs={{0,24},{4,28},{8,16},{12,20},{16,8},{20,12},{24,0},{28,4},{1,25},{... | collective-permute-start | bytes 196616 | tf_op jit(solution)/shard_map/ppermute | solution.py:254
  6.9 10.0 %collective-permute-start = (bf16[128,256]{1,0:T(8,128)(2,1)S(1)}, bf16[128,256]{1,0:T(8,128)(2,1)S(1)}, u32[]{:S(2)}, u32[]{:S(2)}) collective-permute-start(bf16[128,256]{1,0:T(8,128)(2,1)S(1)} %get-tuple-element.19.refs_0_), channel_id=1, source_target_pairs={{0,4},{4,0},{8,12},{12,8},{16,20},{20,16},{24,28},{28,24},{1,5},{5... | collective-permute-start | bytes 196616 | tf_op jit(solution)/shard_map/ppermute | solution.py:254
  11.3 5.6 %collective-permute-start.2 = (bf16[128,256]{1,0:T(8,128)(2,1)S(1)}, bf16[128,256]{1,0:T(8,128)(2,1)S(1)}, u32[]{:S(2)}, u32[]{:S(2)}) collective-permute-start(bf16[128,256]{1,0:T(8,128)(2,1)S(1)} %collective-permute-done.1.refs_2_), channel_id=1, source_target_pairs={{0,4},{4,0},{8,12},{12,8},{16,20},{20,16},{24,28},{28,24},{1,5},{5... | collective-permute-start | bytes 196616 | tf_op jit(solution)/shard_map/ppermute | solution.py:254
  11.6 5.3 %collective-permute-start.4 = (bf16[128,256]{1,0:T(8,128)(2,1)S(1)}, bf16[128,256]{1,0:T(8,128)(2,1)S(1)}, u32[]{:S(2)}, u32[]{:S(2)}) collective-permute-start(bf16[128,256]{1,0:T(8,128)(2,1)S(1)} %collective-permute-done.3.refs_4_), channel_id=1, source_target_pairs={{0,4},{4,0},{8,12},{12,8},{16,20},{20,16},{24,28},{28,24},{1,5},{5... | collective-permute-start | bytes 196616 | tf_op jit(solution)/shard_map/ppermute | solution.py:254
  13.4 4.3 %collective-permute-start.6 = (bf16[128,256]{1,0:T(8,128)(2,1)S(1)}, bf16[128,256]{1,0:T(8,128)(2,1)S(1)}, u32[]{:S(2)}, u32[]{:S(2)}) collective-permute-start(bf16[128,256]{1,0:T(8,128)(2,1)S(1)} %collective-permute-done.5.refs_6_), channel_id=1, source_target_pairs={{0,4},{4,0},{8,12},{12,8},{16,20},{20,16},{24,28},{28,24},{1,5},{5... | collective-permute-start | bytes 196616 | tf_op jit(solution)/shard_map/ppermute | solution.py:254
  14.5 3.2 %copy-start.4 = (bf16[256,256]{1,0:T(8,128)(2,1)S(1)}, bf16[256,256]{1,0:T(8,128)(2,1)}, u32[]{:S(2)}) copy-start(bf16[256,256]{1,0:T(8,128)(2,1)} %constant.14.clone.table_high) | copy-start | bytes 393220
  14.5 3.2 %copy-start.5 = (bf16[256,256]{1,0:T(8,128)(2,1)S(1)}, bf16[256,256]{1,0:T(8,128)(2,1)}, u32[]{:S(2)}) copy-start(bf16[256,256]{1,0:T(8,128)(2,1)} %constant.15.clone.table_low) | copy-start | bytes 393220
  14.5 3.2 %copy-start.6 = (bf16[256,128]{1,0:T(8,128)(2,1)S(1)}, bf16[256,128]{1,0:T(8,128)(2,1)}, u32[]{:S(2)}) copy-start(bf16[256,128]{1,0:T(8,128)(2,1)} %constant.16.clone.back_high) | copy-start | bytes 196612
  14.5 3.2 %copy-start.7 = (bf16[256,128]{1,0:T(8,128)(2,1)S(1)}, bf16[256,128]{1,0:T(8,128)(2,1)}, u32[]{:S(2)}) copy-start(bf16[256,128]{1,0:T(8,128)(2,1)} %constant.17.clone.back_low) | copy-start | bytes 196612
  16.9 14.6 %copy-start.1 = (bf16[256,512]{1,0:T(8,128)(2,1)S(1)}, bf16[256,512]{1,0:T(8,128)(2,1)}, u32[]{:S(2)}) copy-start(bf16[256,512]{1,0:T(8,128)(2,1)} %signal.3) | copy-start | bytes 786436
  16.9 14.6 %copy-start.2 = (bf16[256,512]{1,0:T(8,128)(2,1)S(1)}, bf16[256,512]{1,0:T(8,128)(2,1)}, u32[]{:S(2)}) copy-start(bf16[256,512]{1,0:T(8,128)(2,1)} %gate.1) | copy-start | bytes 786436
  16.9 14.6 %copy-start.3 = (f32[512]{0:T(512)S(1)}, f32[512]{0:T(512)}, u32[]{:S(2)}) copy-start(f32[512]{0:T(512)} %param.18) | copy-start | bytes 6148
  17.7 15.4 %copy-start = (bf16[512,2048]{1,0:T(8,128)(2,1)S(1)}, bf16[512,2048]{1,0:T(8,128)(2,1)}, u32[]{:S(2)}) copy-start(bf16[512,2048]{1,0:T(8,128)(2,1)} %own_w.3) | copy-start | bytes 6291460
  21.2 4.6 %collective-permute-start.7 = (bf16[128,256]{1,0:T(8,128)(2,1)S(1)}, bf16[128,256]{1,0:T(8,128)(2,1)S(1)}, u32[]{:S(2)}, u32[]{:S(2)}) collective-permute-start(bf16[128,256]{1,0:T(8,128)(2,1)S(1)} %get-tuple-element.24), channel_id=1, source_target_pairs={{0,8},{4,12},{8,0},{12,4},{16,24},{20,28},{24,16},{28,20},{1,9},{5... | collective-permute-start | bytes 196616 | tf_op jit(solution)/shard_map/ppermute | solution.py:254
  22.1 6.9 %collective-permute-start.8 = (bf16[128,256]{1,0:T(8,128)(2,1)S(1)}, bf16[128,256]{1,0:T(8,128)(2,1)S(1)}, u32[]{:S(2)}, u32[]{:S(2)}) collective-permute-start(bf16[128,256]{1,0:T(8,128)(2,1)S(1)} %get-tuple-element.25), channel_id=1, source_target_pairs={{0,16},{4,20},{8,24},{12,28},{16,0},{20,4},{24,8},{28,12},{1,17},{... | collective-permute-start | bytes 196616 | tf_op jit(solution)/shard_map/ppermute | solution.py:254
  25.4 6.1 %collective-permute-start.9 = (bf16[128,256]{1,0:T(8,128)(2,1)S(1)}, bf16[128,256]{1,0:T(8,128)(2,1)S(1)}, u32[]{:S(2)}, u32[]{:S(2)}) collective-permute-start(bf16[128,256]{1,0:T(8,128)(2,1)S(1)} %get-tuple-element.26), channel_id=1, source_target_pairs={{0,24},{4,28},{8,16},{12,20},{16,8},{20,12},{24,0},{28,4},{1,25},{... | collective-permute-start | bytes 196616 | tf_op jit(solution)/shard_map/ppermute | solution.py:254
  31.7 1.4 %collective-permute-start.10 = (bf16[128,512]{1,0:T(8,128)(2,1)S(1)}, bf16[128,512]{1,0:T(8,128)(2,1)S(1)}, u32[]{:S(2)}, u32[]{:S(2)}) collective-permute-start(bf16[128,512]{1,0:T(8,128)(2,1)S(1)} %get-tuple-element.28), channel_id=1, source_target_pairs={{0,1},{1,0},{2,3},{3,2},{4,5},{5,4},{6,7},{7,6},{8,9},{9,8},{10,11... | collective-permute-start | bytes 393224 | tf_op jit(solution)/shard_map/ppermute | solution.py:254
  33.6 8.7 %collective-permute-start.14 = (f32[128,512]{1,0:T(8,128)S(1)}, f32[128,512]{1,0:T(8,128)S(1)}, u32[]{:S(2)}, u32[]{:S(2)}) collective-permute-start(f32[128,512]{1,0:T(8,128)S(1)} %get-tuple-element.32), channel_id=1, source_target_pairs={{0,1},{1,0},{2,3},{3,2},{4,5},{5,4},{6,7},{7,6},{8,9},{9,8},{10,11... | collective-permute-start | bytes 786440 | tf_op jit(solution)/shard_map/ppermute | solution.py:254
  34.3 6.4 %collective-permute-start.12 = (bf16[128,512]{1,0:T(8,128)(2,1)S(1)}, bf16[128,512]{1,0:T(8,128)(2,1)S(1)}, u32[]{:S(2)}, u32[]{:S(2)}) collective-permute-start(bf16[128,512]{1,0:T(8,128)(2,1)S(1)} %get-tuple-element.30), channel_id=1, source_target_pairs={{0,2},{1,3},{2,0},{3,1},{4,6},{5,7},{6,4},{7,5},{8,10},{9,11},{10,... | collective-permute-start | bytes 393224 | tf_op jit(solution)/shard_map/ppermute | solution.py:254
  35.9 6.5 %collective-permute-start.13 = (bf16[128,512]{1,0:T(8,128)(2,1)S(1)}, bf16[128,512]{1,0:T(8,128)(2,1)S(1)}, u32[]{:S(2)}, u32[]{:S(2)}) collective-permute-start(bf16[128,512]{1,0:T(8,128)(2,1)S(1)} %get-tuple-element.31), channel_id=1, source_target_pairs={{0,3},{1,2},{2,1},{3,0},{4,7},{5,6},{6,5},{7,4},{8,11},{9,10},{10,... | collective-permute-start | bytes 393224 | tf_op jit(solution)/shard_map/ppermute | solution.py:254

commit v4 on v3

--- a/solution.py
+++ b/solution.py
@@ -13,6 +13,7 @@
 K = 2048
 BANDS = 16
 BLOCK = 128
+TILE = 16
 VMEM = pltpu.MemorySpace.VMEM
 BF16 = jnp.bfloat16
 F32 = jnp.float32
@@ -23,7 +24,10 @@
     taps = np.arange(K, dtype=np.float64)
     bands = np.arange(1, BANDS + 1, dtype=np.float64)
     angles = 2.0 * np.pi * ((taps[None, :] * bands[:, None]) % K) / K
-    return np.concatenate([taps[None, :] / K, np.cos(angles), np.sin(angles)], 0).astype(np.float32)
+    features = np.concatenate([taps[None, :] / K, np.cos(angles), np.sin(angles)], 0)
+    features = np.pad(features, ((0, -len(features) % TILE), (0, 0)))
+    high, low = split(features)
+    return np.concatenate([high, low, high], 0)
 
 
 def split(table):
@@ -63,8 +67,7 @@
 def sine(x):
     turns = jnp.round(x * (1.0 / math.pi))
     r = x - turns * 3.140625
-    r = r - turns * 9.67502593994140625e-4
-    r = r - turns * 1.50995799097e-7
+    r = r - turns * 9.676535897932e-4
     odd = turns - 2.0 * jnp.floor(turns * 0.5)
     sign = 1.0 - 2.0 * odd
     s = r * r
@@ -83,10 +86,23 @@
     return jnp.sum(jnp.where(diagonal, jnp.broadcast_to(row, square), 0.0), 1, keepdims=True)
 
 
+def parts_of(x):
+    high = x.astype(BF16)
+    return high, (x - high.astype(F32)).astype(BF16)
+
+
 def dot_first(a, b):
-    return lax.dot_general(
-        a, b, (((0,), (0,)), ((), ())), precision=HIGHEST, preferred_element_type=F32
-    )
+    return lax.dot_general(a, b, (((0,), (0,)), ((), ())), preferred_element_type=F32)
+
+
+def stack_left(x):
+    high, low = parts_of(x)
+    return jnp.concatenate([high, high, low], 0)
+
+
+def stack_right(x):
+    high, low = parts_of(x)
+    return jnp.concatenate([high, low, high], 0)
 
 
 def fetch(sources, targets, sems):
@@ -99,50 +115,47 @@
     return copies
 
 
-def hidden_kernel(count, *refs):
-    out, held, sems = refs[count], refs[count + 1 : 2 * count + 1], refs[2 * count + 1]
-    for copy in fetch(refs[:count], held, sems):
-        copy.wait()
-    feat, w_first, bias, freq, w_mid = held
+def hidden_kernel(feat, w_first, bias, freq, w_mid, out, left):
     freqs = column(freq[...])
-    first = sine(freqs * (dot_first(w_first[...], feat[...]) + column(bias[...])))
-    out[...] = sine(freqs * dot_first(w_mid[...], first))
-
-
-def filter_kernel(count, hidden, *refs):
-    out, held, sems = refs[count], refs[count + 1 : 2 * count + 1], refs[2 * count + 1]
-    for copy in fetch(refs[:count], held, sems):
-        copy.wait()
-    w_last, rate, table = held
+    high, low = parts_of(w_first[...])
+    count = high.shape[0]
+    rows = left.shape[0] // 3
+    left[...] = jnp.zeros(left.shape, BF16)
+    for n, part in enumerate((high, high, low)):
+        left[n * rows : n * rows + count, :] = part
+    first = sine(freqs * (dot_first(left[...], feat[...]) + column(bias[...])))
+    second = sine(freqs * dot_first(stack_left(w_mid[...]), stack_right(first)))
+    out[...] = stack_right(second)
+
+
+def filter_kernel(hidden, w_last, rate, table_high, table_low, out):
     share = out.shape[1]
     own = pl.ds(pl.multiple_of((lax.axis_index("seq") // 2) * share, share), share)
-    raw = dot_first(w_last[:, own], hidden[...])
-    taps = raw.shape[1]
-    position = lax.broadcasted_iota(jnp.int32, (1, taps), 1).astype(F32)
-    filt = (raw * jnp.exp(-column(rate[:, own]) * position)).astype(BF16)
-    blocks = taps // BLOCK
-    rows = jnp.concatenate([filt[:, j * BLOCK : (j + 1) * BLOCK] for j in range(blocks)], 0)
-    spec = dot(jnp.concatenate([rows, rows], 1), table[...])
-    out[...] = spec.reshape(out.shape)
-
-
-def conv_kernel(pieces, filt, table_high, table_low, back_high, back_low, *refs):
+    raw = dot_first(stack_left(w_last[:, own]), hidden[...])
+    rates = column(rate[:, own])
+    lane = lax.broadcasted_iota(jnp.int32, (1, BLOCK), 1).astype(F32)
+    decay, step = jnp.exp(-rates * lane), jnp.exp(-rates * float(BLOCK))
+    before = [jnp.zeros((share, BLOCK), BF16)]
+    for j in range(out.shape[0]):
+        before.append((raw[:, j * BLOCK : (j + 1) * BLOCK] * decay).astype(BF16))
+        decay = decay * step
+    window = jnp.concatenate([jnp.concatenate(before[:-1], 0), jnp.concatenate(before[1:], 0)], 1)
+    out[...] = (dot(window, table_high[...]) + dot(window, table_low[...])).reshape(out.shape)
+
+
+def conv_kernel(pieces, filt, table, back, *refs):
     ins, outs = refs[: 2 * pieces], refs[2 * pieces : 3 * pieces]
-    samples, spec, total, result = refs[3 * pieces :]
+    spec, total, result = refs[3 * pieces :]
     me = lax.axis_index("seq")
     side = lax.rem(me, 2)
-    blocks, channels = samples.shape[0] - 1, samples.shape[1]
+    channels = spec.shape[1]
     per = ins[0].shape[1] // BLOCK
-    samples[0] = jnp.zeros((channels, BLOCK), BF16)
+    spec[0:per] = jnp.zeros((per,) + spec.shape[1:], F32)
     for flips, piece in enumerate(ins):
-        at = lax.bitwise_xor(me, flips) * per
+        at = lax.bitwise_xor(me, flips) * per + per
         for part in range(per):
-            samples[at + (1 + part)] = piece[:, part * BLOCK : (part + 1) * BLOCK]
-    before = samples[0:blocks].reshape(blocks * channels, BLOCK)
-    current = samples[1 : blocks + 1].reshape(blocks * channels, BLOCK)
-    window = jnp.concatenate([before, current], 1)
-    spec[0:per] = jnp.zeros((per,) + spec.shape[1:], F32)
-    spec[per:] = (dot(window, table_high[...]) + dot(window, table_low[...])).reshape((blocks,) + spec.shape[1:])
+            block = piece[:, part * BLOCK : (part + 1) * BLOCK]
+            spec[at + part] = dot(jnp.concatenate([block, block], 1), table[...])
     taps = filt.shape[0]
     packed = lax.broadcasted_iota(jnp.int32, (8, BLOCK), 1) == 0
 
@@ -173,10 +186,9 @@
         return carry
 
     lax.fori_loop(0, channels // 8, group, 0)
-    sums = total[...].reshape(-1, 2 * BLOCK)
-    high = sums.astype(BF16)
-    low = (sums - high.astype(F32)).astype(BF16)
-    conv = dot(high, back_high[...]) + dot(low, back_high[...]) + dot(high, back_low[...])
+    high, low = parts_of(total[...].reshape(-1, 2 * BLOCK))
+    conv = dot(high, back[...])
+    conv = conv[:, :BLOCK] + conv[:, BLOCK:] + dot(low, back[:, :BLOCK])
     result[...] = conv.astype(BF16).reshape(result.shape)
     for k, out in enumerate(outs):
         at = lax.bitwise_xor(me // 2, k) * per
@@ -215,16 +227,20 @@
     out[pl.ds(pl.multiple_of((1 - core) * half, half), half), :] = there.astype(BF16)
 
 
-def turn_kernel(pieces, signal, *outs):
-    outs, (held, sems) = outs[:pieces], outs[pieces:]
+def turn_kernel(pieces, count, signal, *refs):
+    others, outs, copied = refs[:count], refs[count : count + pieces], refs[count + pieces : 2 * count + pieces]
+    held, sems = refs[2 * count + pieces :]
     place = lax.axis_index("seq") // 2
     share = outs[0].shape[0]
     order = [*range(1, pieces), 0]
     starts = [pl.multiple_of(lax.bitwise_xor(place, k) * share, share) for k in order]
-    copies = fetch([signal.at[:, pl.ds(at, share)] for at in starts], [held.at[n] for n in range(pieces)], sems)
+    sources = [signal.at[:, pl.ds(at, share)] for at in starts]
+    copies = fetch([*sources, *others], [*(held.at[n] for n in range(pieces)), *copied], sems)
     for n, k in enumerate(order):
         copies[n].wait()
         outs[k][...] = held[n].T
+    for copy in copies[pieces:]:
+        copy.wait()
 
 
 def call(kernel, outs, *args, scratch=(), flops=0, grant=12, hbm=()):
@@ -266,55 +282,55 @@
     width = out_w.shape[1] // heads
     row = lambda v: v.reshape(1, -1)
 
+    forward_high, forward_low = split(forward_table())
+    block_table = np.concatenate([forward_high[:BLOCK], forward_low[:BLOCK]], 0)
+    back_table = np.concatenate(split(backward_table()), 1)
+    operands = (
+        jnp.asarray(feature_table()),
+        w_first,
+        row(b_first),
+        row(freq),
+        w_mid,
+        w_last,
+        row(rate),
+        jnp.asarray(forward_high),
+        jnp.asarray(forward_low),
+    )
     piece = shape((share, length_local))
-    own = call(
-        functools.partial(turn_kernel, pieces),
-        (piece,) * pieces,
+    turned = call(
+        functools.partial(turn_kernel, pieces, len(operands)),
+        (piece,) * pieces + tuple(shape(v.shape, v.dtype) for v in operands),
         signal,
-        scratch=[pltpu.VMEM((pieces, length_local, share), BF16), pltpu.SemaphoreType.DMA((pieces,))],
-        hbm=(0,),
-    )
+        *operands,
+        scratch=[
+            pltpu.VMEM((pieces, length_local, share), BF16),
+            pltpu.SemaphoreType.DMA((pieces + len(operands),)),
+        ],
+        hbm=range(1 + len(operands)),
+    )
+    own, operands = turned[:pieces], turned[pieces:]
     parts = []
     for k in range(pieces):
         part = flip(own[k], "seq", 2 * k) if k else own[0]
         parts += [part, flip(part, "seq", 1)]
 
-    forward_high, forward_low = split(forward_table())
-    back_high, back_low = split(backward_table())
-    filter_table = np.concatenate([forward_high[:BLOCK], forward_low[:BLOCK]], 0)
-    operands = (jnp.asarray(feature_table()), w_first, row(b_first), row(freq), w_mid)
     hidden = call(
-        functools.partial(hidden_kernel, len(operands)),
-        shape((w_mid.shape[1], K), F32),
-        *operands,
-        scratch=[pltpu.VMEM(v.shape, v.dtype) for v in operands]
-        + [pltpu.SemaphoreType.DMA((len(operands),))],
+        hidden_kernel,
+        shape((3 * w_mid.shape[1], K)),
+        *operands[:5],
+        scratch=[pltpu.VMEM((operands[0].shape[0], w_first.shape[1]), BF16)],
         flops=1_000_000_000,
-        hbm=range(len(operands)),
-    )
-    operands = (w_last, row(rate), jnp.asarray(filter_table))
-    filt = call(
-        functools.partial(filter_kernel, len(operands)),
-        shape((taps, share, 2 * BLOCK), F32),
-        hidden,
-        *operands,
-        scratch=[pltpu.VMEM(v.shape, v.dtype) for v in operands]
-        + [pltpu.SemaphoreType.DMA((len(operands),))],
-        flops=2_000_000_000,
-        hbm=range(1, 1 + len(operands)),
-    )
+    )
+    filt = call(filter_kernel, shape((taps, share, 2 * BLOCK), F32), hidden, *operands[5:], flops=2_000_000_000)
     other_w = flip(out_w, "head", 1)
     convs = call(
         functools.partial(conv_kernel, pieces),
         (piece,) * pieces,
         filt,
-        forward_high,
-        forward_low,
-        back_high,
-        back_low,
+        block_table,
+        back_table,
         *parts,
         scratch=[
-            pltpu.VMEM((blocks + 1, share, BLOCK), BF16),
             pltpu.VMEM((per + blocks, share, 2 * BLOCK), F32),
             pltpu.VMEM((blocks // 2, share, 2 * BLOCK), F32),
             pltpu.VMEM((blocks // 2, share, BLOCK), BF16),

time: 43.3 us -> 42.2 us (0.975)
  Pallas kernels: 11.6 us -> 7.81 us
  waiting for transfers between devices: 14.2 us -> 16.6 us
    pallas_call x8, Pallas kernels: 11.6 us -> 7.81 us  [call(): return run(*args)]
    ppermute x15, waiting for transfers between devices: 14.2 us -> 16.6 us  [flip(): return lax.ppermute(x, axis, [(i, i ^ by) for i in range(size)])]
  transfers between devices with their start and end apart: 15 -> 15, of which waited for: 7 -> 10; matrix products, arithmetic and copies ran while one was open for 0% -> 0% of each run, Pallas kernels for 24% -> 16%
where the time goes in v4:
time: 42.2 us; the launch traced here: 42.1 us
  starting transfers between devices  17.5 us (41%)
  waiting for transfers between devices  16.6 us (39%)
  Pallas kernels  7.81 us (19%)
    ppermute x15, starting transfers between devices, flip(): return lax.ppermute(x, axis, [(i, i ^ by) for i in range(size)])  17.5 us
    ppermute x15, waiting for transfers between devices, flip(): return lax.ppermute(x, axis, [(i, i ^ by) for i in range(size)])  16.6 us
    pallas_call x8, Pallas kernels, call(): return run(*args)  7.81 us
  transfers between devices with their start and end apart: 15, of which 10 were waited for; matrix products, arithmetic and copies ran while one was open for 0% of the time, Pallas kernels for 16%

profile of v4, /device:TPU:0, one launch (start us, length us, event | category | flops | bytes accessed | tf_op | source)
XLA Modules:
  0.0 42.1 jit_solution(7963563315707600372)
XLA Ops:
  0.0 0.5 %collective-permute-start.11 = (bf16[512,2048]{1,0:T(8,128)(2,1)}, bf16[512,2048]{1,0:T(8,128)(2,1)S(1)}, u32[]{:S(2)}, u32[]{:S(2)}) collective-permute-start(bf16[512,2048]{1,0:T(8,128)(2,1)} %own_w.3), channel_id=1, source_target_pairs={{0,1},{1,0},{2,3},{3,2},{4,5},{5,4},{6,7},{7,6},{8,9},{9,8},{10,11... | collective-permute-start | bytes 6291464 | tf_op jit(solution)/shard_map/ppermute | solution.py:270
  0.5 1.5 %shard_map.145 = (bf16[128,256]{1,0:T(8,128)(2,1)S(1)}, bf16[128,256]{1,0:T(8,128)(2,1)S(1)}, bf16[128,256]{1,0:T(8,128)(2,1)S(1)}, bf16[128,256]{1,0:T(8,128)(2...) custom-call(bf16[256,512]{1,0:T(8,128)(2,1)} %signal.3, ...), custom_call_target="tpu_custom_call" | custom-call | tf_op jit(solution)/shard_map/pallas_call | solution.py:261
  2.0 2.6 %collective-permute-start.1 = (bf16[128,256]{1,0:T(8,128)(2,1)S(1)}, bf16[128,256]{1,0:T(8,128)(2,1)S(1)}, u32[]{:S(2)}, u32[]{:S(2)}) collective-permute-start(bf16[128,256]{1,0:T(8,128)(2,1)S(1)} %get-tuple-element.38), channel_id=1, source_target_pairs={{0,8},{4,12},{8,0},{12,4},{16,24},{20,28},{24,16},{28,20},{1,9},{5... | collective-permute-start | bytes 196616 | tf_op jit(solution)/shard_map/ppermute | solution.py:270
  4.6 2.6 %collective-permute-start.3 = (bf16[128,256]{1,0:T(8,128)(2,1)S(1)}, bf16[128,256]{1,0:T(8,128)(2,1)S(1)}, u32[]{:S(2)}, u32[]{:S(2)}) collective-permute-start(bf16[128,256]{1,0:T(8,128)(2,1)S(1)} %get-tuple-element.39), channel_id=1, source_target_pairs={{0,16},{4,20},{8,24},{12,28},{16,0},{20,4},{24,8},{28,12},{1,17},{... | collective-permute-start | bytes 196616 | tf_op jit(solution)/shard_map/ppermute | solution.py:270
  7.2 0.0 collective-permute-start.5
  7.2 1.7 %collective-permute-start = (bf16[128,256]{1,0:T(8,128)(2,1)S(1)}, bf16[128,256]{1,0:T(8,128)(2,1)S(1)}, u32[]{:S(2)}, u32[]{:S(2)}) collective-permute-start(bf16[128,256]{1,0:T(8,128)(2,1)S(1)} %get-tuple-element.37.refs_0_), channel_id=1, source_target_pairs={{0,4},{4,0},{8,12},{12,8},{16,20},{20,16},{24,28},{28,24},{1,5},{5... | collective-permute-start | bytes 196616 | tf_op jit(solution)/shard_map/ppermute | solution.py:270
  8.9 1.3 %shard_map.146.hidden = bf16[192,2048]{1,0:T(8,128)(2,1)S(1)} custom-call(bf16[144,2048]{1,0:T(8,128)(2,1)S(1)} %get-tuple-element.28.feat, f32[33,64]{1,0:T(8,128)S(1)} %get-tuple-element.29.w_first, f32[1,64]{1,0:T(1,128)S(1)} %get-tuple-element.30.bias, f32[1,64]{1,0:T(1,128)S(1)} %get-tuple-element.31.freq, f32[64,64]{1,0:T(8,128)S(1)} %get-tuple-element.32.w_mid), custom_call_target="tpu_custom_call" | custom-call | flops 1000000000 | tf_op jit(solution)/shard_map/pallas_call | solution.py:261
  10.2 0.0 collective-permute-done.1.refs_2_
  10.2 0.4 collective-permute-start.2
  10.6 1.0 %collective-permute-done.3.refs_4_ = bf16[128,256]{1,0:T(8,128)(2,1)S(1)} collective-permute-done((bf16[128,256]{1,0:T(8,128)(2,1)S(1)}, bf16[128,256]{1,0:T(8,128)(2,1)S(1)}, u32[]{:S(2)}, u32[]{:S(2)}) %collective-permute-start.3) | collective-permute-done | bytes 65568 | tf_op jit(solution)/shard_map/ppermute | solution.py:270
  11.6 1.5 %collective-permute-start.4 = (bf16[128,256]{1,0:T(8,128)(2,1)S(1)}, bf16[128,256]{1,0:T(8,128)(2,1)S(1)}, u32[]{:S(2)}, u32[]{:S(2)}) collective-permute-start(bf16[128,256]{1,0:T(8,128)(2,1)S(1)} %collective-permute-done.3.refs_4_), channel_id=1, source_target_pairs={{0,4},{4,0},{8,12},{12,8},{16,20},{20,16},{24,28},{28,24},{1,5},{5... | collective-permute-start | bytes 196616 | tf_op jit(solution)/shard_map/ppermute | solution.py:270
  13.1 0.1 collective-permute-done.5.refs_6_
  13.3 1.5 %collective-permute-start.6 = (bf16[128,256]{1,0:T(8,128)(2,1)S(1)}, bf16[128,256]{1,0:T(8,128)(2,1)S(1)}, u32[]{:S(2)}, u32[]{:S(2)}) collective-permute-start(bf16[128,256]{1,0:T(8,128)(2,1)S(1)} %collective-permute-done.5.refs_6_), channel_id=1, source_target_pairs={{0,4},{4,0},{8,12},{12,8},{16,20},{20,16},{24,28},{28,24},{1,5},{5... | collective-permute-start | bytes 196616 | tf_op jit(solution)/shard_map/ppermute | solution.py:270
  14.8 0.0 copy-start.4
  14.8 0.9 %shard_map.147.filt = f32[16,128,256]{2,1,0:T(8,128)S(1)} custom-call(bf16[192,2048]{1,0:T(8,128)(2,1)S(1)} %shard_map.146.hidden, f32[64,512]{1,0:T(8,128)S(1)} %get-tuple-element.33.w_last, f32[1,512]{1,0:T(1,128)S(1)} %get-tuple-element.34.rate, bf16[256,256]{1,0:T(8,128)(2,1)S(1)} %get-tuple-element.35.table_high, ...), custom_call_target="tpu_custom_call" | custom-call | flops 2000000000 | tf_op jit(solution)/shard_map/pallas_call | solution.py:261
  15.7 0.0 copy-start.1
  15.7 0.0 copy-start.2
  15.7 0.0 copy-start.3
  15.7 0.0 collective-permute-done.refs_1_
  15.8 0.0 collective-permute-done.2.refs_3_
  15.8 0.4 collective-permute-done.4.refs_5_
  16.2 1.4 %collective-permute-done.6.refs_7_ = bf16[128,256]{1,0:T(8,128)(2,1)S(1)} collective-permute-done((bf16[128,256]{1,0:T(8,128)(2,1)S(1)}, bf16[128,256]{1,0:T(8,128)(2,1)S(1)}, u32[]{:S(2)}, u32[]{:S(2)}) %collective-permute-start.6) | collective-permute-done | bytes 65568 | tf_op jit(solution)/shard_map/ppermute | solution.py:270
  17.5 0.0 copy-done.4
  17.5 0.0 copy-done.5
  17.5 2.3 %shard_map.148 = (bf16[128,256]{1,0:T(8,128)(2,1)S(1)}, bf16[128,256]{1,0:T(8,128)(2,1)S(1)}, bf16[128,256]{1,0:T(8,128)(2,1)S(1)}, bf16[128,256]{1,0:T(8,128)(2,1)S(1)}) custom-call(f32[16,128,256]{2,1,0:T(8,128)S(1)} %shard_map.147.filt, bf16[256,256]{1,0:T(8,128)(2,1)S(1)} %copy-done.4, bf16[256,256]{1,0:T(8,128)(2,1)S(1)} %copy-done.5, ...), custom_call_target="tpu_custom_call" | custom-call | flops 3000000000 | tf_op jit(solution)/shard_map/pallas_call | solution.py:261
  19.8 1.4 %collective-permute-start.7 = (bf16[128,256]{1,0:T(8,128)(2,1)S(1)}, bf16[128,256]{1,0:T(8,128)(2,1)S(1)}, u32[]{:S(2)}, u32[]{:S(2)}) collective-permute-start(bf16[128,256]{1,0:T(8,128)(2,1)S(1)} %get-tuple-element.42), channel_id=1, source_target_pairs={{0,8},{4,12},{8,0},{12,4},{16,24},{20,28},{24,16},{28,20},{1,9},{5... | collective-permute-start | bytes 196616 | tf_op jit(solution)/shard_map/ppermute | solution.py:270
  21.2 3.3 %collective-permute-start.8 = (bf16[128,256]{1,0:T(8,128)(2,1)S(1)}, bf16[128,256]{1,0:T(8,128)(2,1)S(1)}, u32[]{:S(2)}, u32[]{:S(2)}) collective-permute-start(bf16[128,256]{1,0:T(8,128)(2,1)S(1)} %get-tuple-element.43), channel_id=1, source_target_pairs={{0,16},{4,20},{8,24},{12,28},{16,0},{20,4},{24,8},{28,12},{1,17},{... | collective-permute-start | bytes 196616 | tf_op jit(solution)/shard_map/ppermute | solution.py:270
  24.4 0.0 collective-permute-start.9
  24.4 0.4 collective-permute-done.7.refs_1_
  24.9 3.0 %collective-permute-done.8.refs_2_ = bf16[128,256]{1,0:T(8,128)(2,1)S(1)} collective-permute-done((bf16[128,256]{1,0:T(8,128)(2,1)S(1)}, bf16[128,256]{1,0:T(8,128)(2,1)S(1)}, u32[]{:S(2)}, u32[]{:S(2)}) %collective-permute-start.8) | collective-permute-done | bytes 65568 | tf_op jit(solution)/shard_map/ppermute | solution.py:270
  27.9 2.6 %collective-permute-done.9.refs_3_ = bf16[128,256]{1,0:T(8,128)(2,1)S(1)} collective-permute-done((bf16[128,256]{1,0:T(8,128)(2,1)S(1)}, bf16[128,256]{1,0:T(8,128)(2,1)S(1)}, u32[]{:S(2)}, u32[]{:S(2)}) %collective-permute-start.9) | collective-permute-done | bytes 65568 | tf_op jit(solution)/shard_map/ppermute | solution.py:270
  30.5 0.0 copy-done.1
  30.5 0.0 copy-done.2
  30.5 0.0 copy-done.3
  30.5 0.2 shard_map.149
  30.7 0.1 collective-permute-start.10
  30.8 1.3 %collective-permute-done.10.other = bf16[128,512]{1,0:T(8,128)(2,1)S(1)} collective-permute-done((bf16[128,512]{1,0:T(8,128)(2,1)S(1)}, bf16[128,512]{1,0:T(8,128)(2,1)S(1)}, u32[]{:S(2)}, u32[]{:S(2)}) %collective-permute-start.10) | collective-permute-done | bytes 131104 | tf_op jit(solution)/shard_map/ppermute | solution.py:270
  32.1 0.0 collective-permute-done.11.other_w
  32.1 0.0 copy-done
  32.1 0.5 %shard_map.150 = (f32[128,512]{1,0:T(8,128)S(1)}, f32[128,512]{1,0:T(8,128)S(1)}) custom-call(bf16[128,512]{1,0:T(8,128)(2,1)S(1)} %get-tuple-element.45.own, bf16[128,512]{1,0:T(8,128)(2,1)S(1)} %collective-permute-done.10.other, bf16[512,2048]{1,0:T(8,128)(2,1)S(1)} %copy-done, bf16[512,2048]{1,0:T(8,128)(2,1)S(1)} %collective-permute-done.11.other_w), custom_call_target="tpu_custom_call" | custom-call | flops 500000000 | tf_op jit(solution)/shard_map/pallas_call | solution.py:261
  32.6 0.2 collective-permute-start.14
  32.8 0.5 %shard_map.151 = (bf16[128,512]{1,0:T(8,128)(2,1)S(1)}, bf16[128,512]{1,0:T(8,128)(2,1)S(1)}) custom-call(bf16[128,512]{1,0:T(8,128)(2,1)S(1)} %get-tuple-element.45.own, bf16[128,512]{1,0:T(8,128)(2,1)S(1)} %collective-permute-done.10.other, bf16[512,2048]{1,0:T(8,128)(2,1)S(1)} %copy-done, bf16[512,2048]{1,0:T(8,128)(2,1)S(1)} %collective-permute-done.11.other_w), custom_call_target="tpu_custom_call" | custom-call | flops 500000000 | tf_op jit(solution)/shard_map/pallas_call | solution.py:261
  33.3 1.6 %collective-permute-start.12 = (bf16[128,512]{1,0:T(8,128)(2,1)S(1)}, bf16[128,512]{1,0:T(8,128)(2,1)S(1)}, u32[]{:S(2)}, u32[]{:S(2)}) collective-permute-start(bf16[128,512]{1,0:T(8,128)(2,1)S(1)} %get-tuple-element.48), channel_id=1, source_target_pairs={{0,2},{1,3},{2,0},{3,1},{4,6},{5,7},{6,4},{7,5},{8,10},{9,11},{10,... | collective-permute-start | bytes 393224 | tf_op jit(solution)/shard_map/ppermute | solution.py:270
  34.8 0.2 collective-permute-start.13
  35.1 4.6 %collective-permute-done.12.a = bf16[128,512]{1,0:T(8,128)(2,1)S(1)} collective-permute-done((bf16[128,512]{1,0:T(8,128)(2,1)S(1)}, bf16[128,512]{1,0:T(8,128)(2,1)S(1)}, u32[]{:S(2)}, u32[]{:S(2)}) %collective-permute-start.12) | collective-permute-done | bytes 131104 | tf_op jit(solution)/shard_map/ppermute | solution.py:270
  39.7 1.6 %collective-permute-done.13.b = bf16[128,512]{1,0:T(8,128)(2,1)S(1)} collective-permute-done((bf16[128,512]{1,0:T(8,128)(2,1)S(1)}, bf16[128,512]{1,0:T(8,128)(2,1)S(1)}, u32[]{:S(2)}, u32[]{:S(2)}) %collective-permute-start.13) | collective-permute-done | bytes 131104 | tf_op jit(solution)/shard_map/ppermute | solution.py:270
  41.3 0.0 collective-permute-done.14.c
  41.3 0.8 %shard_map.152 = bf16[256,512]{1,0:T(8,128)(2,1)} custom-call(f32[128,512]{1,0:T(8,128)S(1)} %get-tuple-element.47.own, bf16[128,512]{1,0:T(8,128)(2,1)S(1)} %collective-permute-done.12.a, bf16[128,512]{1,0:T(8,128)(2,1)S(1)} %collective-permute-done.13.b, f32[128,512]{1,0:T(8,128)S(1)} %collective-permute-done.14.c), custom_call_target="tpu_custom_call" | custom-call | tf_op jit(solution)/shard_map/pallas_call | solution.py:261
  (2 shorter events, 0.0 us)
Async XLA Ops:
  0.0 32.1 %collective-permute-start.11 = (bf16[512,2048]{1,0:T(8,128)(2,1)}, bf16[512,2048]{1,0:T(8,128)(2,1)S(1)}, u32[]{:S(2)}, u32[]{:S(2)}) collective-permute-start(bf16[512,2048]{1,0:T(8,128)(2,1)} %own_w.3), channel_id=1, source_target_pairs={{0,1},{1,0},{2,3},{3,2},{4,5},{5,4},{6,7},{7,6},{8,9},{9,8},{10,11... | collective-permute-start | bytes 6291464 | tf_op jit(solution)/shard_map/ppermute | solution.py:270
  2.0 8.2 %collective-permute-start.1 = (bf16[128,256]{1,0:T(8,128)(2,1)S(1)}, bf16[128,256]{1,0:T(8,128)(2,1)S(1)}, u32[]{:S(2)}, u32[]{:S(2)}) collective-permute-start(bf16[128,256]{1,0:T(8,128)(2,1)S(1)} %get-tuple-element.38), channel_id=1, source_target_pairs={{0,8},{4,12},{8,0},{12,4},{16,24},{20,28},{24,16},{28,20},{1,9},{5... | collective-permute-start | bytes 196616 | tf_op jit(solution)/shard_map/ppermute | solution.py:270
  4.6 7.0 %collective-permute-start.3 = (bf16[128,256]{1,0:T(8,128)(2,1)S(1)}, bf16[128,256]{1,0:T(8,128)(2,1)S(1)}, u32[]{:S(2)}, u32[]{:S(2)}) collective-permute-start(bf16[128,256]{1,0:T(8,128)(2,1)S(1)} %get-tuple-element.39), channel_id=1, source_target_pairs={{0,16},{4,20},{8,24},{12,28},{16,0},{20,4},{24,8},{28,12},{1,17},{... | collective-permute-start | bytes 196616 | tf_op jit(solution)/shard_map/ppermute | solution.py:270
  7.2 6.1 %collective-permute-start.5 = (bf16[128,256]{1,0:T(8,128)(2,1)S(1)}, bf16[128,256]{1,0:T(8,128)(2,1)S(1)}, u32[]{:S(2)}, u32[]{:S(2)}) collective-permute-start(bf16[128,256]{1,0:T(8,128)(2,1)S(1)} %get-tuple-element.40), channel_id=1, source_target_pairs={{0,24},{4,28},{8,16},{12,20},{16,8},{20,12},{24,0},{28,4},{1,25},{... | collective-permute-start | bytes 196616 | tf_op jit(solution)/shard_map/ppermute | solution.py:270
  7.2 8.5 %collective-permute-start = (bf16[128,256]{1,0:T(8,128)(2,1)S(1)}, bf16[128,256]{1,0:T(8,128)(2,1)S(1)}, u32[]{:S(2)}, u32[]{:S(2)}) collective-permute-start(bf16[128,256]{1,0:T(8,128)(2,1)S(1)} %get-tuple-element.37.refs_0_), channel_id=1, source_target_pairs={{0,4},{4,0},{8,12},{12,8},{16,20},{20,16},{24,28},{28,24},{1,5},{5... | collective-permute-start | bytes 196616 | tf_op jit(solution)/shard_map/ppermute | solution.py:270
  10.2 5.5 %collective-permute-start.2 = (bf16[128,256]{1,0:T(8,128)(2,1)S(1)}, bf16[128,256]{1,0:T(8,128)(2,1)S(1)}, u32[]{:S(2)}, u32[]{:S(2)}) collective-permute-start(bf16[128,256]{1,0:T(8,128)(2,1)S(1)} %collective-permute-done.1.refs_2_), channel_id=1, source_target_pairs={{0,4},{4,0},{8,12},{12,8},{16,20},{20,16},{24,28},{28,24},{1,5},{5... | collective-permute-start | bytes 196616 | tf_op jit(solution)/shard_map/ppermute | solution.py:270
  11.6 4.6 %collective-permute-start.4 = (bf16[128,256]{1,0:T(8,128)(2,1)S(1)}, bf16[128,256]{1,0:T(8,128)(2,1)S(1)}, u32[]{:S(2)}, u32[]{:S(2)}) collective-permute-start(bf16[128,256]{1,0:T(8,128)(2,1)S(1)} %collective-permute-done.3.refs_4_), channel_id=1, source_target_pairs={{0,4},{4,0},{8,12},{12,8},{16,20},{20,16},{24,28},{28,24},{1,5},{5... | collective-permute-start | bytes 196616 | tf_op jit(solution)/shard_map/ppermute | solution.py:270
  13.3 4.3 %collective-permute-start.6 = (bf16[128,256]{1,0:T(8,128)(2,1)S(1)}, bf16[128,256]{1,0:T(8,128)(2,1)S(1)}, u32[]{:S(2)}, u32[]{:S(2)}) collective-permute-start(bf16[128,256]{1,0:T(8,128)(2,1)S(1)} %collective-permute-done.5.refs_6_), channel_id=1, source_target_pairs={{0,4},{4,0},{8,12},{12,8},{16,20},{20,16},{24,28},{28,24},{1,5},{5... | collective-permute-start | bytes 196616 | tf_op jit(solution)/shard_map/ppermute | solution.py:270
  14.8 2.7 %copy-start.4 = (bf16[256,256]{1,0:T(8,128)(2,1)S(1)}, bf16[256,256]{1,0:T(8,128)(2,1)}, u32[]{:S(2)}) copy-start(bf16[256,256]{1,0:T(8,128)(2,1)} %constant.13.clone.table) | copy-start | bytes 393220
  14.8 2.7 %copy-start.5 = (bf16[256,256]{1,0:T(8,128)(2,1)S(1)}, bf16[256,256]{1,0:T(8,128)(2,1)}, u32[]{:S(2)}) copy-start(bf16[256,256]{1,0:T(8,128)(2,1)} %constant.14.clone.back) | copy-start | bytes 393220
  15.7 14.8 %copy-start.1 = (bf16[256,512]{1,0:T(8,128)(2,1)S(1)}, bf16[256,512]{1,0:T(8,128)(2,1)}, u32[]{:S(2)}) copy-start(bf16[256,512]{1,0:T(8,128)(2,1)} %signal.3) | copy-start | bytes 786436
  15.7 14.8 %copy-start.2 = (bf16[256,512]{1,0:T(8,128)(2,1)S(1)}, bf16[256,512]{1,0:T(8,128)(2,1)}, u32[]{:S(2)}) copy-start(bf16[256,512]{1,0:T(8,128)(2,1)} %gate.1) | copy-start | bytes 786436
  15.7 14.8 %copy-start.3 = (f32[512]{0:T(512)S(1)}, f32[512]{0:T(512)}, u32[]{:S(2)}) copy-start(f32[512]{0:T(512)} %param.17) | copy-start | bytes 6148
  17.5 14.6 %copy-start = (bf16[512,2048]{1,0:T(8,128)(2,1)S(1)}, bf16[512,2048]{1,0:T(8,128)(2,1)}, u32[]{:S(2)}) copy-start(bf16[512,2048]{1,0:T(8,128)(2,1)} %own_w.3) | copy-start | bytes 6291460
  19.8 5.0 %collective-permute-start.7 = (bf16[128,256]{1,0:T(8,128)(2,1)S(1)}, bf16[128,256]{1,0:T(8,128)(2,1)S(1)}, u32[]{:S(2)}, u32[]{:S(2)}) collective-permute-start(bf16[128,256]{1,0:T(8,128)(2,1)S(1)} %get-tuple-element.42), channel_id=1, source_target_pairs={{0,8},{4,12},{8,0},{12,4},{16,24},{20,28},{24,16},{28,20},{1,9},{5... | collective-permute-start | bytes 196616 | tf_op jit(solution)/shard_map/ppermute | solution.py:270
  21.2 6.7 %collective-permute-start.8 = (bf16[128,256]{1,0:T(8,128)(2,1)S(1)}, bf16[128,256]{1,0:T(8,128)(2,1)S(1)}, u32[]{:S(2)}, u32[]{:S(2)}) collective-permute-start(bf16[128,256]{1,0:T(8,128)(2,1)S(1)} %get-tuple-element.43), channel_id=1, source_target_pairs={{0,16},{4,20},{8,24},{12,28},{16,0},{20,4},{24,8},{28,12},{1,17},{... | collective-permute-start | bytes 196616 | tf_op jit(solution)/shard_map/ppermute | solution.py:270
  24.4 6.1 %collective-permute-start.9 = (bf16[128,256]{1,0:T(8,128)(2,1)S(1)}, bf16[128,256]{1,0:T(8,128)(2,1)S(1)}, u32[]{:S(2)}, u32[]{:S(2)}) collective-permute-start(bf16[128,256]{1,0:T(8,128)(2,1)S(1)} %get-tuple-element.44), channel_id=1, source_target_pairs={{0,24},{4,28},{8,16},{12,20},{16,8},{20,12},{24,0},{28,4},{1,25},{... | collective-permute-start | bytes 196616 | tf_op jit(solution)/shard_map/ppermute | solution.py:270
  30.7 1.4 %collective-permute-start.10 = (bf16[128,512]{1,0:T(8,128)(2,1)S(1)}, bf16[128,512]{1,0:T(8,128)(2,1)S(1)}, u32[]{:S(2)}, u32[]{:S(2)}) collective-permute-start(bf16[128,512]{1,0:T(8,128)(2,1)S(1)} %get-tuple-element.46), channel_id=1, source_target_pairs={{0,1},{1,0},{2,3},{3,2},{4,5},{5,4},{6,7},{7,6},{8,9},{9,8},{10,11... | collective-permute-start | bytes 393224 | tf_op jit(solution)/shard_map/ppermute | solution.py:270
  32.6 8.7 %collective-permute-start.14 = (f32[128,512]{1,0:T(8,128)S(1)}, f32[128,512]{1,0:T(8,128)S(1)}, u32[]{:S(2)}, u32[]{:S(2)}) collective-permute-start(f32[128,512]{1,0:T(8,128)S(1)} %get-tuple-element.50), channel_id=1, source_target_pairs={{0,1},{1,0},{2,3},{3,2},{4,5},{5,4},{6,7},{7,6},{8,9},{9,8},{10,11... | collective-permute-start | bytes 786440 | tf_op jit(solution)/shard_map/ppermute | solution.py:270
  33.3 6.4 %collective-permute-start.12 = (bf16[128,512]{1,0:T(8,128)(2,1)S(1)}, bf16[128,512]{1,0:T(8,128)(2,1)S(1)}, u32[]{:S(2)}, u32[]{:S(2)}) collective-permute-start(bf16[128,512]{1,0:T(8,128)(2,1)S(1)} %get-tuple-element.48), channel_id=1, source_target_pairs={{0,2},{1,3},{2,0},{3,1},{4,6},{5,7},{6,4},{7,5},{8,10},{9,11},{10,... | collective-permute-start | bytes 393224 | tf_op jit(solution)/shard_map/ppermute | solution.py:270
  34.8 6.5 %collective-permute-start.13 = (bf16[128,512]{1,0:T(8,128)(2,1)S(1)}, bf16[128,512]{1,0:T(8,128)(2,1)S(1)}, u32[]{:S(2)}, u32[]{:S(2)}) collective-permute-start(bf16[128,512]{1,0:T(8,128)(2,1)S(1)} %get-tuple-element.49), channel_id=1, source_target_pairs={{0,3},{1,2},{2,1},{3,0},{4,7},{5,6},{6,5},{7,4},{8,11},{9,10},{10,... | collective-permute-start | bytes 393224 | tf_op jit(solution)/shard_map/ppermute | solution.py:270

commit v5 on v4

--- a/solution.py
+++ b/solution.py
@@ -143,19 +143,17 @@
     out[...] = (dot(window, table_high[...]) + dot(window, table_low[...])).reshape(out.shape)
 
 
-def conv_kernel(pieces, filt, table, back, *refs):
-    ins, outs = refs[: 2 * pieces], refs[2 * pieces : 3 * pieces]
-    spec, total, result = refs[3 * pieces :]
-    me = lax.axis_index("seq")
-    side = lax.rem(me, 2)
-    channels = spec.shape[1]
-    per = ins[0].shape[1] // BLOCK
-    spec[0:per] = jnp.zeros((per,) + spec.shape[1:], F32)
-    for flips, piece in enumerate(ins):
-        at = lax.bitwise_xor(me, flips) * per + per
+def spectra(pieces, spec, first, flips, table):
+    place = lax.axis_index("seq") // 2
+    per = pieces[0].shape[1] // BLOCK
+    for flip, piece in zip(flips, pieces):
+        at = (lax.bitwise_xor(place, flip) + first) * per
         for part in range(per):
             block = piece[:, part * BLOCK : (part + 1) * BLOCK]
             spec[at + part] = dot(jnp.concatenate([block, block], 1), table[...])
+
+
+def products(filt, spec, places, per, shift, apart, done):
     taps = filt.shape[0]
     packed = lax.broadcasted_iota(jnp.int32, (8, BLOCK), 1) == 0
 
@@ -166,26 +164,56 @@
             real, imag = ref[index, at, :BLOCK], ref[index, at, BLOCK:]
             return real, imag, real + imag
 
-        for place in range(pieces):
-            first = 2 * per * place + per
-            count = min(first + per, taps)
+        for place in range(places):
             sums = [None] * per
-            held = [load(spec, side * per + (first + q)) for q in range(per)]
-            for j in range(count):
-                taken = load(filt, j)
+            for d in range(place + 1):
+                held = [load(spec, (place - d + shift) * per + r) for r in range(per)]
+                windows = {}
                 for q in range(per):
-                    if j <= first + q:
-                        terms = tuple(x * f for x, f in zip(held[q], taken))
-                        sums[q] = terms if sums[q] is None else tuple(s + t for s, t in zip(sums[q], terms))
-                if j + 1 < count:
-                    below = [load(spec, side * per + (first - j - 1))] if j < first else [None]
-                    held = below + held[:-1]
+                    for r in range(per):
+                        j = 2 * per * d + apart + q - r
+                        if 0 <= j < taps:
+                            if j not in windows:
+                                windows[j] = load(filt, j)
+                            terms = tuple(x * f for x, f in zip(held[r], windows[j]))
+                            sums[q] = terms if sums[q] is None else tuple(s + t for s, t in zip(sums[q], terms))
             for q, (real, imag, both) in enumerate(sums):
-                total[per * place + q, at, :BLOCK] = real - jnp.where(packed, 0.0, imag)
-                total[per * place + q, at, BLOCK:] = jnp.where(packed, imag, both - real - imag)
+                done(
+                    per * place + q,
+                    at,
+                    real - jnp.where(packed, 0.0, imag),
+                    jnp.where(packed, imag, both - real - imag),
+                )
         return carry
 
-    lax.fori_loop(0, channels // 8, group, 0)
+    lax.fori_loop(0, spec.shape[1] // 8, group, 0)
+
+
+def own_kernel(pieces, filt, table, *refs):
+    ins, out, spec = refs[:pieces], refs[pieces], refs[pieces + 1]
+    per = ins[0].shape[1] // BLOCK
+    spectra(ins, spec, 0, range(pieces), table)
+
+    def done(block, at, real, imag):
+        out[block, at, :BLOCK] = real
+        out[block, at, BLOCK:] = imag
+
+    products(filt, spec, pieces, per, 0, 0, done)
+
+
+def conv_kernel(pieces, filt, table, back, own, *refs):
+    ins, outs = refs[:pieces], refs[pieces : 2 * pieces]
+    spec, total, result = refs[2 * pieces :]
+    me = lax.axis_index("seq")
+    per = ins[0].shape[1] // BLOCK
+    spec[0:per] = jnp.zeros((per,) + spec.shape[1:], F32)
+    spectra(ins, spec, 1, range(pieces), table)
+
+    def done(block, at, real, imag):
+        total[block, at, :BLOCK] = own[block, at, :BLOCK] + real
+        total[block, at, BLOCK:] = own[block, at, BLOCK:] + imag
+
+    products(filt, spec, pieces, per, lax.rem(me, 2), per, done)
     high, low = parts_of(total[...].reshape(-1, 2 * BLOCK))
     conv = dot(high, back[...])
     conv = conv[:, :BLOCK] + conv[:, BLOCK:] + dot(low, back[:, :BLOCK])
@@ -218,13 +246,31 @@
         out[...] = terms.astype(out.dtype)
 
 
-def sum_kernel(own, a, b, c, out):
-    core = lax.rem(lax.axis_index("head"), 2)
-    half = own.shape[0]
-    here = own[...] + a[...].astype(F32)
-    there = c[...].astype(F32) + b[...].astype(F32)
-    out[pl.ds(pl.multiple_of(core * half, half), half), :] = here.astype(BF16)
-    out[pl.ds(pl.multiple_of((1 - core) * half, half), half), :] = there.astype(BF16)
+def sum_kernel(other_half, first, second, *refs):
+    out, held, sem = refs[-3:]
+    half = held.shape[0]
+    part = lax.bitwise_xor(lax.rem(lax.axis_index("head"), 2), other_half)
+    held[...] = (first[...].astype(F32) + second[...].astype(F32)).astype(BF16)
+    rows = pl.ds(pl.multiple_of(part * half, half), half)
+    copy = pltpu.make_async_copy(held, out.at[rows, :], sem)
+    copy.start()
+    copy.wait()
+
+
+def add_half(other_half, out, first, second):
+    fresh = isinstance(out, jax.ShapeDtypeStruct)
+    half, width = first.shape
+    run = pl.pallas_call(
+        functools.partial(sum_kernel, other_half),
+        out_shape=shape(out.shape),
+        in_specs=[pl.BlockSpec(memory_space=VMEM)] * 2 + [pl.BlockSpec(memory_space=pltpu.HBM)] * (not fresh),
+        out_specs=pl.BlockSpec(memory_space=pltpu.HBM),
+        scratch_shapes=[pltpu.VMEM((half, width), BF16), pltpu.SemaphoreType.DMA(())],
+        input_output_aliases={} if fresh else {2: 0},
+        cost_estimate=pl.CostEstimate(flops=100_000_000, bytes_accessed=0, transcendentals=0),
+        compiler_params=pltpu.CompilerParams(vmem_limit_bytes=4 << 20),
+    )
+    return run(first, second) if fresh else run(first, second, out)
 
 
 def turn_kernel(pieces, count, signal, *refs):
@@ -309,10 +355,8 @@
         hbm=range(1 + len(operands)),
     )
     own, operands = turned[:pieces], turned[pieces:]
-    parts = []
-    for k in range(pieces):
-        part = flip(own[k], "seq", 2 * k) if k else own[0]
-        parts += [part, flip(part, "seq", 1)]
+    near = [flip(own[k], "seq", 2 * k) if k else own[0] for k in range(pieces)]
+    beside = [flip(near[k], "seq", 1) for k in range(pieces)]
 
     hidden = call(
         hidden_kernel,
@@ -323,16 +367,27 @@
     )
     filt = call(filter_kernel, shape((taps, share, 2 * BLOCK), F32), hidden, *operands[5:], flops=2_000_000_000)
     other_w = flip(out_w, "head", 1)
+    sums = shape((blocks // 2, share, 2 * BLOCK), F32)
+    early = call(
+        functools.partial(own_kernel, pieces),
+        sums,
+        filt,
+        block_table,
+        *near,
+        scratch=[pltpu.VMEM(sums.shape, F32)],
+        flops=1_000_000_000,
+    )
     convs = call(
         functools.partial(conv_kernel, pieces),
         (piece,) * pieces,
         filt,
         block_table,
         back_table,
-        *parts,
+        early,
+        *beside,
         scratch=[
-            pltpu.VMEM((per + blocks, share, 2 * BLOCK), F32),
-            pltpu.VMEM((blocks // 2, share, 2 * BLOCK), F32),
+            pltpu.VMEM((per + blocks // 2, share, 2 * BLOCK), F32),
+            pltpu.VMEM(sums.shape, F32),
             pltpu.VMEM((blocks // 2, share, BLOCK), BF16),
         ],
         flops=3_000_000_000,
@@ -353,11 +408,18 @@
     received = flip(send, "head", 1)
     terms, wide = shape((half, width)), shape((half, width), F32)
     factors = (keep, received, out_w, other_w)
-    a, b = call(functools.partial(project_kernel, (2, 3)), (terms, terms), *factors, flops=500_000_000)
-    a, b = flip(a, "head", 2), flip(b, "head", 3)
-    c, here = call(functools.partial(project_kernel, (1, 0)), (wide, wide), *factors, flops=500_000_000)
+
+    def project(flips, outs):
+        return call(functools.partial(project_kernel, flips), outs, *factors, flops=500_000_000)
+
+    (a,) = project((2,), (terms,))
+    a = flip(a, "head", 2)
+    (b,) = project((3,), (terms,))
+    b = flip(b, "head", 3)
+    c, here = project((1, 0), (wide, wide))
     c = flip(c, "head", 1)
-    return call(sum_kernel, shape((length_local, width)), here, a, b, c)
+    out = add_half(0, shape((length_local, width)), here, a)
+    return add_half(1, out, c, b)
 
 
 def shifted(x, axis, by):

time: 42.2 us -> 41.3 us (0.979)
  waiting for transfers between devices: 16.6 us -> 14.4 us
  Pallas kernels: 7.81 us -> 8.87 us
    ppermute x15, waiting for transfers between devices: 16.6 us -> 14.4 us  [flip(): return lax.ppermute(x, axis, [(i, i ^ by) for i in range(size)])]
    pallas_call x0 -> x2, Pallas kernels: none -> 1.38 us  [add_half(): return run(first, second) if fresh else run(first, second, out)]
    pallas_call x8 -> x9, Pallas kernels: 7.81 us -> 7.49 us  [call(): return run(*args)]
  transfers between devices with their start and end apart: 15 -> 15, of which waited for: 10 -> 10; matrix products, arithmetic and copies ran while one was open for 0% -> 0% of each run, Pallas kernels for 16% -> 19%
where the time goes in v5:
time: 41.3 us; the launch traced here: 41.2 us
  starting transfers between devices  17.7 us (43%)
  waiting for transfers between devices  14.4 us (35%)
  Pallas kernels  8.87 us (21%)
    ppermute x15, starting transfers between devices, flip(): return lax.ppermute(x, axis, [(i, i ^ by) for i in range(size)])  17.7 us
    ppermute x15, waiting for transfers between devices, flip(): return lax.ppermute(x, axis, [(i, i ^ by) for i in range(size)])  14.4 us
    pallas_call x9, Pallas kernels, call(): return run(*args)  7.49 us
    pallas_call x2, Pallas kernels, add_half(): return run(first, second) if fresh else run(first, second, out)  1.38 us
  transfers between devices with their start and end apart: 15, of which 10 were waited for; matrix products, arithmetic and copies ran while one was open for 0% of the time, Pallas kernels for 19%

profile of v5, /device:TPU:0, one launch (start us, length us, event | category | flops | bytes accessed | tf_op | source)
XLA Modules:
  0.0 41.2 jit_solution(14279937933983458204)
XLA Ops:
  0.0 0.5 %collective-permute-start.11 = (bf16[512,2048]{1,0:T(8,128)(2,1)}, bf16[512,2048]{1,0:T(8,128)(2,1)S(1)}, u32[]{:S(2)}, u32[]{:S(2)}) collective-permute-start(bf16[512,2048]{1,0:T(8,128)(2,1)} %own_w.5), channel_id=1, source_target_pairs={{0,1},{1,0},{2,3},{3,2},{4,5},{5,4},{6,7},{7,6},{8,9},{9,8},{10,11... | collective-permute-start | bytes 6291464 | tf_op jit(solution)/shard_map/ppermute | solution.py:316
  0.5 1.5 %shard_map.145 = (bf16[128,256]{1,0:T(8,128)(2,1)S(1)}, bf16[128,256]{1,0:T(8,128)(2,1)S(1)}, bf16[128,256]{1,0:T(8,128)(2,1)S(1)}, bf16[128,256]{1,0:T(8,128)(2...) custom-call(bf16[256,512]{1,0:T(8,128)(2,1)} %signal.3, ...), custom_call_target="tpu_custom_call" | custom-call | tf_op jit(solution)/shard_map/pallas_call | solution.py:307
  2.0 2.6 %collective-permute-start = (bf16[128,256]{1,0:T(8,128)(2,1)S(1)}, bf16[128,256]{1,0:T(8,128)(2,1)S(1)}, u32[]{:S(2)}, u32[]{:S(2)}) collective-permute-start(bf16[128,256]{1,0:T(8,128)(2,1)S(1)} %get-tuple-element.36), channel_id=1, source_target_pairs={{0,8},{4,12},{8,0},{12,4},{16,24},{20,28},{24,16},{28,20},{1,9},{5... | collective-permute-start | bytes 196616 | tf_op jit(solution)/shard_map/ppermute | solution.py:316
  4.6 2.6 %collective-permute-start.1 = (bf16[128,256]{1,0:T(8,128)(2,1)S(1)}, bf16[128,256]{1,0:T(8,128)(2,1)S(1)}, u32[]{:S(2)}, u32[]{:S(2)}) collective-permute-start(bf16[128,256]{1,0:T(8,128)(2,1)S(1)} %get-tuple-element.37), channel_id=1, source_target_pairs={{0,16},{4,20},{8,24},{12,28},{16,0},{20,4},{24,8},{28,12},{1,17},{... | collective-permute-start | bytes 196616 | tf_op jit(solution)/shard_map/ppermute | solution.py:316
  7.2 0.0 collective-permute-start.2
  7.2 1.7 %collective-permute-start.3 = (bf16[128,256]{1,0:T(8,128)(2,1)S(1)}, bf16[128,256]{1,0:T(8,128)(2,1)S(1)}, u32[]{:S(2)}, u32[]{:S(2)}) collective-permute-start(bf16[128,256]{1,0:T(8,128)(2,1)S(1)} %get-tuple-element.35.refs_0_), channel_id=1, source_target_pairs={{0,4},{4,0},{8,12},{12,8},{16,20},{20,16},{24,28},{28,24},{1,5},{5... | collective-permute-start | bytes 196616 | tf_op jit(solution)/shard_map/ppermute | solution.py:316
  8.9 1.3 %shard_map.146.hidden = bf16[192,2048]{1,0:T(8,128)(2,1)S(1)} custom-call(bf16[144,2048]{1,0:T(8,128)(2,1)S(1)} %get-tuple-element.26.feat, f32[33,64]{1,0:T(8,128)S(1)} %get-tuple-element.27.w_first, f32[1,64]{1,0:T(1,128)S(1)} %get-tuple-element.28.bias, f32[1,64]{1,0:T(1,128)S(1)} %get-tuple-element.29.freq, f32[64,64]{1,0:T(8,128)S(1)} %get-tuple-element.30.w_mid), custom_call_target="tpu_custom_call" | custom-call | flops 1000000000 | tf_op jit(solution)/shard_map/pallas_call | solution.py:307
  10.2 0.0 copy-start.4
  10.2 0.9 %shard_map.147.filt = f32[16,128,256]{2,1,0:T(8,128)S(1)} custom-call(bf16[192,2048]{1,0:T(8,128)(2,1)S(1)} %shard_map.146.hidden, f32[64,512]{1,0:T(8,128)S(1)} %get-tuple-element.31.w_last, f32[1,512]{1,0:T(1,128)S(1)} %get-tuple-element.32.rate, bf16[256,256]{1,0:T(8,128)(2,1)S(1)} %get-tuple-element.33.table_high, ...), custom_call_target="tpu_custom_call" | custom-call | flops 2000000000 | tf_op jit(solution)/shard_map/pallas_call | solution.py:307
  11.1 0.0 copy-start.5
  11.2 0.0 collective-permute-done.refs_1_
  11.2 0.4 collective-permute-start.4
  11.5 0.1 collective-permute-done.1.refs_2_
  11.6 1.7 %collective-permute-start.5 = (bf16[128,256]{1,0:T(8,128)(2,1)S(1)}, bf16[128,256]{1,0:T(8,128)(2,1)S(1)}, u32[]{:S(2)}, u32[]{:S(2)}) collective-permute-start(bf16[128,256]{1,0:T(8,128)(2,1)S(1)} %collective-permute-done.1.refs_2_), channel_id=1, source_target_pairs={{0,4},{4,0},{8,12},{12,8},{16,20},{20,16},{24,28},{28,24},{1,5},{5... | collective-permute-start | bytes 196616 | tf_op jit(solution)/shard_map/ppermute | solution.py:316
  13.3 0.0 collective-permute-done.2.refs_3_
  13.3 1.5 %collective-permute-start.6 = (bf16[128,256]{1,0:T(8,128)(2,1)S(1)}, bf16[128,256]{1,0:T(8,128)(2,1)S(1)}, u32[]{:S(2)}, u32[]{:S(2)}) collective-permute-start(bf16[128,256]{1,0:T(8,128)(2,1)S(1)} %collective-permute-done.2.refs_3_), channel_id=1, source_target_pairs={{0,4},{4,0},{8,12},{12,8},{16,20},{20,16},{24,28},{28,24},{1,5},{5... | collective-permute-start | bytes 196616 | tf_op jit(solution)/shard_map/ppermute | solution.py:316
  14.8 0.0 copy-done.4
  14.8 1.0 %shard_map.148.own = f32[8,128,256]{2,1,0:T(8,128)S(1)} custom-call(f32[16,128,256]{2,1,0:T(8,128)S(1)} %shard_map.147.filt, bf16[256,256]{1,0:T(8,128)(2,1)S(1)} %copy-done.4, bf16[128,256]{1,0:T(8,128)(2,1)S(1)} %get-tuple-element.35.refs_0_, bf16[128,256]{1,0:T(8,128)(2,1)S(1)} %collective-permute-done.refs_1_, ...), custom_call_target="tpu_custom_call" | custom-call | flops 1000000000 | tf_op jit(solution)/shard_map/pallas_call | solution.py:307
  15.8 0.0 copy-start.1
  15.8 0.0 copy-start.2
  15.8 0.0 copy-start.3
  15.8 0.0 collective-permute-done.3.refs_0_
  15.8 0.3 collective-permute-done.4.refs_1_
  16.2 0.7 %collective-permute-done.5.refs_2_ = bf16[128,256]{1,0:T(8,128)(2,1)S(1)} collective-permute-done((bf16[128,256]{1,0:T(8,128)(2,1)S(1)}, bf16[128,256]{1,0:T(8,128)(2,1)S(1)}, u32[]{:S(2)}, u32[]{:S(2)}) %collective-permute-start.5) | collective-permute-done | bytes 65568 | tf_op jit(solution)/shard_map/ppermute | solution.py:316
  16.9 0.7 %collective-permute-done.6.refs_3_ = bf16[128,256]{1,0:T(8,128)(2,1)S(1)} collective-permute-done((bf16[128,256]{1,0:T(8,128)(2,1)S(1)}, bf16[128,256]{1,0:T(8,128)(2,1)S(1)}, u32[]{:S(2)}, u32[]{:S(2)}) %collective-permute-start.6) | collective-permute-done | bytes 65568 | tf_op jit(solution)/shard_map/ppermute | solution.py:316
  17.6 1.6 %shard_map.149 = (bf16[128,256]{1,0:T(8,128)(2,1)S(1)}, bf16[128,256]{1,0:T(8,128)(2,1)S(1)}, bf16[128,256]{1,0:T(8,128)(2,1)S(1)}, bf16[128,256]{1,0:T(8,128)(2,1)S(1)}) custom-call(f32[16,128,256]{2,1,0:T(8,128)S(1)} %shard_map.147.filt, bf16[256,256]{1,0:T(8,128)(2,1)S(1)} %copy-done.4, bf16[256,256]{1,0:T(8,128)(2,1)S(1)} %copy-done.5, ...), custom_call_target="tpu_custom_call" | custom-call | flops 3000000000 | tf_op jit(solution)/shard_map/pallas_call | solution.py:307
  19.2 1.3 %collective-permute-start.7 = (bf16[128,256]{1,0:T(8,128)(2,1)S(1)}, bf16[128,256]{1,0:T(8,128)(2,1)S(1)}, u32[]{:S(2)}, u32[]{:S(2)}) collective-permute-start(bf16[128,256]{1,0:T(8,128)(2,1)S(1)} %get-tuple-element.40), channel_id=1, source_target_pairs={{0,8},{4,12},{8,0},{12,4},{16,24},{20,28},{24,16},{28,20},{1,9},{5... | collective-permute-start | bytes 196616 | tf_op jit(solution)/shard_map/ppermute | solution.py:316
  20.5 3.3 %collective-permute-start.8 = (bf16[128,256]{1,0:T(8,128)(2,1)S(1)}, bf16[128,256]{1,0:T(8,128)(2,1)S(1)}, u32[]{:S(2)}, u32[]{:S(2)}) collective-permute-start(bf16[128,256]{1,0:T(8,128)(2,1)S(1)} %get-tuple-element.41), channel_id=1, source_target_pairs={{0,16},{4,20},{8,24},{12,28},{16,0},{20,4},{24,8},{28,12},{1,17},{... | collective-permute-start | bytes 196616 | tf_op jit(solution)/shard_map/ppermute | solution.py:316
  23.7 0.0 collective-permute-start.9
  23.7 0.1 collective-permute-done.7.refs_1_
  23.9 3.5 %collective-permute-done.8.refs_2_ = bf16[128,256]{1,0:T(8,128)(2,1)S(1)} collective-permute-done((bf16[128,256]{1,0:T(8,128)(2,1)S(1)}, bf16[128,256]{1,0:T(8,128)(2,1)S(1)}, u32[]{:S(2)}, u32[]{:S(2)}) %collective-permute-start.8) | collective-permute-done | bytes 65568 | tf_op jit(solution)/shard_map/ppermute | solution.py:316
  27.4 2.4 %collective-permute-done.9.refs_3_ = bf16[128,256]{1,0:T(8,128)(2,1)S(1)} collective-permute-done((bf16[128,256]{1,0:T(8,128)(2,1)S(1)}, bf16[128,256]{1,0:T(8,128)(2,1)S(1)}, u32[]{:S(2)}, u32[]{:S(2)}) %collective-permute-start.9) | collective-permute-done | bytes 65568 | tf_op jit(solution)/shard_map/ppermute | solution.py:316
  29.8 0.0 copy-done.3
  29.8 0.2 shard_map.150
  30.0 0.1 collective-permute-start.10
  30.1 1.3 %collective-permute-done.10.other = bf16[128,512]{1,0:T(8,128)(2,1)S(1)} collective-permute-done((bf16[128,512]{1,0:T(8,128)(2,1)S(1)}, bf16[128,512]{1,0:T(8,128)(2,1)S(1)}, u32[]{:S(2)}, u32[]{:S(2)}) %collective-permute-start.10) | collective-permute-done | bytes 131104 | tf_op jit(solution)/shard_map/ppermute | solution.py:316
  31.4 0.0 collective-permute-done.11.other_w
  31.4 0.5 %shard_map.151 = (f32[128,512]{1,0:T(8,128)S(1)}, f32[128,512]{1,0:T(8,128)S(1)}) custom-call(bf16[128,512]{1,0:T(8,128)(2,1)S(1)} %get-tuple-element.43.own, bf16[128,512]{1,0:T(8,128)(2,1)S(1)} %collective-permute-done.10.other, bf16[512,2048]{1,0:T(8,128)(2,1)S(1)} %copy-done, bf16[512,2048]{1,0:T(8,128)(2,1)S(1)} %collective-permute-done.11.other_w), custom_call_target="tpu_custom_call" | custom-call | flops 500000000 | tf_op jit(solution)/shard_map/pallas_call | solution.py:307
  31.9 0.2 collective-permute-start.12
  32.1 0.3 shard_map.153
  32.4 1.6 %collective-permute-start.14 = (bf16[128,512]{1,0:T(8,128)(2,1)S(1)}, bf16[128,512]{1,0:T(8,128)(2,1)S(1)}, u32[]{:S(2)}, u32[]{:S(2)}) collective-permute-start(bf16[128,512]{1,0:T(8,128)(2,1)S(1)} %shard_map.153), channel_id=1, source_target_pairs={{0,2},{1,3},{2,0},{3,1},{4,6},{5,7},{6,4},{7,5},{8,10},{9,11},{10,... | collective-permute-start | bytes 393224 | tf_op jit(solution)/shard_map/ppermute | solution.py:316
  34.0 0.3 shard_map.152
  34.3 0.3 collective-permute-start.13
  34.6 4.3 %collective-permute-done.14.second = bf16[128,512]{1,0:T(8,128)(2,1)S(1)} collective-permute-done((bf16[128,512]{1,0:T(8,128)(2,1)S(1)}, bf16[128,512]{1,0:T(8,128)(2,1)S(1)}, u32[]{:S(2)}, u32[]{:S(2)}) %collective-permute-start.14) | collective-permute-done | bytes 131104 | tf_op jit(solution)/shard_map/ppermute | solution.py:316
  38.9 0.7 %shard_map.154.refs_0_ = bf16[256,512]{1,0:T(8,128)(2,1)} custom-call(f32[128,512]{1,0:T(8,128)S(1)} %get-tuple-element.46.first, bf16[128,512]{1,0:T(8,128)(2,1)S(1)} %collective-permute-done.14.second), custom_call_target="tpu_custom_call" | custom-call | flops 100000000 | tf_op jit(solution)/shard_map/pallas_call | solution.py:273
  39.6 0.9 %collective-permute-done.13.second = bf16[128,512]{1,0:T(8,128)(2,1)S(1)} collective-permute-done((bf16[128,512]{1,0:T(8,128)(2,1)S(1)}, bf16[128,512]{1,0:T(8,128)(2,1)S(1)}, u32[]{:S(2)}, u32[]{:S(2)}) %collective-permute-start.13) | collective-permute-done | bytes 131104 | tf_op jit(solution)/shard_map/ppermute | solution.py:316
  40.5 0.0 collective-permute-done.12.first
  40.5 0.7 %shard_map.155 = bf16[256,512]{1,0:T(8,128)(2,1)} custom-call(f32[128,512]{1,0:T(8,128)S(1)} %collective-permute-done.12.first, bf16[128,512]{1,0:T(8,128)(2,1)S(1)} %collective-permute-done.13.second, bf16[256,512]{1,0:T(8,128)(2,1)} %shard_map.154.refs_0_), custom_call_target="tpu_custom_call", output_to_operand_aliasing={{}: (2, {})} | custom-call | flops 100000000 | tf_op jit(solution)/shard_map/pallas_call | solution.py:273
  (5 shorter events, 0.0 us)
Async XLA Ops:
  0.0 31.4 %collective-permute-start.11 = (bf16[512,2048]{1,0:T(8,128)(2,1)}, bf16[512,2048]{1,0:T(8,128)(2,1)S(1)}, u32[]{:S(2)}, u32[]{:S(2)}) collective-permute-start(bf16[512,2048]{1,0:T(8,128)(2,1)} %own_w.5), channel_id=1, source_target_pairs={{0,1},{1,0},{2,3},{3,2},{4,5},{5,4},{6,7},{7,6},{8,9},{9,8},{10,11... | collective-permute-start | bytes 6291464 | tf_op jit(solution)/shard_map/ppermute | solution.py:316
  2.0 9.2 %collective-permute-start = (bf16[128,256]{1,0:T(8,128)(2,1)S(1)}, bf16[128,256]{1,0:T(8,128)(2,1)S(1)}, u32[]{:S(2)}, u32[]{:S(2)}) collective-permute-start(bf16[128,256]{1,0:T(8,128)(2,1)S(1)} %get-tuple-element.36), channel_id=1, source_target_pairs={{0,8},{4,12},{8,0},{12,4},{16,24},{20,28},{24,16},{28,20},{1,9},{5... | collective-permute-start | bytes 196616 | tf_op jit(solution)/shard_map/ppermute | solution.py:316
  4.6 7.0 %collective-permute-start.1 = (bf16[128,256]{1,0:T(8,128)(2,1)S(1)}, bf16[128,256]{1,0:T(8,128)(2,1)S(1)}, u32[]{:S(2)}, u32[]{:S(2)}) collective-permute-start(bf16[128,256]{1,0:T(8,128)(2,1)S(1)} %get-tuple-element.37), channel_id=1, source_target_pairs={{0,16},{4,20},{8,24},{12,28},{16,0},{20,4},{24,8},{28,12},{1,17},{... | collective-permute-start | bytes 196616 | tf_op jit(solution)/shard_map/ppermute | solution.py:316
  7.2 6.1 %collective-permute-start.2 = (bf16[128,256]{1,0:T(8,128)(2,1)S(1)}, bf16[128,256]{1,0:T(8,128)(2,1)S(1)}, u32[]{:S(2)}, u32[]{:S(2)}) collective-permute-start(bf16[128,256]{1,0:T(8,128)(2,1)S(1)} %get-tuple-element.38), channel_id=1, source_target_pairs={{0,24},{4,28},{8,16},{12,20},{16,8},{20,12},{24,0},{28,4},{1,25},{... | collective-permute-start | bytes 196616 | tf_op jit(solution)/shard_map/ppermute | solution.py:316
  7.2 8.6 %collective-permute-start.3 = (bf16[128,256]{1,0:T(8,128)(2,1)S(1)}, bf16[128,256]{1,0:T(8,128)(2,1)S(1)}, u32[]{:S(2)}, u32[]{:S(2)}) collective-permute-start(bf16[128,256]{1,0:T(8,128)(2,1)S(1)} %get-tuple-element.35.refs_0_), channel_id=1, source_target_pairs={{0,4},{4,0},{8,12},{12,8},{16,20},{20,16},{24,28},{28,24},{1,5},{5... | collective-permute-start | bytes 196616 | tf_op jit(solution)/shard_map/ppermute | solution.py:316
  10.2 4.6 %copy-start.4 = (bf16[256,256]{1,0:T(8,128)(2,1)S(1)}, bf16[256,256]{1,0:T(8,128)(2,1)}, u32[]{:S(2)}) copy-start(bf16[256,256]{1,0:T(8,128)(2,1)} %constant.13.clone.table) | copy-start | bytes 393220
  11.1 6.4 %copy-start.5 = (bf16[256,256]{1,0:T(8,128)(2,1)S(1)}, bf16[256,256]{1,0:T(8,128)(2,1)}, u32[]{:S(2)}) copy-start(bf16[256,256]{1,0:T(8,128)(2,1)} %constant.14.clone.back) | copy-start | bytes 393220
  11.2 5.0 %collective-permute-start.4 = (bf16[128,256]{1,0:T(8,128)(2,1)S(1)}, bf16[128,256]{1,0:T(8,128)(2,1)S(1)}, u32[]{:S(2)}, u32[]{:S(2)}) collective-permute-start(bf16[128,256]{1,0:T(8,128)(2,1)S(1)} %collective-permute-done.refs_1_), channel_id=1, source_target_pairs={{0,4},{4,0},{8,12},{12,8},{16,20},{20,16},{24,28},{28,24},{1,5},{5... | collective-permute-start | bytes 196616 | tf_op jit(solution)/shard_map/ppermute | solution.py:316
  11.6 5.3 %collective-permute-start.5 = (bf16[128,256]{1,0:T(8,128)(2,1)S(1)}, bf16[128,256]{1,0:T(8,128)(2,1)S(1)}, u32[]{:S(2)}, u32[]{:S(2)}) collective-permute-start(bf16[128,256]{1,0:T(8,128)(2,1)S(1)} %collective-permute-done.1.refs_2_), channel_id=1, source_target_pairs={{0,4},{4,0},{8,12},{12,8},{16,20},{20,16},{24,28},{28,24},{1,5},{5... | collective-permute-start | bytes 196616 | tf_op jit(solution)/shard_map/ppermute | solution.py:316
  13.3 4.3 %collective-permute-start.6 = (bf16[128,256]{1,0:T(8,128)(2,1)S(1)}, bf16[128,256]{1,0:T(8,128)(2,1)S(1)}, u32[]{:S(2)}, u32[]{:S(2)}) collective-permute-start(bf16[128,256]{1,0:T(8,128)(2,1)S(1)} %collective-permute-done.2.refs_3_), channel_id=1, source_target_pairs={{0,4},{4,0},{8,12},{12,8},{16,20},{20,16},{24,28},{28,24},{1,5},{5... | collective-permute-start | bytes 196616 | tf_op jit(solution)/shard_map/ppermute | solution.py:316
  15.8 14.0 %copy-start.1 = (bf16[256,512]{1,0:T(8,128)(2,1)S(1)}, bf16[256,512]{1,0:T(8,128)(2,1)}, u32[]{:S(2)}) copy-start(bf16[256,512]{1,0:T(8,128)(2,1)} %signal.3) | copy-start | bytes 786436
  15.8 14.0 %copy-start.2 = (bf16[256,512]{1,0:T(8,128)(2,1)S(1)}, bf16[256,512]{1,0:T(8,128)(2,1)}, u32[]{:S(2)}) copy-start(bf16[256,512]{1,0:T(8,128)(2,1)} %gate.1) | copy-start | bytes 786436
  15.8 14.0 %copy-start.3 = (f32[512]{0:T(512)S(1)}, f32[512]{0:T(512)}, u32[]{:S(2)}) copy-start(f32[512]{0:T(512)} %param.17) | copy-start | bytes 6148
  17.6 13.8 %copy-start = (bf16[512,2048]{1,0:T(8,128)(2,1)S(1)}, bf16[512,2048]{1,0:T(8,128)(2,1)}, u32[]{:S(2)}) copy-start(bf16[512,2048]{1,0:T(8,128)(2,1)} %own_w.5) | copy-start | bytes 6291460
  19.2 4.7 %collective-permute-start.7 = (bf16[128,256]{1,0:T(8,128)(2,1)S(1)}, bf16[128,256]{1,0:T(8,128)(2,1)S(1)}, u32[]{:S(2)}, u32[]{:S(2)}) collective-permute-start(bf16[128,256]{1,0:T(8,128)(2,1)S(1)} %get-tuple-element.40), channel_id=1, source_target_pairs={{0,8},{4,12},{8,0},{12,4},{16,24},{20,28},{24,16},{28,20},{1,9},{5... | collective-permute-start | bytes 196616 | tf_op jit(solution)/shard_map/ppermute | solution.py:316
  20.5 6.9 %collective-permute-start.8 = (bf16[128,256]{1,0:T(8,128)(2,1)S(1)}, bf16[128,256]{1,0:T(8,128)(2,1)S(1)}, u32[]{:S(2)}, u32[]{:S(2)}) collective-permute-start(bf16[128,256]{1,0:T(8,128)(2,1)S(1)} %get-tuple-element.41), channel_id=1, source_target_pairs={{0,16},{4,20},{8,24},{12,28},{16,0},{20,4},{24,8},{28,12},{1,17},{... | collective-permute-start | bytes 196616 | tf_op jit(solution)/shard_map/ppermute | solution.py:316
  23.7 6.1 %collective-permute-start.9 = (bf16[128,256]{1,0:T(8,128)(2,1)S(1)}, bf16[128,256]{1,0:T(8,128)(2,1)S(1)}, u32[]{:S(2)}, u32[]{:S(2)}) collective-permute-start(bf16[128,256]{1,0:T(8,128)(2,1)S(1)} %get-tuple-element.42), channel_id=1, source_target_pairs={{0,24},{4,28},{8,16},{12,20},{16,8},{20,12},{24,0},{28,4},{1,25},{... | collective-permute-start | bytes 196616 | tf_op jit(solution)/shard_map/ppermute | solution.py:316
  30.0 1.4 %collective-permute-start.10 = (bf16[128,512]{1,0:T(8,128)(2,1)S(1)}, bf16[128,512]{1,0:T(8,128)(2,1)S(1)}, u32[]{:S(2)}, u32[]{:S(2)}) collective-permute-start(bf16[128,512]{1,0:T(8,128)(2,1)S(1)} %get-tuple-element.44), channel_id=1, source_target_pairs={{0,1},{1,0},{2,3},{3,2},{4,5},{5,4},{6,7},{7,6},{8,9},{9,8},{10,11... | collective-permute-start | bytes 393224 | tf_op jit(solution)/shard_map/ppermute | solution.py:316
  31.9 8.6 %collective-permute-start.12 = (f32[128,512]{1,0:T(8,128)S(1)}, f32[128,512]{1,0:T(8,128)S(1)}, u32[]{:S(2)}, u32[]{:S(2)}) collective-permute-start(f32[128,512]{1,0:T(8,128)S(1)} %get-tuple-element.45), channel_id=1, source_target_pairs={{0,1},{1,0},{2,3},{3,2},{4,5},{5,4},{6,7},{7,6},{8,9},{9,8},{10,11... | collective-permute-start | bytes 786440 | tf_op jit(solution)/shard_map/ppermute | solution.py:316
  32.4 6.4 %collective-permute-start.14 = (bf16[128,512]{1,0:T(8,128)(2,1)S(1)}, bf16[128,512]{1,0:T(8,128)(2,1)S(1)}, u32[]{:S(2)}, u32[]{:S(2)}) collective-permute-start(bf16[128,512]{1,0:T(8,128)(2,1)S(1)} %shard_map.153), channel_id=1, source_target_pairs={{0,2},{1,3},{2,0},{3,1},{4,6},{5,7},{6,4},{7,5},{8,10},{9,11},{10,... | collective-permute-start | bytes 393224 | tf_op jit(solution)/shard_map/ppermute | solution.py:316
  34.3 6.2 %collective-permute-start.13 = (bf16[128,512]{1,0:T(8,128)(2,1)S(1)}, bf16[128,512]{1,0:T(8,128)(2,1)S(1)}, u32[]{:S(2)}, u32[]{:S(2)}) collective-permute-start(bf16[128,512]{1,0:T(8,128)(2,1)S(1)} %shard_map.152), channel_id=1, source_target_pairs={{0,3},{1,2},{2,1},{3,0},{4,7},{5,6},{6,5},{7,4},{8,11},{9,10},{10,... | collective-permute-start | bytes 393224 | tf_op jit(solution)/shard_map/ppermute | solution.py:316

commit v6 on v5

--- a/solution.py
+++ b/solution.py
@@ -26,8 +26,7 @@
     angles = 2.0 * np.pi * ((taps[None, :] * bands[:, None]) % K) / K
     features = np.concatenate([taps[None, :] / K, np.cos(angles), np.sin(angles)], 0)
     features = np.pad(features, ((0, -len(features) % TILE), (0, 0)))
-    high, low = split(features)
-    return np.concatenate([high, low, high], 0)
+    return np.concatenate(split(features), 0)
 
 
 def split(table):
@@ -64,19 +63,16 @@
     return jnp.dot(a, b, preferred_element_type=F32)
 
 
-def sine(x):
-    turns = jnp.round(x * (1.0 / math.pi))
-    r = x - turns * 3.140625
-    r = r - turns * 9.676535897932e-4
-    odd = turns - 2.0 * jnp.floor(turns * 0.5)
-    sign = 1.0 - 2.0 * odd
+SINE = (6.283182621, -41.34142303, 81.59618378, -76.58010101, 41.20539856, -12.27126789)
+
+
+def sine(turns):
+    r = turns - jnp.round(turns)
     s = r * r
-    p = -2.5052108385e-8
-    p = p * s + 2.7557319224e-6
-    p = p * s - 1.9841269841e-4
-    p = p * s + 8.3333333333e-3
-    p = p * s - 1.6666666667e-1
-    return sign * (r + r * (s * p))
+    p = SINE[-1] * s + SINE[-2]
+    for value in SINE[-3::-1]:
+        p = p * s + value
+    return p * r
 
 
 def column(row):
@@ -116,15 +112,16 @@
 
 
 def hidden_kernel(feat, w_first, bias, freq, w_mid, out, left):
-    freqs = column(freq[...])
+    turns = column(freq[...] * (0.5 / math.pi))
     high, low = parts_of(w_first[...])
     count = high.shape[0]
     rows = left.shape[0] // 3
     left[...] = jnp.zeros(left.shape, BF16)
     for n, part in enumerate((high, high, low)):
         left[n * rows : n * rows + count, :] = part
-    first = sine(freqs * (dot_first(left[...], feat[...]) + column(bias[...])))
-    second = sine(freqs * dot_first(stack_left(w_mid[...]), stack_right(first)))
+    features = jnp.concatenate([feat[...], feat[:rows]], 0)
+    first = sine(turns * (dot_first(left[...], features) + column(bias[...])))
+    second = sine(turns * dot_first(stack_left(w_mid[...]), stack_right(first)))
     out[...] = stack_right(second)
 
 
@@ -237,13 +234,21 @@
     send_out[...] = jnp.where(core == 0, high, low)
 
 
-def project_kernel(flips, own, other, own_w, other_w, *outs):
+def project_kernel(flips, own, weights, *outs):
     head = lax.axis_index("head")
     width = outs[0].shape[1]
     for flip, out in zip(flips, outs):
         columns = pl.ds(pl.multiple_of(lax.bitwise_xor(head, flip) * width, width), width)
-        terms = dot(own[...], own_w[:, columns]) + dot(other[...], other_w[:, columns])
-        out[...] = terms.astype(out.dtype)
+        out[...] = dot(own[...], weights[:, columns])
+
+
+def add_kernel(flips, other, weights, *refs):
+    sums, outs = refs[: len(flips)], refs[len(flips) :]
+    head = lax.axis_index("head")
+    width = outs[0].shape[1]
+    for flip, total, out in zip(flips, sums, outs):
+        columns = pl.ds(pl.multiple_of(lax.bitwise_xor(head, flip) * width, width), width)
+        out[...] = (total[...] + dot(other[...], weights[:, columns])).astype(out.dtype)
 
 
 def sum_kernel(other_half, first, second, *refs):
@@ -339,8 +344,6 @@
         w_mid,
         w_last,
         row(rate),
-        jnp.asarray(forward_high),
-        jnp.asarray(forward_low),
     )
     piece = shape((share, length_local))
     turned = call(
@@ -362,10 +365,18 @@
         hidden_kernel,
         shape((3 * w_mid.shape[1], K)),
         *operands[:5],
-        scratch=[pltpu.VMEM((operands[0].shape[0], w_first.shape[1]), BF16)],
+        scratch=[pltpu.VMEM((operands[0].shape[0] // 2 * 3, w_first.shape[1]), BF16)],
         flops=1_000_000_000,
     )
-    filt = call(filter_kernel, shape((taps, share, 2 * BLOCK), F32), hidden, *operands[5:], flops=2_000_000_000)
+    filt = call(
+        filter_kernel,
+        shape((taps, share, 2 * BLOCK), F32),
+        hidden,
+        *operands[5:],
+        forward_high,
+        forward_low,
+        flops=2_000_000_000,
+    )
     other_w = flip(out_w, "head", 1)
     sums = shape((blocks // 2, share, 2 * BLOCK), F32)
     early = call(
@@ -406,17 +417,25 @@
         flops=500_000_000,
     )
     received = flip(send, "head", 1)
-    terms, wide = shape((half, width)), shape((half, width), F32)
-    factors = (keep, received, out_w, other_w)
-
-    def project(flips, outs):
-        return call(functools.partial(project_kernel, flips), outs, *factors, flops=500_000_000)
-
-    (a,) = project((2,), (terms,))
+    wide = shape((half, width), F32)
+    flips = (2, 3, 1, 0)
+    sums = call(functools.partial(project_kernel, flips), (wide,) * 4, keep, out_w, flops=500_000_000)
+
+    def project(which, dtype):
+        return call(
+            functools.partial(add_kernel, [flips[n] for n in which]),
+            (shape((half, width), dtype),) * len(which),
+            received,
+            other_w,
+            *(sums[n] for n in which),
+            flops=500_000_000,
+        )
+
+    (a,) = project((0,), BF16)
     a = flip(a, "head", 2)
-    (b,) = project((3,), (terms,))
+    (b,) = project((1,), BF16)
     b = flip(b, "head", 3)
-    c, here = project((1, 0), (wide, wide))
+    c, here = project((2, 3), F32)
     c = flip(c, "head", 1)
     out = add_half(0, shape((length_local, width)), here, a)
     return add_half(1, out, c, b)

time: 41.3 us -> 40.9 us (level)
    pallas_call x9 -> x10, Pallas kernels: 7.49 us -> 7.13 us  [call(): return run(*args)]
  transfers between devices with their start and end apart: 15 -> 15, of which waited for: 10 -> 9; matrix products, arithmetic and copies ran while one was open for 0% -> 0% of each run, Pallas kernels for 19% -> 18%
where the time goes in v6:
time: 40.9 us; the launch traced here: 40.8 us
  starting transfers between devices  17.6 us (43%)
  waiting for transfers between devices  14.4 us (35%)
  Pallas kernels  8.51 us (21%)
    ppermute x15, starting transfers between devices, flip(): return lax.ppermute(x, axis, [(i, i ^ by) for i in range(size)])  17.6 us
    ppermute x15, waiting for transfers between devices, flip(): return lax.ppermute(x, axis, [(i, i ^ by) for i in range(size)])  14.4 us
    pallas_call x10, Pallas kernels, call(): return run(*args)  7.13 us
    pallas_call x2, Pallas kernels, add_half(): return run(first, second) if fresh else run(first, second, out)  1.38 us
  transfers between devices with their start and end apart: 15, of which 9 were waited for; matrix products, arithmetic and copies ran while one was open for 0% of the time, Pallas kernels for 18%

profile of v6, /device:TPU:0, one launch (start us, length us, event | category | flops | bytes accessed | tf_op | source)
XLA Modules:
  0.0 40.8 jit_solution(2151061613177194734)
XLA Ops:
  0.0 0.5 %collective-permute-start.11 = (bf16[512,2048]{1,0:T(8,128)(2,1)}, bf16[512,2048]{1,0:T(8,128)(2,1)S(1)}, u32[]{:S(2)}, u32[]{:S(2)}) collective-permute-start(bf16[512,2048]{1,0:T(8,128)(2,1)} %weights.1), channel_id=1, source_target_pairs={{0,1},{1,0},{2,3},{3,2},{4,5},{5,4},{6,7},{7,6},{8,9},{9,8},{10,11... | collective-permute-start | bytes 6291464 | tf_op jit(solution)/shard_map/ppermute | solution.py:321
  0.5 1.3 %shard_map.145 = (bf16[128,256]{1,0:T(8,128)(2,1)S(1)}, bf16[128,256]{1,0:T(8,128)(2,1)S(1)}, bf16[128,256]{1,0:T(8,128)(2,1)S(1)}, bf16[128,256]{1,0:T(8,128)(2...) custom-call(bf16[256,512]{1,0:T(8,128)(2,1)} %signal.3, ...), custom_call_target="tpu_custom_call" | custom-call | tf_op jit(solution)/shard_map/pallas_call | solution.py:312
  1.8 2.7 %collective-permute-start = (bf16[128,256]{1,0:T(8,128)(2,1)S(1)}, bf16[128,256]{1,0:T(8,128)(2,1)S(1)}, u32[]{:S(2)}, u32[]{:S(2)}) collective-permute-start(bf16[128,256]{1,0:T(8,128)(2,1)S(1)} %get-tuple-element.36), channel_id=1, source_target_pairs={{0,8},{4,12},{8,0},{12,4},{16,24},{20,28},{24,16},{28,20},{1,9},{5... | collective-permute-start | bytes 196616 | tf_op jit(solution)/shard_map/ppermute | solution.py:321
  4.5 2.6 %collective-permute-start.1 = (bf16[128,256]{1,0:T(8,128)(2,1)S(1)}, bf16[128,256]{1,0:T(8,128)(2,1)S(1)}, u32[]{:S(2)}, u32[]{:S(2)}) collective-permute-start(bf16[128,256]{1,0:T(8,128)(2,1)S(1)} %get-tuple-element.37), channel_id=1, source_target_pairs={{0,16},{4,20},{8,24},{12,28},{16,0},{20,4},{24,8},{28,12},{1,17},{... | collective-permute-start | bytes 196616 | tf_op jit(solution)/shard_map/ppermute | solution.py:321
  7.1 0.0 collective-permute-start.2
  7.1 1.7 %collective-permute-start.3 = (bf16[128,256]{1,0:T(8,128)(2,1)S(1)}, bf16[128,256]{1,0:T(8,128)(2,1)S(1)}, u32[]{:S(2)}, u32[]{:S(2)}) collective-permute-start(bf16[128,256]{1,0:T(8,128)(2,1)S(1)} %get-tuple-element.35.refs_0_), channel_id=1, source_target_pairs={{0,4},{4,0},{8,12},{12,8},{16,20},{20,16},{24,28},{28,24},{1,5},{5... | collective-permute-start | bytes 196616 | tf_op jit(solution)/shard_map/ppermute | solution.py:321
  8.8 0.9 %shard_map.146.hidden = bf16[192,2048]{1,0:T(8,128)(2,1)S(1)} custom-call(bf16[96,2048]{1,0:T(8,128)(2,1)S(1)} %get-tuple-element.28.feat, f32[33,64]{1,0:T(8,128)S(1)} %get-tuple-element.29.w_first, f32[1,64]{1,0:T(1,128)S(1)} %get-tuple-element.30.bias, f32[1,64]{1,0:T(1,128)S(1)} %get-tuple-element.31.freq, f32[64,64]{1,0:T(8,128)S(1)} %get-tuple-element.32.w_mid), custom_call_target="tpu_custom_call" | custom-call | flops 1000000000 | tf_op jit(solution)/shard_map/pallas_call | solution.py:312
  9.8 0.0 copy-start.4
  9.8 0.9 %shard_map.147.filt = f32[16,128,256]{2,1,0:T(8,128)S(1)} custom-call(bf16[192,2048]{1,0:T(8,128)(2,1)S(1)} %shard_map.146.hidden, f32[64,512]{1,0:T(8,128)S(1)} %get-tuple-element.33.w_last, f32[1,512]{1,0:T(1,128)S(1)} %get-tuple-element.34.rate, bf16[256,256]{1,0:T(8,128)(2,1)S(1)} %copy-done.7, bf16[256,256]{1,0:T(8,128)(2,1)S(1)} %copy-done.6), custom_call_target="tpu_custom_call" | custom-call | flops 2000000000 | tf_op jit(solution)/shard_map/pallas_call | solution.py:312
  10.7 0.0 copy-start.5
  10.7 0.0 collective-permute-done.refs_1_
  10.7 0.4 collective-permute-start.4
  11.1 0.4 %collective-permute-done.1.refs_2_ = bf16[128,256]{1,0:T(8,128)(2,1)S(1)} collective-permute-done((bf16[128,256]{1,0:T(8,128)(2,1)S(1)}, bf16[128,256]{1,0:T(8,128)(2,1)S(1)}, u32[]{:S(2)}, u32[]{:S(2)}) %collective-permute-start.1) | collective-permute-done | bytes 65568 | tf_op jit(solution)/shard_map/ppermute | solution.py:321
  11.5 1.5 %collective-permute-start.5 = (bf16[128,256]{1,0:T(8,128)(2,1)S(1)}, bf16[128,256]{1,0:T(8,128)(2,1)S(1)}, u32[]{:S(2)}, u32[]{:S(2)}) collective-permute-start(bf16[128,256]{1,0:T(8,128)(2,1)S(1)} %collective-permute-done.1.refs_2_), channel_id=1, source_target_pairs={{0,4},{4,0},{8,12},{12,8},{16,20},{20,16},{24,28},{28,24},{1,5},{5... | collective-permute-start | bytes 196616 | tf_op jit(solution)/shard_map/ppermute | solution.py:321
  13.0 0.1 collective-permute-done.2.refs_3_
  13.2 1.5 %collective-permute-start.6 = (bf16[128,256]{1,0:T(8,128)(2,1)S(1)}, bf16[128,256]{1,0:T(8,128)(2,1)S(1)}, u32[]{:S(2)}, u32[]{:S(2)}) collective-permute-start(bf16[128,256]{1,0:T(8,128)(2,1)S(1)} %collective-permute-done.2.refs_3_), channel_id=1, source_target_pairs={{0,4},{4,0},{8,12},{12,8},{16,20},{20,16},{24,28},{28,24},{1,5},{5... | collective-permute-start | bytes 196616 | tf_op jit(solution)/shard_map/ppermute | solution.py:321
  14.7 1.0 %shard_map.148.own = f32[8,128,256]{2,1,0:T(8,128)S(1)} custom-call(f32[16,128,256]{2,1,0:T(8,128)S(1)} %shard_map.147.filt, bf16[256,256]{1,0:T(8,128)(2,1)S(1)} %copy-done.4, bf16[128,256]{1,0:T(8,128)(2,1)S(1)} %get-tuple-element.35.refs_0_, bf16[128,256]{1,0:T(8,128)(2,1)S(1)} %collective-permute-done.refs_1_, ...), custom_call_target="tpu_custom_call" | custom-call | flops 1000000000 | tf_op jit(solution)/shard_map/pallas_call | solution.py:312
  15.7 0.0 copy-start.1
  15.7 0.0 copy-start.2
  15.7 0.0 copy-start.3
  15.7 0.0 collective-permute-done.3.refs_0_
  15.7 0.0 collective-permute-done.4.refs_1_
  15.7 0.7 %collective-permute-done.5.refs_2_ = bf16[128,256]{1,0:T(8,128)(2,1)S(1)} collective-permute-done((bf16[128,256]{1,0:T(8,128)(2,1)S(1)}, bf16[128,256]{1,0:T(8,128)(2,1)S(1)}, u32[]{:S(2)}, u32[]{:S(2)}) %collective-permute-start.5) | collective-permute-done | bytes 65568 | tf_op jit(solution)/shard_map/ppermute | solution.py:321
  16.5 1.0 %collective-permute-done.6.refs_3_ = bf16[128,256]{1,0:T(8,128)(2,1)S(1)} collective-permute-done((bf16[128,256]{1,0:T(8,128)(2,1)S(1)}, bf16[128,256]{1,0:T(8,128)(2,1)S(1)}, u32[]{:S(2)}, u32[]{:S(2)}) %collective-permute-start.6) | collective-permute-done | bytes 65568 | tf_op jit(solution)/shard_map/ppermute | solution.py:321
  17.4 0.0 copy-done.5
  17.4 1.6 %shard_map.149 = (bf16[128,256]{1,0:T(8,128)(2,1)S(1)}, bf16[128,256]{1,0:T(8,128)(2,1)S(1)}, bf16[128,256]{1,0:T(8,128)(2,1)S(1)}, bf16[128,256]{1,0:T(8,128)(2,1)S(1)}) custom-call(f32[16,128,256]{2,1,0:T(8,128)S(1)} %shard_map.147.filt, bf16[256,256]{1,0:T(8,128)(2,1)S(1)} %copy-done.4, bf16[256,256]{1,0:T(8,128)(2,1)S(1)} %copy-done.5, ...), custom_call_target="tpu_custom_call" | custom-call | flops 3000000000 | tf_op jit(solution)/shard_map/pallas_call | solution.py:312
  19.0 1.3 %collective-permute-start.7 = (bf16[128,256]{1,0:T(8,128)(2,1)S(1)}, bf16[128,256]{1,0:T(8,128)(2,1)S(1)}, u32[]{:S(2)}, u32[]{:S(2)}) collective-permute-start(bf16[128,256]{1,0:T(8,128)(2,1)S(1)} %get-tuple-element.40), channel_id=1, source_target_pairs={{0,8},{4,12},{8,0},{12,4},{16,24},{20,28},{24,16},{28,20},{1,9},{5... | collective-permute-start | bytes 196616 | tf_op jit(solution)/shard_map/ppermute | solution.py:321
  20.3 3.2 %collective-permute-start.8 = (bf16[128,256]{1,0:T(8,128)(2,1)S(1)}, bf16[128,256]{1,0:T(8,128)(2,1)S(1)}, u32[]{:S(2)}, u32[]{:S(2)}) collective-permute-start(bf16[128,256]{1,0:T(8,128)(2,1)S(1)} %get-tuple-element.41), channel_id=1, source_target_pairs={{0,16},{4,20},{8,24},{12,28},{16,0},{20,4},{24,8},{28,12},{1,17},{... | collective-permute-start | bytes 196616 | tf_op jit(solution)/shard_map/ppermute | solution.py:321
  23.6 0.0 collective-permute-start.9
  23.6 0.0 collective-permute-done.7.refs_1_
  23.6 3.6 %collective-permute-done.8.refs_2_ = bf16[128,256]{1,0:T(8,128)(2,1)S(1)} collective-permute-done((bf16[128,256]{1,0:T(8,128)(2,1)S(1)}, bf16[128,256]{1,0:T(8,128)(2,1)S(1)}, u32[]{:S(2)}, u32[]{:S(2)}) %collective-permute-start.8) | collective-permute-done | bytes 65568 | tf_op jit(solution)/shard_map/ppermute | solution.py:321
  27.2 2.4 %collective-permute-done.9.refs_3_ = bf16[128,256]{1,0:T(8,128)(2,1)S(1)} collective-permute-done((bf16[128,256]{1,0:T(8,128)(2,1)S(1)}, bf16[128,256]{1,0:T(8,128)(2,1)S(1)}, u32[]{:S(2)}, u32[]{:S(2)}) %collective-permute-start.9) | collective-permute-done | bytes 65568 | tf_op jit(solution)/shard_map/ppermute | solution.py:321
  29.7 0.2 shard_map.150
  29.9 0.1 collective-permute-start.10
  29.9 0.5 %shard_map.151 = (f32[128,512]{1,0:T(8,128)S(1)}, f32[128,512]{1,0:T(8,128)S(1)}, f32[128,512]{1,0:T(8,128)S(1)}, f32[128,512]{1,0:T(8,128)S(1)}) custom-call(bf16[128,512]{1,0:T(8,128)(2,1)S(1)} %get-tuple-element.44.own, bf16[512,2048]{1,0:T(8,128)(2,1)S(1)} %copy-done), custom_call_target="tpu_custom_call" | custom-call | flops 500000000 | tf_op jit(solution)/shard_map/pallas_call | solution.py:312
  30.4 0.9 %collective-permute-done.10.other = bf16[128,512]{1,0:T(8,128)(2,1)S(1)} collective-permute-done((bf16[128,512]{1,0:T(8,128)(2,1)S(1)}, bf16[128,512]{1,0:T(8,128)(2,1)S(1)}, u32[]{:S(2)}, u32[]{:S(2)}) %collective-permute-start.10) | collective-permute-done | bytes 131104 | tf_op jit(solution)/shard_map/ppermute | solution.py:321
  31.3 0.0 collective-permute-done.11.weights
  31.3 0.3 shard_map.152
  31.6 0.2 collective-permute-start.12
  31.8 0.2 shard_map.154
  32.0 1.6 %collective-permute-start.14 = (bf16[128,512]{1,0:T(8,128)(2,1)S(1)}, bf16[128,512]{1,0:T(8,128)(2,1)S(1)}, u32[]{:S(2)}, u32[]{:S(2)}) collective-permute-start(bf16[128,512]{1,0:T(8,128)(2,1)S(1)} %shard_map.154), channel_id=1, source_target_pairs={{0,2},{1,3},{2,0},{3,1},{4,6},{5,7},{6,4},{7,5},{8,10},{9,11},{10,... | collective-permute-start | bytes 393224 | tf_op jit(solution)/shard_map/ppermute | solution.py:321
  33.6 0.2 shard_map.153
  33.8 0.3 collective-permute-start.13
  34.1 4.4 %collective-permute-done.14.second = bf16[128,512]{1,0:T(8,128)(2,1)S(1)} collective-permute-done((bf16[128,512]{1,0:T(8,128)(2,1)S(1)}, bf16[128,512]{1,0:T(8,128)(2,1)S(1)}, u32[]{:S(2)}, u32[]{:S(2)}) %collective-permute-start.14) | collective-permute-done | bytes 131104 | tf_op jit(solution)/shard_map/ppermute | solution.py:321
  38.5 0.7 %shard_map.155.refs_0_ = bf16[256,512]{1,0:T(8,128)(2,1)} custom-call(f32[128,512]{1,0:T(8,128)S(1)} %get-tuple-element.49.first, bf16[128,512]{1,0:T(8,128)(2,1)S(1)} %collective-permute-done.14.second), custom_call_target="tpu_custom_call" | custom-call | flops 100000000 | tf_op jit(solution)/shard_map/pallas_call | solution.py:278
  39.2 0.9 %collective-permute-done.13.second = bf16[128,512]{1,0:T(8,128)(2,1)S(1)} collective-permute-done((bf16[128,512]{1,0:T(8,128)(2,1)S(1)}, bf16[128,512]{1,0:T(8,128)(2,1)S(1)}, u32[]{:S(2)}, u32[]{:S(2)}) %collective-permute-start.13) | collective-permute-done | bytes 131104 | tf_op jit(solution)/shard_map/ppermute | solution.py:321
  40.1 0.0 collective-permute-done.12.first
  40.1 0.7 %shard_map.156 = bf16[256,512]{1,0:T(8,128)(2,1)} custom-call(f32[128,512]{1,0:T(8,128)S(1)} %collective-permute-done.12.first, bf16[128,512]{1,0:T(8,128)(2,1)S(1)} %collective-permute-done.13.second, bf16[256,512]{1,0:T(8,128)(2,1)} %shard_map.155.refs_0_), custom_call_target="tpu_custom_call", output_to_operand_aliasing={{}: (2, {})} | custom-call | flops 100000000 | tf_op jit(solution)/shard_map/pallas_call | solution.py:278
  (10 shorter events, 0.0 us)
Async XLA Ops:
  0.0 31.3 %collective-permute-start.11 = (bf16[512,2048]{1,0:T(8,128)(2,1)}, bf16[512,2048]{1,0:T(8,128)(2,1)S(1)}, u32[]{:S(2)}, u32[]{:S(2)}) collective-permute-start(bf16[512,2048]{1,0:T(8,128)(2,1)} %weights.1), channel_id=1, source_target_pairs={{0,1},{1,0},{2,3},{3,2},{4,5},{5,4},{6,7},{7,6},{8,9},{9,8},{10,11... | collective-permute-start | bytes 6291464 | tf_op jit(solution)/shard_map/ppermute | solution.py:321
  0.5 9.3 %copy-start.6 = (bf16[256,256]{1,0:T(8,128)(2,1)S(1)}, bf16[256,256]{1,0:T(8,128)(2,1)}, u32[]{:S(2)}) copy-start(bf16[256,256]{1,0:T(8,128)(2,1)} %constant.12.clone.table_low) | copy-start | bytes 393220
  0.5 9.3 %copy-start.7 = (bf16[256,256]{1,0:T(8,128)(2,1)S(1)}, bf16[256,256]{1,0:T(8,128)(2,1)}, u32[]{:S(2)}) copy-start(bf16[256,256]{1,0:T(8,128)(2,1)} %constant.11.clone.table_high) | copy-start | bytes 393220
  1.8 8.9 %collective-permute-start = (bf16[128,256]{1,0:T(8,128)(2,1)S(1)}, bf16[128,256]{1,0:T(8,128)(2,1)S(1)}, u32[]{:S(2)}, u32[]{:S(2)}) collective-permute-start(bf16[128,256]{1,0:T(8,128)(2,1)S(1)} %get-tuple-element.36), channel_id=1, source_target_pairs={{0,8},{4,12},{8,0},{12,4},{16,24},{20,28},{24,16},{28,20},{1,9},{5... | collective-permute-start | bytes 196616 | tf_op jit(solution)/shard_map/ppermute | solution.py:321
  4.5 7.0 %collective-permute-start.1 = (bf16[128,256]{1,0:T(8,128)(2,1)S(1)}, bf16[128,256]{1,0:T(8,128)(2,1)S(1)}, u32[]{:S(2)}, u32[]{:S(2)}) collective-permute-start(bf16[128,256]{1,0:T(8,128)(2,1)S(1)} %get-tuple-element.37), channel_id=1, source_target_pairs={{0,16},{4,20},{8,24},{12,28},{16,0},{20,4},{24,8},{28,12},{1,17},{... | collective-permute-start | bytes 196616 | tf_op jit(solution)/shard_map/ppermute | solution.py:321
  7.1 6.1 %collective-permute-start.2 = (bf16[128,256]{1,0:T(8,128)(2,1)S(1)}, bf16[128,256]{1,0:T(8,128)(2,1)S(1)}, u32[]{:S(2)}, u32[]{:S(2)}) collective-permute-start(bf16[128,256]{1,0:T(8,128)(2,1)S(1)} %get-tuple-element.38), channel_id=1, source_target_pairs={{0,24},{4,28},{8,16},{12,20},{16,8},{20,12},{24,0},{28,4},{1,25},{... | collective-permute-start | bytes 196616 | tf_op jit(solution)/shard_map/ppermute | solution.py:321
  7.1 8.6 %collective-permute-start.3 = (bf16[128,256]{1,0:T(8,128)(2,1)S(1)}, bf16[128,256]{1,0:T(8,128)(2,1)S(1)}, u32[]{:S(2)}, u32[]{:S(2)}) collective-permute-start(bf16[128,256]{1,0:T(8,128)(2,1)S(1)} %get-tuple-element.35.refs_0_), channel_id=1, source_target_pairs={{0,4},{4,0},{8,12},{12,8},{16,20},{20,16},{24,28},{28,24},{1,5},{5... | collective-permute-start | bytes 196616 | tf_op jit(solution)/shard_map/ppermute | solution.py:321
  9.8 4.9 %copy-start.4 = (bf16[256,256]{1,0:T(8,128)(2,1)S(1)}, bf16[256,256]{1,0:T(8,128)(2,1)}, u32[]{:S(2)}) copy-start(bf16[256,256]{1,0:T(8,128)(2,1)} %constant.13.clone.table) | copy-start | bytes 393220
  10.7 6.7 %copy-start.5 = (bf16[256,256]{1,0:T(8,128)(2,1)S(1)}, bf16[256,256]{1,0:T(8,128)(2,1)}, u32[]{:S(2)}) copy-start(bf16[256,256]{1,0:T(8,128)(2,1)} %constant.14.clone.back) | copy-start | bytes 393220
  10.7 5.0 %collective-permute-start.4 = (bf16[128,256]{1,0:T(8,128)(2,1)S(1)}, bf16[128,256]{1,0:T(8,128)(2,1)S(1)}, u32[]{:S(2)}, u32[]{:S(2)}) collective-permute-start(bf16[128,256]{1,0:T(8,128)(2,1)S(1)} %collective-permute-done.refs_1_), channel_id=1, source_target_pairs={{0,4},{4,0},{8,12},{12,8},{16,20},{20,16},{24,28},{28,24},{1,5},{5... | collective-permute-start | bytes 196616 | tf_op jit(solution)/shard_map/ppermute | solution.py:321
  11.5 4.9 %collective-permute-start.5 = (bf16[128,256]{1,0:T(8,128)(2,1)S(1)}, bf16[128,256]{1,0:T(8,128)(2,1)S(1)}, u32[]{:S(2)}, u32[]{:S(2)}) collective-permute-start(bf16[128,256]{1,0:T(8,128)(2,1)S(1)} %collective-permute-done.1.refs_2_), channel_id=1, source_target_pairs={{0,4},{4,0},{8,12},{12,8},{16,20},{20,16},{24,28},{28,24},{1,5},{5... | collective-permute-start | bytes 196616 | tf_op jit(solution)/shard_map/ppermute | solution.py:321
  13.2 4.3 %collective-permute-start.6 = (bf16[128,256]{1,0:T(8,128)(2,1)S(1)}, bf16[128,256]{1,0:T(8,128)(2,1)S(1)}, u32[]{:S(2)}, u32[]{:S(2)}) collective-permute-start(bf16[128,256]{1,0:T(8,128)(2,1)S(1)} %collective-permute-done.2.refs_3_), channel_id=1, source_target_pairs={{0,4},{4,0},{8,12},{12,8},{16,20},{20,16},{24,28},{28,24},{1,5},{5... | collective-permute-start | bytes 196616 | tf_op jit(solution)/shard_map/ppermute | solution.py:321
  15.7 14.0 %copy-start.1 = (bf16[256,512]{1,0:T(8,128)(2,1)S(1)}, bf16[256,512]{1,0:T(8,128)(2,1)}, u32[]{:S(2)}) copy-start(bf16[256,512]{1,0:T(8,128)(2,1)} %signal.3) | copy-start | bytes 786436
  15.7 14.0 %copy-start.2 = (bf16[256,512]{1,0:T(8,128)(2,1)S(1)}, bf16[256,512]{1,0:T(8,128)(2,1)}, u32[]{:S(2)}) copy-start(bf16[256,512]{1,0:T(8,128)(2,1)} %gate.1) | copy-start | bytes 786436
  15.7 14.0 %copy-start.3 = (f32[512]{0:T(512)S(1)}, f32[512]{0:T(512)}, u32[]{:S(2)}) copy-start(f32[512]{0:T(512)} %param.17) | copy-start | bytes 6148
  17.4 12.5 %copy-start = (bf16[512,2048]{1,0:T(8,128)(2,1)S(1)}, bf16[512,2048]{1,0:T(8,128)(2,1)}, u32[]{:S(2)}) copy-start(bf16[512,2048]{1,0:T(8,128)(2,1)} %weights.1) | copy-start | bytes 6291460
  19.0 4.6 %collective-permute-start.7 = (bf16[128,256]{1,0:T(8,128)(2,1)S(1)}, bf16[128,256]{1,0:T(8,128)(2,1)S(1)}, u32[]{:S(2)}, u32[]{:S(2)}) collective-permute-start(bf16[128,256]{1,0:T(8,128)(2,1)S(1)} %get-tuple-element.40), channel_id=1, source_target_pairs={{0,8},{4,12},{8,0},{12,4},{16,24},{20,28},{24,16},{28,20},{1,9},{5... | collective-permute-start | bytes 196616 | tf_op jit(solution)/shard_map/ppermute | solution.py:321
  20.3 6.9 %collective-permute-start.8 = (bf16[128,256]{1,0:T(8,128)(2,1)S(1)}, bf16[128,256]{1,0:T(8,128)(2,1)S(1)}, u32[]{:S(2)}, u32[]{:S(2)}) collective-permute-start(bf16[128,256]{1,0:T(8,128)(2,1)S(1)} %get-tuple-element.41), channel_id=1, source_target_pairs={{0,16},{4,20},{8,24},{12,28},{16,0},{20,4},{24,8},{28,12},{1,17},{... | collective-permute-start | bytes 196616 | tf_op jit(solution)/shard_map/ppermute | solution.py:321
  23.6 6.1 %collective-permute-start.9 = (bf16[128,256]{1,0:T(8,128)(2,1)S(1)}, bf16[128,256]{1,0:T(8,128)(2,1)S(1)}, u32[]{:S(2)}, u32[]{:S(2)}) collective-permute-start(bf16[128,256]{1,0:T(8,128)(2,1)S(1)} %get-tuple-element.42), channel_id=1, source_target_pairs={{0,24},{4,28},{8,16},{12,20},{16,8},{20,12},{24,0},{28,4},{1,25},{... | collective-permute-start | bytes 196616 | tf_op jit(solution)/shard_map/ppermute | solution.py:321
  29.9 1.4 %collective-permute-start.10 = (bf16[128,512]{1,0:T(8,128)(2,1)S(1)}, bf16[128,512]{1,0:T(8,128)(2,1)S(1)}, u32[]{:S(2)}, u32[]{:S(2)}) collective-permute-start(bf16[128,512]{1,0:T(8,128)(2,1)S(1)} %get-tuple-element.43), channel_id=1, source_target_pairs={{0,1},{1,0},{2,3},{3,2},{4,5},{5,4},{6,7},{7,6},{8,9},{9,8},{10,11... | collective-permute-start | bytes 393224 | tf_op jit(solution)/shard_map/ppermute | solution.py:321
  31.6 8.5 %collective-permute-start.12 = (f32[128,512]{1,0:T(8,128)S(1)}, f32[128,512]{1,0:T(8,128)S(1)}, u32[]{:S(2)}, u32[]{:S(2)}) collective-permute-start(f32[128,512]{1,0:T(8,128)S(1)} %get-tuple-element.47), channel_id=1, source_target_pairs={{0,1},{1,0},{2,3},{3,2},{4,5},{5,4},{6,7},{7,6},{8,9},{9,8},{10,11... | collective-permute-start | bytes 786440 | tf_op jit(solution)/shard_map/ppermute | solution.py:321
  32.0 6.4 %collective-permute-start.14 = (bf16[128,512]{1,0:T(8,128)(2,1)S(1)}, bf16[128,512]{1,0:T(8,128)(2,1)S(1)}, u32[]{:S(2)}, u32[]{:S(2)}) collective-permute-start(bf16[128,512]{1,0:T(8,128)(2,1)S(1)} %shard_map.154), channel_id=1, source_target_pairs={{0,2},{1,3},{2,0},{3,1},{4,6},{5,7},{6,4},{7,5},{8,10},{9,11},{10,... | collective-permute-start | bytes 393224 | tf_op jit(solution)/shard_map/ppermute | solution.py:321
  33.8 6.2 %collective-permute-start.13 = (bf16[128,512]{1,0:T(8,128)(2,1)S(1)}, bf16[128,512]{1,0:T(8,128)(2,1)S(1)}, u32[]{:S(2)}, u32[]{:S(2)}) collective-permute-start(bf16[128,512]{1,0:T(8,128)(2,1)S(1)} %shard_map.153), channel_id=1, source_target_pairs={{0,3},{1,2},{2,1},{3,0},{4,7},{5,6},{6,5},{7,4},{8,11},{9,10},{10,... | collective-permute-start | bytes 393224 | tf_op jit(solution)/shard_map/ppermute | solution.py:321

commit v7 on v6

--- a/solution.py
+++ b/solution.py
@@ -198,13 +198,18 @@
     products(filt, spec, pieces, per, 0, 0, done)
 
 
-def conv_kernel(pieces, filt, table, back, own, *refs):
-    ins, outs = refs[:pieces], refs[pieces : 2 * pieces]
-    spec, total, result = refs[2 * pieces :]
-    me = lax.axis_index("seq")
+def side_kernel(table, *refs):
+    ins, spec = refs[:-1], refs[-1]
     per = ins[0].shape[1] // BLOCK
     spec[0:per] = jnp.zeros((per,) + spec.shape[1:], F32)
-    spectra(ins, spec, 1, range(pieces), table)
+    spectra(ins, spec, 1, range(len(ins)), table)
+
+
+def conv_kernel(pieces, filt, table, back, own, spec, last, *refs):
+    outs, total, result = refs[:pieces], *refs[pieces + 1 :]
+    me = lax.axis_index("seq")
+    per = last.shape[1] // BLOCK
+    spectra([last], spec, 1, [pieces - 1], table)
 
     def done(block, at, real, imag):
         total[block, at, :BLOCK] = own[block, at, :BLOCK] + real
@@ -220,26 +225,30 @@
         out[...] = jnp.concatenate([result[at + part] for part in range(per)], 1)
 
 
+def gated(part, signal, gate, skip, pieces, ordered):
+    place = lax.axis_index("seq") // 2
+    half = signal.shape[0] // 2
+    at = pl.ds(pl.multiple_of(part * half, half), half)
+    for k, piece in enumerate(pieces):
+        ordered[lax.bitwise_xor(place, k)] = piece[:, at]
+    turned = ordered[...].reshape(-1, half).T.astype(F32)
+    return (gate[at, :].astype(F32) * (turned + skip[...] * signal[at, :].astype(F32))).astype(BF16)
+
+
 def mix_kernel(pieces, signal, gate, skip, *refs):
-    ins, (keep_out, send_out, conv) = refs[:pieces], refs[pieces:]
-    place = lax.axis_index("seq") // 2
+    ins, (out, ordered) = refs[:pieces], refs[pieces:]
     core = lax.rem(lax.axis_index("head"), 2)
-    for k in range(pieces):
-        conv[lax.bitwise_xor(place, k)] = ins[k][...]
-    turned = conv[...].reshape(-1, conv.shape[-1]).T.astype(F32)
-    mixed = (gate[...].astype(F32) * (turned + skip[...] * signal[...].astype(F32))).astype(BF16)
-    half = keep_out.shape[0]
-    low, high = mixed[:half], mixed[half:]
-    keep_out[...] = jnp.where(core == 0, low, high)
-    send_out[...] = jnp.where(core == 0, high, low)
-
-
-def project_kernel(flips, own, weights, *outs):
+    out[...] = gated(1 - core, signal, gate, skip, ins, ordered)
+
+
+def project_kernel(pieces, flips, weights, signal, gate, skip, *refs):
+    ins, outs, ordered = refs[:pieces], refs[pieces:-1], refs[-1]
     head = lax.axis_index("head")
+    own = gated(lax.rem(head, 2), signal, gate, skip, ins, ordered)
     width = outs[0].shape[1]
     for flip, out in zip(flips, outs):
         columns = pl.ds(pl.multiple_of(lax.bitwise_xor(head, flip) * width, width), width)
-        out[...] = dot(own[...], weights[:, columns])
+        out[...] = dot(own, weights[:, columns])
 
 
 def add_kernel(flips, other, weights, *refs):
@@ -294,7 +303,7 @@
         copy.wait()
 
 
-def call(kernel, outs, *args, scratch=(), flops=0, grant=12, hbm=()):
+def call(kernel, outs, *args, scratch=(), flops=0, grant=12, hbm=(), aliases=None):
     spaces = [pltpu.HBM if n in hbm else VMEM for n in range(len(args))]
     run = pl.pallas_call(
         kernel,
@@ -302,6 +311,7 @@
         in_specs=[pl.BlockSpec(memory_space=space) for space in spaces],
         out_specs=jax.tree.map(lambda _: pl.BlockSpec(memory_space=VMEM), outs),
         scratch_shapes=list(scratch),
+        input_output_aliases=aliases or {},
         cost_estimate=pl.CostEstimate(flops=flops, bytes_accessed=0, transcendentals=0),
         compiler_params=pltpu.CompilerParams(vmem_limit_bytes=grant << 20),
     )
@@ -388,38 +398,42 @@
         scratch=[pltpu.VMEM(sums.shape, F32)],
         flops=1_000_000_000,
     )
-    convs = call(
+    side = shape((per + blocks // 2, share, 2 * BLOCK), F32)
+    first = call(side_kernel, side, block_table, *beside[:-1], flops=500_000_000)
+    *convs, _ = call(
         functools.partial(conv_kernel, pieces),
-        (piece,) * pieces,
+        (piece,) * pieces + (side,),
         filt,
         block_table,
         back_table,
         early,
-        *beside,
+        first,
+        beside[-1],
         scratch=[
-            pltpu.VMEM((per + blocks // 2, share, 2 * BLOCK), F32),
             pltpu.VMEM(sums.shape, F32),
             pltpu.VMEM((blocks // 2, share, BLOCK), BF16),
         ],
         flops=3_000_000_000,
+        aliases={4: pieces},
     )
 
     convs = [flip(conv, "seq", 2 * k) if k else conv for k, conv in enumerate(convs)]
-    mixed = shape((half, channels))
-    keep, send = call(
-        functools.partial(mix_kernel, pieces),
-        (mixed, mixed),
-        signal,
-        gate,
-        row(skip),
-        *convs,
-        scratch=[pltpu.VMEM((pieces, share, length_local), BF16)],
-        flops=500_000_000,
+    gating = (signal, gate, row(skip), *convs)
+    ordered = pltpu.VMEM((pieces, share, half), BF16)
+    send = call(
+        functools.partial(mix_kernel, pieces), shape((half, channels)), *gating, scratch=[ordered], flops=500_000_000
     )
     received = flip(send, "head", 1)
     wide = shape((half, width), F32)
     flips = (2, 3, 1, 0)
-    sums = call(functools.partial(project_kernel, flips), (wide,) * 4, keep, out_w, flops=500_000_000)
+    sums = call(
+        functools.partial(project_kernel, pieces, flips),
+        (wide,) * 4,
+        out_w,
+        *gating,
+        scratch=[ordered],
+        flops=500_000_000,
+    )
 
     def project(which, dtype):
         return call(

time: 40.9 us -> 40.7 us (level)
    pallas_call x10 -> x11, Pallas kernels: 7.13 us -> 7.28 us  [call(): return run(*args)]
  transfers between devices with their start and end apart: 15 -> 15, of which waited for: 9 -> 9; matrix products, arithmetic and copies ran while one was open for 0% -> 0% of each run, Pallas kernels for 18% -> 19%
where the time goes in v7:
time: 40.7 us; the launch traced here: 40.6 us
  starting transfers between devices  17.6 us (43%)
  waiting for transfers between devices  14.1 us (35%)
  Pallas kernels  8.66 us (21%)
    ppermute x15, starting transfers between devices, flip(): return lax.ppermute(x, axis, [(i, i ^ by) for i in range(size)])  17.6 us
    ppermute x15, waiting for transfers between devices, flip(): return lax.ppermute(x, axis, [(i, i ^ by) for i in range(size)])  14.1 us
    pallas_call x11, Pallas kernels, call(): return run(*args)  7.28 us
    pallas_call x2, Pallas kernels, add_half(): return run(first, second) if fresh else run(first, second, out)  1.38 us
  transfers between devices with their start and end apart: 15, of which 9 were waited for; matrix products, arithmetic and copies ran while one was open for 0% of the time, Pallas kernels for 19%

profile of v7, /device:TPU:0, one launch (start us, length us, event | category | flops | bytes accessed | tf_op | source)
XLA Modules:
  0.0 40.6 jit_solution(18023645273365864568)
XLA Ops:
  0.0 0.5 %collective-permute-start.11 = (bf16[512,2048]{1,0:T(8,128)(2,1)}, bf16[512,2048]{1,0:T(8,128)(2,1)S(1)}, u32[]{:S(2)}, u32[]{:S(2)}) collective-permute-start(bf16[512,2048]{1,0:T(8,128)(2,1)} %weights.1), channel_id=1, source_target_pairs={{0,1},{1,0},{2,3},{3,2},{4,5},{5,4},{6,7},{7,6},{8,9},{9,8},{10,11... | collective-permute-start | bytes 6291464 | tf_op jit(solution)/shard_map/ppermute | solution.py:331
  0.5 1.3 %shard_map.145 = (bf16[128,256]{1,0:T(8,128)(2,1)S(1)}, bf16[128,256]{1,0:T(8,128)(2,1)S(1)}, bf16[128,256]{1,0:T(8,128)(2,1)S(1)}, bf16[128,256]{1,0:T(8,128)(2...) custom-call(bf16[256,512]{1,0:T(8,128)(2,1)} %signal.5, ...), custom_call_target="tpu_custom_call" | custom-call | tf_op jit(solution)/shard_map/pallas_call | solution.py:322
  1.8 2.7 %collective-permute-start = (bf16[128,256]{1,0:T(8,128)(2,1)S(1)}, bf16[128,256]{1,0:T(8,128)(2,1)S(1)}, u32[]{:S(2)}, u32[]{:S(2)}) collective-permute-start(bf16[128,256]{1,0:T(8,128)(2,1)S(1)} %get-tuple-element.34), channel_id=1, source_target_pairs={{0,8},{4,12},{8,0},{12,4},{16,24},{20,28},{24,16},{28,20},{1,9},{5... | collective-permute-start | bytes 196616 | tf_op jit(solution)/shard_map/ppermute | solution.py:331
  4.5 2.6 %collective-permute-start.1 = (bf16[128,256]{1,0:T(8,128)(2,1)S(1)}, bf16[128,256]{1,0:T(8,128)(2,1)S(1)}, u32[]{:S(2)}, u32[]{:S(2)}) collective-permute-start(bf16[128,256]{1,0:T(8,128)(2,1)S(1)} %get-tuple-element.35), channel_id=1, source_target_pairs={{0,16},{4,20},{8,24},{12,28},{16,0},{20,4},{24,8},{28,12},{1,17},{... | collective-permute-start | bytes 196616 | tf_op jit(solution)/shard_map/ppermute | solution.py:331
  7.1 0.0 collective-permute-start.2
  7.1 1.7 %collective-permute-start.3 = (bf16[128,256]{1,0:T(8,128)(2,1)S(1)}, bf16[128,256]{1,0:T(8,128)(2,1)S(1)}, u32[]{:S(2)}, u32[]{:S(2)}) collective-permute-start(bf16[128,256]{1,0:T(8,128)(2,1)S(1)} %get-tuple-element.33.refs_0_), channel_id=1, source_target_pairs={{0,4},{4,0},{8,12},{12,8},{16,20},{20,16},{24,28},{28,24},{1,5},{5... | collective-permute-start | bytes 196616 | tf_op jit(solution)/shard_map/ppermute | solution.py:331
  8.8 0.9 %shard_map.146.hidden = bf16[192,2048]{1,0:T(8,128)(2,1)S(1)} custom-call(bf16[96,2048]{1,0:T(8,128)(2,1)S(1)} %get-tuple-element.26.feat, f32[33,64]{1,0:T(8,128)S(1)} %get-tuple-element.27.w_first, f32[1,64]{1,0:T(1,128)S(1)} %get-tuple-element.28.bias, f32[1,64]{1,0:T(1,128)S(1)} %get-tuple-element.29.freq, f32[64,64]{1,0:T(8,128)S(1)} %get-tuple-element.30.w_mid), custom_call_target="tpu_custom_call" | custom-call | flops 1000000000 | tf_op jit(solution)/shard_map/pallas_call | solution.py:322
  9.8 0.0 copy-start.4
  9.8 0.9 %shard_map.147.filt = f32[16,128,256]{2,1,0:T(8,128)S(1)} custom-call(bf16[192,2048]{1,0:T(8,128)(2,1)S(1)} %shard_map.146.hidden, f32[64,512]{1,0:T(8,128)S(1)} %get-tuple-element.31.w_last, f32[1,512]{1,0:T(1,128)S(1)} %get-tuple-element.32.rate, bf16[256,256]{1,0:T(8,128)(2,1)S(1)} %copy-done.7, bf16[256,256]{1,0:T(8,128)(2,1)S(1)} %copy-done.6), custom_call_target="tpu_custom_call" | custom-call | flops 2000000000 | tf_op jit(solution)/shard_map/pallas_call | solution.py:322
  10.7 0.0 copy-start.5
  10.7 0.0 collective-permute-done.refs_1_
  10.7 0.4 collective-permute-start.4
  11.1 0.4 %collective-permute-done.1.refs_2_ = bf16[128,256]{1,0:T(8,128)(2,1)S(1)} collective-permute-done((bf16[128,256]{1,0:T(8,128)(2,1)S(1)}, bf16[128,256]{1,0:T(8,128)(2,1)S(1)}, u32[]{:S(2)}, u32[]{:S(2)}) %collective-permute-start.1) | collective-permute-done | bytes 65568 | tf_op jit(solution)/shard_map/ppermute | solution.py:331
  11.5 1.5 %collective-permute-start.5 = (bf16[128,256]{1,0:T(8,128)(2,1)S(1)}, bf16[128,256]{1,0:T(8,128)(2,1)S(1)}, u32[]{:S(2)}, u32[]{:S(2)}) collective-permute-start(bf16[128,256]{1,0:T(8,128)(2,1)S(1)} %collective-permute-done.1.refs_2_), channel_id=1, source_target_pairs={{0,4},{4,0},{8,12},{12,8},{16,20},{20,16},{24,28},{28,24},{1,5},{5... | collective-permute-start | bytes 196616 | tf_op jit(solution)/shard_map/ppermute | solution.py:331
  13.0 0.1 collective-permute-done.2.refs_3_
  13.2 1.5 %collective-permute-start.6 = (bf16[128,256]{1,0:T(8,128)(2,1)S(1)}, bf16[128,256]{1,0:T(8,128)(2,1)S(1)}, u32[]{:S(2)}, u32[]{:S(2)}) collective-permute-start(bf16[128,256]{1,0:T(8,128)(2,1)S(1)} %collective-permute-done.2.refs_3_), channel_id=1, source_target_pairs={{0,4},{4,0},{8,12},{12,8},{16,20},{20,16},{24,28},{28,24},{1,5},{5... | collective-permute-start | bytes 196616 | tf_op jit(solution)/shard_map/ppermute | solution.py:331
  14.7 1.0 %shard_map.148.own = f32[8,128,256]{2,1,0:T(8,128)S(1)} custom-call(f32[16,128,256]{2,1,0:T(8,128)S(1)} %shard_map.147.filt, bf16[256,256]{1,0:T(8,128)(2,1)S(1)} %copy-done.4, bf16[128,256]{1,0:T(8,128)(2,1)S(1)} %get-tuple-element.33.refs_0_, bf16[128,256]{1,0:T(8,128)(2,1)S(1)} %collective-permute-done.refs_1_, ...), custom_call_target="tpu_custom_call" | custom-call | flops 1000000000 | tf_op jit(solution)/shard_map/pallas_call | solution.py:322
  15.7 0.0 collective-permute-done.3.refs_0_
  15.7 0.0 collective-permute-done.4.refs_1_
  15.7 0.8 %collective-permute-done.5.refs_2_ = bf16[128,256]{1,0:T(8,128)(2,1)S(1)} collective-permute-done((bf16[128,256]{1,0:T(8,128)(2,1)S(1)}, bf16[128,256]{1,0:T(8,128)(2,1)S(1)}, u32[]{:S(2)}, u32[]{:S(2)}) %collective-permute-start.5) | collective-permute-done | bytes 65568 | tf_op jit(solution)/shard_map/ppermute | solution.py:331
  16.5 0.3 shard_map.149.spec
  16.7 0.0 copy-start.1
  16.7 0.0 copy-start.2
  16.7 0.0 copy-start.3
  16.8 0.7 %collective-permute-done.6.last = bf16[128,256]{1,0:T(8,128)(2,1)S(1)} collective-permute-done((bf16[128,256]{1,0:T(8,128)(2,1)S(1)}, bf16[128,256]{1,0:T(8,128)(2,1)S(1)}, u32[]{:S(2)}, u32[]{:S(2)}) %collective-permute-start.6) | collective-permute-done | bytes 65568 | tf_op jit(solution)/shard_map/ppermute | solution.py:331
  17.4 1.5 %shard_map.150 = (bf16[128,256]{1,0:T(8,128)(2,1)S(1)}, bf16[128,256]{1,0:T(8,128)(2,1)S(1)}, bf16[128,256]{1,0:T(8,128)(2,1)S(1)}, bf16[128,256]{1,0:T(8,128)(2,1)S(1)}, f32[10,128,256]{2,1,0:T(8,128)S(1)}) custom-call(f32[16,128,256]{2,1,0:T(8,128)S(1)} %shard_map.147.filt, bf16[256,256]{1,0:T(8,128)(2,1)S(1)} %copy-done.4, ...), custom_call_target="tpu_custom_call", output_to_operand_aliasing={{4}: (4, {})} | custom-call | flops 3000000000 | tf_op jit(solution)/shard_map/pallas_call | solution.py:322
  18.9 1.3 %collective-permute-start.7 = (bf16[128,256]{1,0:T(8,128)(2,1)S(1)}, bf16[128,256]{1,0:T(8,128)(2,1)S(1)}, u32[]{:S(2)}, u32[]{:S(2)}) collective-permute-start(bf16[128,256]{1,0:T(8,128)(2,1)S(1)} %get-tuple-element.38), channel_id=1, source_target_pairs={{0,8},{4,12},{8,0},{12,4},{16,24},{20,28},{24,16},{28,20},{1,9},{5... | collective-permute-start | bytes 196616 | tf_op jit(solution)/shard_map/ppermute | solution.py:331
  20.2 3.2 %collective-permute-start.8 = (bf16[128,256]{1,0:T(8,128)(2,1)S(1)}, bf16[128,256]{1,0:T(8,128)(2,1)S(1)}, u32[]{:S(2)}, u32[]{:S(2)}) collective-permute-start(bf16[128,256]{1,0:T(8,128)(2,1)S(1)} %get-tuple-element.39), channel_id=1, source_target_pairs={{0,16},{4,20},{8,24},{12,28},{16,0},{20,4},{24,8},{28,12},{1,17},{... | collective-permute-start | bytes 196616 | tf_op jit(solution)/shard_map/ppermute | solution.py:331
  23.5 0.0 collective-permute-start.9
  23.5 0.0 collective-permute-done.7.refs_1_
  23.5 3.6 %collective-permute-done.8.refs_2_ = bf16[128,256]{1,0:T(8,128)(2,1)S(1)} collective-permute-done((bf16[128,256]{1,0:T(8,128)(2,1)S(1)}, bf16[128,256]{1,0:T(8,128)(2,1)S(1)}, u32[]{:S(2)}, u32[]{:S(2)}) %collective-permute-start.8) | collective-permute-done | bytes 65568 | tf_op jit(solution)/shard_map/ppermute | solution.py:331
  27.1 2.4 %collective-permute-done.9.refs_3_ = bf16[128,256]{1,0:T(8,128)(2,1)S(1)} collective-permute-done((bf16[128,256]{1,0:T(8,128)(2,1)S(1)}, bf16[128,256]{1,0:T(8,128)(2,1)S(1)}, u32[]{:S(2)}, u32[]{:S(2)}) %collective-permute-start.9) | collective-permute-done | bytes 65568 | tf_op jit(solution)/shard_map/ppermute | solution.py:331
  29.5 0.1 shard_map.151
  29.7 0.1 collective-permute-start.10
  29.8 0.5 %shard_map.152 = (f32[128,512]{1,0:T(8,128)S(1)}, f32[128,512]{1,0:T(8,128)S(1)}, f32[128,512]{1,0:T(8,128)S(1)}, f32[128,512]{1,0:T(8,128)S(1)}) custom-call(bf16[512,2048]{1,0:T(8,128)(2,1)S(1)} %copy-done, bf16[256,512]{1,0:T(8,128)(2,1)S(1)} %copy-done.1, bf16[256,512]{1,0:T(8,128)(2,1)S(1)} %copy-done.2, f32[1,512]{1,0:T(1,128)S(1)} %bitcast.5, ...), custom_call_target="tpu_custom_call" | custom-call | flops 500000000 | tf_op jit(solution)/shard_map/pallas_call | solution.py:322
  30.3 0.8 %collective-permute-done.10.other = bf16[128,512]{1,0:T(8,128)(2,1)S(1)} collective-permute-done((bf16[128,512]{1,0:T(8,128)(2,1)S(1)}, bf16[128,512]{1,0:T(8,128)(2,1)S(1)}, u32[]{:S(2)}, u32[]{:S(2)}) %collective-permute-start.10) | collective-permute-done | bytes 131104 | tf_op jit(solution)/shard_map/ppermute | solution.py:331
  31.1 0.0 collective-permute-done.11.weights
  31.1 0.3 shard_map.153
  31.4 0.2 collective-permute-start.12
  31.6 0.2 shard_map.155
  31.9 1.6 %collective-permute-start.14 = (bf16[128,512]{1,0:T(8,128)(2,1)S(1)}, bf16[128,512]{1,0:T(8,128)(2,1)S(1)}, u32[]{:S(2)}, u32[]{:S(2)}) collective-permute-start(bf16[128,512]{1,0:T(8,128)(2,1)S(1)} %shard_map.155), channel_id=1, source_target_pairs={{0,2},{1,3},{2,0},{3,1},{4,6},{5,7},{6,4},{7,5},{8,10},{9,11},{10,... | collective-permute-start | bytes 393224 | tf_op jit(solution)/shard_map/ppermute | solution.py:331
  33.4 0.2 shard_map.154
  33.7 0.3 collective-permute-start.13
  34.0 4.4 %collective-permute-done.14.second = bf16[128,512]{1,0:T(8,128)(2,1)S(1)} collective-permute-done((bf16[128,512]{1,0:T(8,128)(2,1)S(1)}, bf16[128,512]{1,0:T(8,128)(2,1)S(1)}, u32[]{:S(2)}, u32[]{:S(2)}) %collective-permute-start.14) | collective-permute-done | bytes 131104 | tf_op jit(solution)/shard_map/ppermute | solution.py:331
  38.3 0.7 %shard_map.156.refs_0_ = bf16[256,512]{1,0:T(8,128)(2,1)} custom-call(f32[128,512]{1,0:T(8,128)S(1)} %get-tuple-element.45.first, bf16[128,512]{1,0:T(8,128)(2,1)S(1)} %collective-permute-done.14.second), custom_call_target="tpu_custom_call" | custom-call | flops 100000000 | tf_op jit(solution)/shard_map/pallas_call | solution.py:287
  39.0 0.9 %collective-permute-done.13.second = bf16[128,512]{1,0:T(8,128)(2,1)S(1)} collective-permute-done((bf16[128,512]{1,0:T(8,128)(2,1)S(1)}, bf16[128,512]{1,0:T(8,128)(2,1)S(1)}, u32[]{:S(2)}, u32[]{:S(2)}) %collective-permute-start.13) | collective-permute-done | bytes 131104 | tf_op jit(solution)/shard_map/ppermute | solution.py:331
  39.9 0.0 collective-permute-done.12.first
  39.9 0.7 %shard_map.157 = bf16[256,512]{1,0:T(8,128)(2,1)} custom-call(f32[128,512]{1,0:T(8,128)S(1)} %collective-permute-done.12.first, bf16[128,512]{1,0:T(8,128)(2,1)S(1)} %collective-permute-done.13.second, bf16[256,512]{1,0:T(8,128)(2,1)} %shard_map.156.refs_0_), custom_call_target="tpu_custom_call", output_to_operand_aliasing={{}: (2, {})} | custom-call | flops 100000000 | tf_op jit(solution)/shard_map/pallas_call | solution.py:287
  (11 shorter events, 0.0 us)
Async XLA Ops:
  0.0 31.1 %collective-permute-start.11 = (bf16[512,2048]{1,0:T(8,128)(2,1)}, bf16[512,2048]{1,0:T(8,128)(2,1)S(1)}, u32[]{:S(2)}, u32[]{:S(2)}) collective-permute-start(bf16[512,2048]{1,0:T(8,128)(2,1)} %weights.1), channel_id=1, source_target_pairs={{0,1},{1,0},{2,3},{3,2},{4,5},{5,4},{6,7},{7,6},{8,9},{9,8},{10,11... | collective-permute-start | bytes 6291464 | tf_op jit(solution)/shard_map/ppermute | solution.py:331
  0.5 9.3 %copy-start.6 = (bf16[256,256]{1,0:T(8,128)(2,1)S(1)}, bf16[256,256]{1,0:T(8,128)(2,1)}, u32[]{:S(2)}) copy-start(bf16[256,256]{1,0:T(8,128)(2,1)} %constant.12.clone.table_low) | copy-start | bytes 393220
  0.5 9.3 %copy-start.7 = (bf16[256,256]{1,0:T(8,128)(2,1)S(1)}, bf16[256,256]{1,0:T(8,128)(2,1)}, u32[]{:S(2)}) copy-start(bf16[256,256]{1,0:T(8,128)(2,1)} %constant.11.clone.table_high) | copy-start | bytes 393220
  1.8 8.9 %collective-permute-start = (bf16[128,256]{1,0:T(8,128)(2,1)S(1)}, bf16[128,256]{1,0:T(8,128)(2,1)S(1)}, u32[]{:S(2)}, u32[]{:S(2)}) collective-permute-start(bf16[128,256]{1,0:T(8,128)(2,1)S(1)} %get-tuple-element.34), channel_id=1, source_target_pairs={{0,8},{4,12},{8,0},{12,4},{16,24},{20,28},{24,16},{28,20},{1,9},{5... | collective-permute-start | bytes 196616 | tf_op jit(solution)/shard_map/ppermute | solution.py:331
  4.5 7.0 %collective-permute-start.1 = (bf16[128,256]{1,0:T(8,128)(2,1)S(1)}, bf16[128,256]{1,0:T(8,128)(2,1)S(1)}, u32[]{:S(2)}, u32[]{:S(2)}) collective-permute-start(bf16[128,256]{1,0:T(8,128)(2,1)S(1)} %get-tuple-element.35), channel_id=1, source_target_pairs={{0,16},{4,20},{8,24},{12,28},{16,0},{20,4},{24,8},{28,12},{1,17},{... | collective-permute-start | bytes 196616 | tf_op jit(solution)/shard_map/ppermute | solution.py:331
  7.1 6.1 %collective-permute-start.2 = (bf16[128,256]{1,0:T(8,128)(2,1)S(1)}, bf16[128,256]{1,0:T(8,128)(2,1)S(1)}, u32[]{:S(2)}, u32[]{:S(2)}) collective-permute-start(bf16[128,256]{1,0:T(8,128)(2,1)S(1)} %get-tuple-element.36), channel_id=1, source_target_pairs={{0,24},{4,28},{8,16},{12,20},{16,8},{20,12},{24,0},{28,4},{1,25},{... | collective-permute-start | bytes 196616 | tf_op jit(solution)/shard_map/ppermute | solution.py:331
  7.1 8.6 %collective-permute-start.3 = (bf16[128,256]{1,0:T(8,128)(2,1)S(1)}, bf16[128,256]{1,0:T(8,128)(2,1)S(1)}, u32[]{:S(2)}, u32[]{:S(2)}) collective-permute-start(bf16[128,256]{1,0:T(8,128)(2,1)S(1)} %get-tuple-element.33.refs_0_), channel_id=1, source_target_pairs={{0,4},{4,0},{8,12},{12,8},{16,20},{20,16},{24,28},{28,24},{1,5},{5... | collective-permute-start | bytes 196616 | tf_op jit(solution)/shard_map/ppermute | solution.py:331
  9.8 4.9 %copy-start.4 = (bf16[256,256]{1,0:T(8,128)(2,1)S(1)}, bf16[256,256]{1,0:T(8,128)(2,1)}, u32[]{:S(2)}) copy-start(bf16[256,256]{1,0:T(8,128)(2,1)} %constant.13.clone.table) | copy-start | bytes 393220
  10.7 6.7 %copy-start.5 = (bf16[256,256]{1,0:T(8,128)(2,1)S(1)}, bf16[256,256]{1,0:T(8,128)(2,1)}, u32[]{:S(2)}) copy-start(bf16[256,256]{1,0:T(8,128)(2,1)} %constant.14.clone.back) | copy-start | bytes 393220
  10.7 5.0 %collective-permute-start.4 = (bf16[128,256]{1,0:T(8,128)(2,1)S(1)}, bf16[128,256]{1,0:T(8,128)(2,1)S(1)}, u32[]{:S(2)}, u32[]{:S(2)}) collective-permute-start(bf16[128,256]{1,0:T(8,128)(2,1)S(1)} %collective-permute-done.refs_1_), channel_id=1, source_target_pairs={{0,4},{4,0},{8,12},{12,8},{16,20},{20,16},{24,28},{28,24},{1,5},{5... | collective-permute-start | bytes 196616 | tf_op jit(solution)/shard_map/ppermute | solution.py:331
  11.5 4.9 %collective-permute-start.5 = (bf16[128,256]{1,0:T(8,128)(2,1)S(1)}, bf16[128,256]{1,0:T(8,128)(2,1)S(1)}, u32[]{:S(2)}, u32[]{:S(2)}) collective-permute-start(bf16[128,256]{1,0:T(8,128)(2,1)S(1)} %collective-permute-done.1.refs_2_), channel_id=1, source_target_pairs={{0,4},{4,0},{8,12},{12,8},{16,20},{20,16},{24,28},{28,24},{1,5},{5... | collective-permute-start | bytes 196616 | tf_op jit(solution)/shard_map/ppermute | solution.py:331
  13.2 4.3 %collective-permute-start.6 = (bf16[128,256]{1,0:T(8,128)(2,1)S(1)}, bf16[128,256]{1,0:T(8,128)(2,1)S(1)}, u32[]{:S(2)}, u32[]{:S(2)}) collective-permute-start(bf16[128,256]{1,0:T(8,128)(2,1)S(1)} %collective-permute-done.2.refs_3_), channel_id=1, source_target_pairs={{0,4},{4,0},{8,12},{12,8},{16,20},{20,16},{24,28},{28,24},{1,5},{5... | collective-permute-start | bytes 196616 | tf_op jit(solution)/shard_map/ppermute | solution.py:331
  16.7 12.8 %copy-start.1 = (bf16[256,512]{1,0:T(8,128)(2,1)S(1)}, bf16[256,512]{1,0:T(8,128)(2,1)}, u32[]{:S(2)}) copy-start(bf16[256,512]{1,0:T(8,128)(2,1)} %signal.5) | copy-start | bytes 786436
  16.7 12.8 %copy-start.2 = (bf16[256,512]{1,0:T(8,128)(2,1)S(1)}, bf16[256,512]{1,0:T(8,128)(2,1)}, u32[]{:S(2)}) copy-start(bf16[256,512]{1,0:T(8,128)(2,1)} %gate.3) | copy-start | bytes 786436
  16.7 12.8 %copy-start.3 = (f32[512]{0:T(512)S(1)}, f32[512]{0:T(512)}, u32[]{:S(2)}) copy-start(f32[512]{0:T(512)} %param.17) | copy-start | bytes 6148
  17.4 12.3 %copy-start = (bf16[512,2048]{1,0:T(8,128)(2,1)S(1)}, bf16[512,2048]{1,0:T(8,128)(2,1)}, u32[]{:S(2)}) copy-start(bf16[512,2048]{1,0:T(8,128)(2,1)} %weights.1) | copy-start | bytes 6291460
  18.9 4.6 %collective-permute-start.7 = (bf16[128,256]{1,0:T(8,128)(2,1)S(1)}, bf16[128,256]{1,0:T(8,128)(2,1)S(1)}, u32[]{:S(2)}, u32[]{:S(2)}) collective-permute-start(bf16[128,256]{1,0:T(8,128)(2,1)S(1)} %get-tuple-element.38), channel_id=1, source_target_pairs={{0,8},{4,12},{8,0},{12,4},{16,24},{20,28},{24,16},{28,20},{1,9},{5... | collective-permute-start | bytes 196616 | tf_op jit(solution)/shard_map/ppermute | solution.py:331
  20.2 6.9 %collective-permute-start.8 = (bf16[128,256]{1,0:T(8,128)(2,1)S(1)}, bf16[128,256]{1,0:T(8,128)(2,1)S(1)}, u32[]{:S(2)}, u32[]{:S(2)}) collective-permute-start(bf16[128,256]{1,0:T(8,128)(2,1)S(1)} %get-tuple-element.39), channel_id=1, source_target_pairs={{0,16},{4,20},{8,24},{12,28},{16,0},{20,4},{24,8},{28,12},{1,17},{... | collective-permute-start | bytes 196616 | tf_op jit(solution)/shard_map/ppermute | solution.py:331
  23.5 6.1 %collective-permute-start.9 = (bf16[128,256]{1,0:T(8,128)(2,1)S(1)}, bf16[128,256]{1,0:T(8,128)(2,1)S(1)}, u32[]{:S(2)}, u32[]{:S(2)}) collective-permute-start(bf16[128,256]{1,0:T(8,128)(2,1)S(1)} %get-tuple-element.40), channel_id=1, source_target_pairs={{0,24},{4,28},{8,16},{12,20},{16,8},{20,12},{24,0},{28,4},{1,25},{... | collective-permute-start | bytes 196616 | tf_op jit(solution)/shard_map/ppermute | solution.py:331
  29.7 1.4 %collective-permute-start.10 = (bf16[128,512]{1,0:T(8,128)(2,1)S(1)}, bf16[128,512]{1,0:T(8,128)(2,1)S(1)}, u32[]{:S(2)}, u32[]{:S(2)}) collective-permute-start(bf16[128,512]{1,0:T(8,128)(2,1)S(1)} %shard_map.151), channel_id=1, source_target_pairs={{0,1},{1,0},{2,3},{3,2},{4,5},{5,4},{6,7},{7,6},{8,9},{9,8},{10,11... | collective-permute-start | bytes 393224 | tf_op jit(solution)/shard_map/ppermute | solution.py:331
  31.4 8.5 %collective-permute-start.12 = (f32[128,512]{1,0:T(8,128)S(1)}, f32[128,512]{1,0:T(8,128)S(1)}, u32[]{:S(2)}, u32[]{:S(2)}) collective-permute-start(f32[128,512]{1,0:T(8,128)S(1)} %get-tuple-element.43), channel_id=1, source_target_pairs={{0,1},{1,0},{2,3},{3,2},{4,5},{5,4},{6,7},{7,6},{8,9},{9,8},{10,11... | collective-permute-start | bytes 786440 | tf_op jit(solution)/shard_map/ppermute | solution.py:331
  31.9 6.4 %collective-permute-start.14 = (bf16[128,512]{1,0:T(8,128)(2,1)S(1)}, bf16[128,512]{1,0:T(8,128)(2,1)S(1)}, u32[]{:S(2)}, u32[]{:S(2)}) collective-permute-start(bf16[128,512]{1,0:T(8,128)(2,1)S(1)} %shard_map.155), channel_id=1, source_target_pairs={{0,2},{1,3},{2,0},{3,1},{4,6},{5,7},{6,4},{7,5},{8,10},{9,11},{10,... | collective-permute-start | bytes 393224 | tf_op jit(solution)/shard_map/ppermute | solution.py:331
  33.7 6.2 %collective-permute-start.13 = (bf16[128,512]{1,0:T(8,128)(2,1)S(1)}, bf16[128,512]{1,0:T(8,128)(2,1)S(1)}, u32[]{:S(2)}, u32[]{:S(2)}) collective-permute-start(bf16[128,512]{1,0:T(8,128)(2,1)S(1)} %shard_map.154), channel_id=1, source_target_pairs={{0,3},{1,2},{2,1},{3,0},{4,7},{5,6},{6,5},{7,4},{8,11},{9,10},{10,... | collective-permute-start | bytes 393224 | tf_op jit(solution)/shard_map/ppermute | solution.py:331
